TPU v7x, 32 devices: a whole 2x2x4 slice. The times are simulated.
32 devices in a mesh: dp: 16 (over z, x, core), mp: 2 (over y).
Axes of the slice: x: 2, y: 2, z: 4, core: 2. Of those that a mesh axis runs over, the one named last changes fastest.
Arguments:
- tokens: bfloat16 [16384, 768], P('dp', 'mp'), may hold values from -6 to 6
- crop_counts: int32 [96], P('dp'), may hold values from 3 to 8, as said below
- crop_patches: int32 [96, 8], P('dp'), may hold values from 9 to 49, as said below
- rel_index: int32 [49, 49], replicated, may hold values from 0 to 168
- ln1_gain: float32 [768], replicated, may hold values from 0.5 to 1.5
- ln1_shift: float32 [768], replicated, may hold values from -4 to 4
- w_qkv: bfloat16 [768, 3, 768], P(None, None, 'mp'), may hold values from -0.21875 to 0.21875
- qv_bias: float32 [2, 768], P(None, 'mp'), may hold values from -4 to 4
- rel_table: float32 [169, 24], P(None, 'mp'), may hold values from -6 to 6
- w_out: bfloat16 [768, 768], P('mp'), may hold values from -0.875 to 0.875
- b_out: float32 [768], replicated, may hold values from -4 to 4
- ln2_gain: float32 [768], replicated, may hold values from 0.5 to 1.5
- ln2_shift: float32 [768], replicated, may hold values from -4 to 4
- w_in: bfloat16 [768, 3072], P(None, 'mp'), may hold values from -0.21875 to 0.21875
- b_in: float32 [3072], P('mp'), may hold values from -4 to 4
- w_back: bfloat16 [3072, 768], P('mp'), may hold values from -0.109375 to 0.109375
- b_back: float32 [768], replicated, may hold values from -4 to 4
- cotangent: bfloat16 [16384, 768], P('dp', 'mp'), may hold values from -6 to 6
Outputs:
- out_tokens: bfloat16 [16384, 768], P('dp', 'mp')
- grad_tokens: bfloat16 [16384, 768], P('dp', 'mp')
- grad_ln1_gain: float32 [768], replicated
- grad_ln1_shift: float32 [768], replicated
- grad_w_qkv: float32 [768, 3, 768], P(None, None, 'mp')
- grad_qv_bias: float32 [2, 768], P(None, 'mp')
- grad_rel_table: float32 [169, 24], P(None, 'mp')
- grad_w_out: float32 [768, 768], P('mp')
- grad_b_out: float32 [768], replicated
- grad_ln2_gain: float32 [768], replicated
- grad_ln2_shift: float32 [768], replicated
- grad_w_in: float32 [768, 3072], P(None, 'mp')
- grad_b_in: float32 [3072], P('mp')
- grad_w_back: float32 [3072, 768], P('mp')
- grad_b_back: float32 [768], replicated
Inputs may be any that keep to these rules, and one draw needn't show every extreme that they name: Image i has crop_counts[i] crops; among every group's 6 images one has exactly 8. `crop_patches`: crop 0 of every image has 49 patches, crop 1 has 49 or 9, all later crops 9; entries past an image's crop count are not used.
All inputs are finite; a program needn't handle non-finite values.
Results may differ from a plain program's by a relative error of at most 0.019.
Values may be sent and summed in bfloat16 or wider, within the bound.
A program may use at most 256 MiB of HBM per device.

v0:
```python
from functools import partial

import jax
import jax.numpy as jnp
from jax import lax
from jax.sharding import PartitionSpec as P

HEAD_DIM = 32
SIDE = 7
LOCAL_SIDE = 3
CELLS = 49
OFFSETS = 169
CROP_MAX = 8
BLOCK = 512
MARGIN = 64


EPS = 1e-05
NEG = -1e30


def layout(counts, patches, row_count):
    live_crop = jnp.arange(CROP_MAX, dtype=jnp.int32)[None, :] < counts[:, None]
    crop_rows = jnp.where(live_crop, patches, 0).reshape(-1)
    crop_ends = jnp.cumsum(crop_rows)
    used_rows = crop_ends[-1]
    row_ids = jnp.arange(row_count, dtype=jnp.int32)
    passed = crop_ends[None, :] <= row_ids[:, None]
    window = jnp.sum(passed.astype(jnp.int32), axis=1)
    starts = jnp.max(jnp.where(passed, crop_ends[None, :], 0), axis=1)
    finish = jnp.min(jnp.where(passed, row_count + used_rows + 1, crop_ends[None, :]), axis=1)
    length = finish - starts
    offset = row_ids - starts
    grid_side = jnp.where(length >= CELLS, SIDE, LOCAL_SIDE).astype(jnp.int32)
    cell_index = offset // grid_side * SIDE + offset % grid_side
    inside = row_ids < used_rows
    cell_ids = jnp.where(inside, cell_index, 0)
    windows = jnp.where(inside, window, crop_rows.shape[0] + row_ids - used_rows)
    return (cell_ids, windows)


def layer_norm(values, gain, shift):
    center = values - jnp.mean(values, axis=-1, keepdims=True)
    spread = jnp.mean(center * center, axis=-1, keepdims=True)
    return center * lax.rsqrt(spread + EPS) * gain + shift


def attention_parts(
    queries,
    keys_ext,
    values_ext,
    query_cells_all,
    query_windows_all,
    key_cells_all,
    key_windows_all,
    table,
    offset_hot,
):
    f32 = jnp.float32
    bf16 = jnp.bfloat16
    highest = lax.Precision.HIGHEST
    head_count = table.shape[1]
    head_cols = queries.shape[1]
    row_count = queries.shape[0]
    blocks = row_count // BLOCK
    key_span = BLOCK + 2 * MARGIN
    score_scale = HEAD_DIM ** (-0.5)
    cell_range = jnp.arange(CELLS, dtype=jnp.int32)
    cell_bias = jnp.einsum("pm,mh->hp", offset_hot, table, precision=highest).reshape(
        head_count, CELLS, CELLS
    )

    def block_scores(block_start):
        query_block = lax.dynamic_slice_in_dim(queries, block_start, BLOCK, 0).reshape(
            BLOCK, head_count, HEAD_DIM
        )
        key_block = lax.dynamic_slice_in_dim(keys_ext, block_start, key_span, 0).reshape(
            key_span, head_count, HEAD_DIM
        )
        value_block = lax.dynamic_slice_in_dim(values_ext, block_start, key_span, 0).reshape(
            key_span, head_count, HEAD_DIM
        )
        query_cells = lax.dynamic_slice_in_dim(query_cells_all, block_start, BLOCK, 0)
        key_cells = lax.dynamic_slice_in_dim(key_cells_all, block_start, key_span, 0)
        query_windows = lax.dynamic_slice_in_dim(query_windows_all, block_start, BLOCK, 0)
        key_windows = lax.dynamic_slice_in_dim(key_windows_all, block_start, key_span, 0)
        query_hot = (query_cells[:, None] == cell_range[None, :]).astype(f32)
        key_hot = (key_cells[:, None] == cell_range[None, :]).astype(bf16)
        left_bias = jnp.einsum("qc,hcm->hqm", query_hot, cell_bias, precision=highest)
        left_high = left_bias.astype(bf16)
        left_rest = (left_bias - left_high.astype(f32)).astype(bf16)
        pair_bias = jnp.einsum(
            "hqm,km->hqk", left_high, key_hot, preferred_element_type=f32
        ) + jnp.einsum("hqm,km->hqk", left_rest, key_hot, preferred_element_type=f32)
        raw_scores = (
            jnp.einsum("qhd,khd->hqk", query_block, key_block, preferred_element_type=f32)
            * score_scale
        )
        same_window = (query_windows[:, None] == key_windows[None, :])[None]
        scores = jnp.where(same_window, raw_scores + pair_bias, NEG)
        return (query_block, key_block, value_block, query_hot, key_hot, scores)

    def forward_block(block_index):
        unused_query, unused_key, value_block, unused_qhot, unused_khot, scores = block_scores(
            block_index * BLOCK
        )
        row_peak = jnp.max(scores, axis=-1, keepdims=True)
        exp_scores = jnp.exp(scores - row_peak)
        row_mass = jnp.sum(exp_scores, axis=-1, keepdims=True)
        weights = (exp_scores / row_mass).astype(bf16)
        block_mixed = jnp.einsum(
            "hqk,khd->qhd", weights, value_block, preferred_element_type=f32
        ).reshape(BLOCK, head_cols)
        return (block_mixed, row_peak + jnp.log(row_mass))

    def forward_all():
        attended, log_mass = lax.map(forward_block, jnp.arange(blocks, dtype=jnp.int32))
        return (attended.reshape(row_count, head_cols).astype(bf16), log_mass)

    def backward_all(grad_heads, log_mass):

        def backward_block(block_index, totals):
            grad_query_all, grad_key_ext, grad_value_ext, grad_cell = totals
            block_start = block_index * BLOCK
            query_block, key_block, value_block, query_hot, key_hot, scores = block_scores(
                block_start
            )
            weights_full = jnp.exp(scores - log_mass[block_index])
            weights = weights_full.astype(bf16)
            grad_block = lax.dynamic_slice_in_dim(grad_heads, block_start, BLOCK, 0).reshape(
                BLOCK, head_count, HEAD_DIM
            )
            grad_weights = jnp.einsum(
                "qhd,khd->hqk", grad_block, value_block, preferred_element_type=f32
            )
            row_inner = jnp.sum(weights_full * grad_weights, axis=-1, keepdims=True)
            grad_scores = (weights_full * (grad_weights - row_inner)).astype(bf16)
            grad_query_block = (
                jnp.einsum(
                    "hqk,khd->qhd", grad_scores, key_block, preferred_element_type=f32
                ).reshape(BLOCK, head_cols)
                * score_scale
            )
            grad_key_block = (
                jnp.einsum(
                    "hqk,qhd->khd", grad_scores, query_block, preferred_element_type=f32
                ).reshape(key_span, head_cols)
                * score_scale
            )
            grad_value_block = jnp.einsum(
                "hqk,qhd->khd", weights, grad_block, preferred_element_type=f32
            ).reshape(key_span, head_cols)
            key_sums = jnp.einsum("hqk,km->hqm", grad_scores, key_hot, preferred_element_type=f32)
            grad_cell = grad_cell + jnp.einsum(
                "qc,hqm->hcm", query_hot, key_sums, precision=highest
            )
            grad_query_all = lax.dynamic_update_slice_in_dim(
                grad_query_all, grad_query_block, block_start, 0
            )
            key_now = lax.dynamic_slice_in_dim(grad_key_ext, block_start, key_span, 0)
            grad_key_ext = lax.dynamic_update_slice_in_dim(
                grad_key_ext, key_now + grad_key_block, block_start, 0
            )
            value_now = lax.dynamic_slice_in_dim(grad_value_ext, block_start, key_span, 0)
            grad_value_ext = lax.dynamic_update_slice_in_dim(
                grad_value_ext, value_now + grad_value_block, block_start, 0
            )
            return (grad_query_all, grad_key_ext, grad_value_ext, grad_cell)

        start_totals = (
            jnp.zeros((row_count, head_cols), f32),
            jnp.zeros((row_count + 2 * MARGIN, head_cols), f32),
            jnp.zeros((row_count + 2 * MARGIN, head_cols), f32),
            jnp.zeros((head_count, CELLS, CELLS), f32),
        )
        grad_query_all, grad_key_ext, grad_value_ext, grad_cell = lax.fori_loop(
            0, blocks, backward_block, start_totals
        )
        grad_table = jnp.einsum(
            "pm,hp->mh", offset_hot, grad_cell.reshape(head_count, CELLS * CELLS), precision=highest
        )
        return (grad_query_all, grad_key_ext, grad_value_ext, grad_table)

    return (forward_all, backward_all)


def body(
    tokens,
    crop_counts,
    crop_patches,
    rel_index,
    ln1_gain,
    ln1_shift,
    w_qkv,
    qv_bias,
    rel_table,
    w_out,
    b_out,
    ln2_gain,
    ln2_shift,
    w_in,
    b_in,
    w_back,
    b_back,
    cotangent,
):
    f32 = jnp.float32
    bf16 = jnp.bfloat16
    full_rows = tokens.shape[0]
    part_width = tokens.shape[1]
    cell_all, window_all = layout(crop_counts, crop_patches, full_rows)
    pad_cells_all = jnp.pad(cell_all, (MARGIN, MARGIN))
    pad_windows_all = jnp.pad(window_all, (MARGIN, MARGIN), constant_values=-1)
    offset_hot = (
        rel_index.reshape(-1)[:, None] == jnp.arange(OFFSETS, dtype=jnp.int32)[None, :]
    ).astype(f32)
    column_start = lax.axis_index("mp") * part_width
    whole_in, whole_cot = (
        lax.all_gather(tokens, "mp", axis=1, tiled=True),
        lax.all_gather(cotangent, "mp", axis=1, tiled=True),
    )
    block_input = whole_in.astype(f32)
    mixer_in = layer_norm(block_input, ln1_gain, ln1_shift).astype(bf16)
    projected = jnp.einsum("td,dcf->tcf", mixer_in, w_qkv, preferred_element_type=f32)
    queries = (projected[:, 0] + qv_bias[0]).astype(bf16)
    keys_ext = jnp.pad(projected[:, 1].astype(bf16), ((MARGIN, MARGIN), (0, 0)))
    values_ext = jnp.pad((projected[:, 2] + qv_bias[1]).astype(bf16), ((MARGIN, MARGIN), (0, 0)))
    forward_all, backward_all = attention_parts(
        queries,
        keys_ext,
        values_ext,
        cell_all,
        window_all,
        pad_cells_all,
        pad_windows_all,
        rel_table,
        offset_hot,
    )
    heads_out, log_mass = forward_all()
    head_terms = jnp.dot(heads_out, w_out, preferred_element_type=f32)
    own_out = lax.dynamic_slice_in_dim(b_out, column_start, part_width, 0)
    mixer_half = (
        lax.psum_scatter(
            head_terms.astype(jnp.bfloat16), "mp", scatter_dimension=1, tiled=True
        ).astype(jnp.float32)
        + own_out
    )
    resid_half = lax.dynamic_slice_in_dim(block_input, column_start, part_width, 1) + mixer_half
    residual = lax.all_gather(resid_half.astype(jnp.bfloat16), "mp", axis=1, tiled=True).astype(
        resid_half.dtype
    )
    hidden_in = layer_norm(residual, ln2_gain, ln2_shift).astype(bf16)
    hidden_pre = jnp.dot(hidden_in, w_in, preferred_element_type=f32) + b_in
    activated = jax.nn.gelu(hidden_pre, approximate=False).astype(bf16)
    back_terms = jnp.dot(activated, w_back, preferred_element_type=f32)
    own_back = lax.dynamic_slice_in_dim(b_back, column_start, part_width, 0)
    out_half = (
        lax.psum_scatter(
            back_terms.astype(jnp.bfloat16), "mp", scatter_dimension=1, tiled=True
        ).astype(jnp.float32)
        + own_back
        + resid_half
    ).astype(bf16)
    grad_b_back = jnp.sum(whole_cot.astype(f32), axis=0)
    grad_w_back = jnp.einsum("tf,td->fd", activated, whole_cot, preferred_element_type=f32)
    grad_act = jnp.einsum("td,fd->tf", whole_cot, w_back, preferred_element_type=f32)
    unused_gelu, gelu_pull = jax.vjp(partial(jax.nn.gelu, approximate=False), hidden_pre)
    grad_pre = gelu_pull(grad_act)[0].astype(bf16)
    grad_b_in = jnp.sum(grad_pre.astype(f32), axis=0)
    grad_w_in = jnp.einsum("td,tf->df", hidden_in, grad_pre, preferred_element_type=f32)
    hidden_terms = jnp.einsum("tf,df->td", grad_pre, w_in, preferred_element_type=f32)
    grad_normed_two = lax.psum(hidden_terms.astype(jnp.bfloat16), "mp").astype(jnp.float32)
    unused_two, norm_two_pull = jax.vjp(layer_norm, residual, ln2_gain, ln2_shift)
    grad_resid_norm, grad_g2, grad_c2 = norm_two_pull(grad_normed_two)
    grad_resid = whole_cot.astype(f32) + grad_resid_norm
    grad_mixer = grad_resid.astype(bf16)
    grad_b_out = jnp.sum(grad_mixer.astype(f32), axis=0)
    grad_w_out = jnp.einsum("tf,td->fd", heads_out, grad_mixer, preferred_element_type=f32)
    grad_heads = jnp.einsum("td,fd->tf", grad_mixer, w_out, preferred_element_type=f32).astype(bf16)
    grad_query_all, grad_key_ext, grad_value_ext, grad_table = backward_all(grad_heads, log_mass)
    grad_query = grad_query_all.astype(bf16)
    grad_key = grad_key_ext[MARGIN : MARGIN + full_rows].astype(bf16)
    grad_value = grad_value_ext[MARGIN : MARGIN + full_rows].astype(bf16)
    grad_qkv = jnp.stack([grad_query, grad_key, grad_value], axis=1)
    grad_w_qkv = jnp.einsum("td,tcf->dcf", mixer_in, grad_qkv, preferred_element_type=f32)
    grad_qv_bias = jnp.stack(
        [jnp.sum(grad_query.astype(f32), axis=0), jnp.sum(grad_value.astype(f32), axis=0)]
    )
    mixer_terms = jnp.einsum("tcf,dcf->td", grad_qkv, w_qkv, preferred_element_type=f32)
    grad_normed_one = lax.psum(mixer_terms.astype(jnp.bfloat16), "mp").astype(jnp.float32)
    unused_one, norm_one_pull = jax.vjp(layer_norm, block_input, ln1_gain, ln1_shift)
    grad_input_norm, grad_g1, grad_c1 = norm_one_pull(grad_normed_one)
    grad_input = grad_resid + grad_input_norm
    grad_half = lax.dynamic_slice_in_dim(grad_input, column_start, part_width, 1).astype(bf16)
    (
        grad_g1,
        grad_c1,
        grad_w_qkv,
        grad_qv_bias,
        grad_table,
        grad_w_out,
        grad_b_out,
        grad_g2,
        grad_c2,
        grad_w_in,
        grad_b_in,
        grad_w_back,
        grad_b_back,
    ) = lax.psum(
        (
            grad_g1,
            grad_c1,
            grad_w_qkv,
            grad_qv_bias,
            grad_table,
            grad_w_out,
            grad_b_out,
            grad_g2,
            grad_c2,
            grad_w_in,
            grad_b_in,
            grad_w_back,
            grad_b_back,
        ),
        "dp",
    )
    return (
        out_half,
        grad_half,
        grad_g1,
        grad_c1,
        grad_w_qkv,
        grad_qv_bias,
        grad_table,
        grad_w_out,
        grad_b_out,
        grad_g2,
        grad_c2,
        grad_w_in,
        grad_b_in,
        grad_w_back,
        grad_b_back,
    )


def solution(mesh):
    return jax.shard_map(
        body,
        mesh=mesh,
        in_specs=(
            P("dp", "mp"),
            P("dp"),
            P("dp", None),
            P(),
            P(),
            P(),
            P(None, None, "mp"),
            P(None, "mp"),
            P(None, "mp"),
            P("mp", None),
            P(),
            P(),
            P(),
            P(None, "mp"),
            P("mp"),
            P("mp", None),
            P(),
            P("dp", "mp"),
        ),
        out_specs=(
            P("dp", "mp"),
            P("dp", "mp"),
            P(),
            P(),
            P(None, None, "mp"),
            P(None, "mp"),
            P(None, "mp"),
            P("mp", None),
            P(),
            P(),
            P(),
            P(None, "mp"),
            P("mp"),
            P("mp", None),
            P(),
        ),
        check_vma=False,
    )
```

profile of v0, /device:TPU:0, one launch (start us, length us, event | category | flops | bytes accessed | tf_op | source)
XLA Modules:
  0.0 874.7 jit_solution(5148712237486980018)
XLA Ops:
  15.4 24.2 %all-gather.4.cloned.1.call-done = bf16[1024,768]{1,0:T(8,128)(2,1)} async-done(((bf16[1024,384]{1,0:T(8,128)(2,1)}), bf16[1024,768]{1,0:T(8,128)(2,1)}) %all-gather.4.cloned.1.call-update) | async-done | bytes 1572880 | tf_op jit(solution)/shard_map/all_gather | solution.py:219
  43.4 4.0 fusion.72
  59.1 2.4 pad.16.clone
  61.5 107.4 %while.35 = (s32[]{:T(128)}, bf16[2,512,384]{2,1,0:T(8,128)(2,1)}, f32[2,12,512,1]{2,1,3,0:T(8,128)S(1)}, s32[2]{0:T(128)S(1)}, bf16[1152,384]{0,1:T(8,128)(2,1)...) while((s32[]{:T(128)}, bf16[2,512,384]{2,1,0:T(8,128)(2,1)}, ...), condition=%wide.region_9.10_spmd.clone.clone, body=%wide.region_6.9_spmd.clone.clone.sunk | while | flops 1492276992 | bytes 186890608 | solution.py:117
  65.9 6.7 fusion.179
  72.6 6.7 fusion.180
  79.7 17.7 %fusion.181 = (f32[12,512]{1,0:T(8,128)S(1)}, f32[12,512,640]{2,1,0:T(8,128)}) fusion(f32[12,512,640]{2,1,0:T(8,128)} %fusion.179, s32[640]{0:T(1024)S(1)} %dynamic_slice.201, f32[12,512,49]{1,2,0:T(8,128)S(1)} %convolution_bitcast_fusion.6, f32[12,512,640]{2,1,0:T(8,128)} %fusion.180, pred[512,640]{1,0:T(8,128)(4,1)S(1)} %broadcast_compare_fusion.4), kind=kOutput, calls=%fused_computation.192.clone.1 | convolution fusion | flops 406241920 | bytes 48744960 | tf_op jit(solution)/shard_map/while/body/eval_jaxpr/hqm,km->hqk/dot_general | solution.py:94
  97.5 7.5 fusion.182
  105.0 2.5 copy-done.3
  107.5 5.8 fusion.183
  119.5 6.7 fusion.179
  126.2 6.7 fusion.180
  133.4 17.7 %fusion.181 = (f32[12,512]{1,0:T(8,128)S(1)}, f32[12,512,640]{2,1,0:T(8,128)}) fusion(f32[12,512,640]{2,1,0:T(8,128)} %fusion.179, s32[640]{0:T(1024)S(1)} %dynamic_slice.201, f32[12,512,49]{1,2,0:T(8,128)S(1)} %convolution_bitcast_fusion.6, f32[12,512,640]{2,1,0:T(8,128)} %fusion.180, pred[512,640]{1,0:T(8,128)(4,1)S(1)} %broadcast_compare_fusion.4), kind=kOutput, calls=%fused_computation.192.clone.1 | convolution fusion | flops 406241920 | bytes 48744960 | tf_op jit(solution)/shard_map/while/body/eval_jaxpr/hqm,km->hqk/dot_general | solution.py:94
  151.1 7.5 fusion.182
  158.6 2.5 copy-done.3
  161.1 5.8 fusion.183
  168.9 3.4 convolution_convert_fusion
  172.4 2.6 copy.97
  175.1 3.3 convert_element_type.156
  178.4 22.9 %reduce-scatter.7.cloned.1.call-done = bf16[384,1024]{1,0:T(8,128)(2,1)} async-done(((bf16[768,1024]{1,0:T(8,128)(2,1)}), bf16[384,1024]{1,0:T(8,128)(2,1)}) %reduce-scatter.7.cloned.1.call-update) | async-done | bytes 786448
  203.5 2.7 fusion.68
  206.9 26.7 %all-gather.6.cloned.1.call-done = bf16[1024,768]{1,0:T(8,128)(2,1)} async-done(((bf16[1024,384]{1,0:T(8,128)(2,1)}), bf16[1024,768]{1,0:T(8,128)(2,1)}) %all-gather.6.cloned.1.call-update) | async-done | bytes 1572880 | tf_op jit(solution)/shard_map/all_gather | solution.py:249
  237.5 6.9 fusion.93
  244.4 17.8 %all-gather.8.cloned.1.call-done = bf16[1024,768]{1,0:T(8,128)(2,1)} async-done(((bf16[1024,384]{1,0:T(8,128)(2,1)}), bf16[1024,768]{1,0:T(8,128)(2,1)}) %all-gather.8.cloned.1.call-update) | async-done | bytes 1572880 | tf_op jit(solution)/shard_map/all_gather | solution.py:220
  262.3 20.0 %convert_reduce_fusion = (f32[1536]{0:T(1024)}, bf16[1024,1536]{1,0:T(8,128)(2,1)S(1)}, f32[1024,1536]{1,0:T(8,128)}) fusion(f32[1024,1536]{1,0:T(8,128)} %fusion.93, f32[1536]{0:T(1024)S(1)} %copy-done.63, bf16[1024,768]{1,0:T(8,128)(2,1)} %all-gather.8.cloned.1.call-done, bf16[1536,768]{1,0:T(8,128)(2,1)S(1)} %copy-done), kind=kOutput, calls=%fused_computation.64 | convolution fusion | flops 2533882368 | bytes 19673088 | tf_op jit(solution)/shard_map/td,fd->tf/dot_general | solution.py:266
  283.9 3.7 convolution_convert_fusion.1
  287.7 6.2 multiply_convert_fusion.1
  295.6 3.7 convolution_convert_fusion.2
  299.2 2.7 copy.99
  302.0 37.3 %all-reduce.10.cloned.1.call-done = bf16[1024,768]{1,0:T(8,128)(2,1)} async-done(((bf16[1024,768]{1,0:T(8,128)(2,1)}), bf16[1024,768]{1,0:T(8,128)(2,1)}) %all-reduce.10.cloned.1.call-update) | async-done | bytes 1572880 | tf_op jit(solution)/shard_map/psum | solution.py:272
  339.3 3.2 convert_reduce_fusion.2
  342.5 2.5 fusion.55
  345.1 3.4 convert_reduce_fusion.5
  354.2 180.6 %while.36 = (s32[]{:T(128)}, bf16[1024,384]{1,0:T(8,128)(2,1)}, f32[1152,384]{1,0:T(8,128)}, f32[1152,384]{1,0:T(8,128)}, f32[12,49,49]{1,2,0:T(8,128)}, /*index...) while((s32[]{:T(128)}, bf16[1024,384]{1,0:T(8,128)(2,1)}, ...), condition=%wide.region_19.20_spmd.clone.clone, body=%wide.region_17.19_spmd.clone.clone.sunk | while | flops 2814801152 | bytes 274809952 | solution.py:176
  358.1 6.8 fusion.202
  365.7 6.7 fusion.203
  372.5 6.8 fusion.204
  379.7 23.1 %multiply_reduce_fusion.3 = (f32[12,512]{1,0:T(8,128)S(1)}, f32[12,512,640]{2,1,0:T(8,128)}) fusion(f32[12,512,640]{2,1,0:T(8,128)} %fusion.202, f32[12,512]{1,0:T(8,128)S(1)} %dynamic-slice_bitcast_fusion.2, f32[12,512,640]{2,1,0:T(8,128)} %fusion.203, s32[640]{0:T(1024)S(1)} %dynamic_slice.212, f32[12,512,49]{1,2,0:T(8,128)S(1)} %convolution_bitcast_fusion.7, ...), kind=kOutput, calls=%fused_computation.26.clone.1 | convolution fusion | flops 414106240 | bytes 64498176 | tf_op jit(solution)/shard_map/while/body/eval_jaxpr/hqm,km->hqk/dot_general | solution.py:94
  402.7 10.7 %multiply_convert_fusion.3 = bf16[12,512,640]{2,1,0:T(8,128)(2,1)S(1)} fusion(f32[12,512,640]{2,1,0:T(8,128)} %get-tuple-element.882, f32[12,512,640]{2,1,0:T(8,128)} %fusion.202, f32[12,512]{1,0:T(8,128)S(1)} %get-tuple-element.883), kind=kLoop, calls=%fused_computation.25.clone.1 | loop fusion | flops 11796480 | bytes 39346176 | tf_op jit(solution)/shard_map/while/body/eval_jaxpr/convert_element_type | solution.py:137
  413.5 2.4 convolution_multiply_fusion.4
  419.4 6.9 fusion.205
  429.3 4.7 convolution_multiply_fusion.5
  434.4 2.6 constant_dynamic-update-slice_fusion.9
  437.1 5.8 fusion.206
  448.2 6.7 fusion.202
  455.8 6.7 fusion.203
  462.5 6.8 fusion.204
  469.7 23.1 %multiply_reduce_fusion.3 = (f32[12,512]{1,0:T(8,128)S(1)}, f32[12,512,640]{2,1,0:T(8,128)}) fusion(f32[12,512,640]{2,1,0:T(8,128)} %fusion.202, f32[12,512]{1,0:T(8,128)S(1)} %dynamic-slice_bitcast_fusion.2, f32[12,512,640]{2,1,0:T(8,128)} %fusion.203, s32[640]{0:T(1024)S(1)} %dynamic_slice.212, f32[12,512,49]{1,2,0:T(8,128)S(1)} %convolution_bitcast_fusion.7, ...), kind=kOutput, calls=%fused_computation.26.clone.1 | convolution fusion | flops 414106240 | bytes 64498176 | tf_op jit(solution)/shard_map/while/body/eval_jaxpr/hqm,km->hqk/dot_general | solution.py:94
  492.8 10.7 %multiply_convert_fusion.3 = bf16[12,512,640]{2,1,0:T(8,128)(2,1)S(1)} fusion(f32[12,512,640]{2,1,0:T(8,128)} %get-tuple-element.882, f32[12,512,640]{2,1,0:T(8,128)} %fusion.202, f32[12,512]{1,0:T(8,128)S(1)} %get-tuple-element.883), kind=kLoop, calls=%fused_computation.25.clone.1 | loop fusion | flops 11796480 | bytes 39346176 | tf_op jit(solution)/shard_map/while/body/eval_jaxpr/convert_element_type | solution.py:137
  503.6 2.4 convolution_multiply_fusion.4
  509.5 6.9 fusion.205
  519.4 4.7 convolution_multiply_fusion.5
  524.5 2.6 constant_dynamic-update-slice_fusion.9
  527.1 5.8 fusion.206
  539.2 3.4 bitcast_convert_fusion
  542.8 6.6 fusion.91
  549.4 4.4 fusion.101
  555.7 4.3 fusion.67
  565.4 28.9 %all-reduce.12.cloned.1.call-done = bf16[1024,768]{1,0:T(8,128)(2,1)} async-done(((bf16[1024,768]{1,0:T(8,128)(2,1)}), bf16[1024,768]{1,0:T(8,128)(2,1)}) %all-reduce.12.cloned.1.call-update) | async-done | bytes 1572880 | tf_op jit(solution)/shard_map/psum | solution.py:290
  594.3 2.8 fusion.56
  597.2 64.8 %all-reduce.4 = (f32[768]{0:T(1024)}, f32[768]{0:T(1024)}, f32[2,384]{1,0:T(2,128)}, f32[169,12]{0,1:T(8,128)}, f32[768]{0:T(1024)}, /*index=5*/f32[768]{0:T(1024)}, f32[768]{0:T(1024)}, f32[1536]{0:T(1024)}, f32[768]{0:T(1024)}) all-reduce(f32[768]{0:T(1024)S(1)} %get-tuple-element.609, ...), channel_id=1, replica_groups=mesh['dp'=16,'mp'=2] {'dp'}, use_global_device_ids=true, to_apply=%region_24.25 | all-reduce | flops 8940 | bytes 71520 | tf_op jit(solution)/shard_map/psum | solution.py:309
  662.0 2.7 fusion.96
  668.5 188.3 %all-reduce.14.cloned.1.call-done = (f32[768,3,384]{2,0,1:T(8,128)}, f32[384,768]{1,0:T(8,128)}, f32[768,1536]{1,0:T(8,128)}, f32[1536,768]{1,0:T(8,128)}) async-done(((f32[768,3,384]{2,0,1:T(8,128)}, f32[384,768]{1,0:T(8,128)}, f32[768,1536]{1,0:T(8,128)}, f32[1536,768]{1,0:T(8,128)}), (f32[768,3,384]{2,0,1:T(8,128)}, f32[384,768]{1,0:T(8,128)}, f32[768,1536]{1,0:T(8,128)}, ...) | async-done | bytes 14155792 | tf_op jit(solution)/shard_map/psum | solution.py:309
  856.8 4.2 copy.180
  (335 shorter events, 99.6 us)
Async XLA Ops:
  7.2 255.1 %copy-start = (bf16[1536,768]{1,0:T(8,128)(2,1)S(1)}, bf16[1536,768]{1,0:T(8,128)(2,1)}, u32[]{:S(2)}) copy-start(bf16[1536,768]{1,0:T(8,128)(2,1)} %param.37) | copy-start | bytes 7077892
  7.2 36.2 %copy-start.71 = (f32[768]{0:T(1024)S(1)}, f32[768]{0:T(1024)}, u32[]{:S(2)}) copy-start(f32[768]{0:T(1024)} %param.27) | copy-start | bytes 9220
  7.2 36.2 %copy-start.59 = (f32[768]{0:T(1024)S(1)}, f32[768]{0:T(1024)}, u32[]{:S(2)}) copy-start(f32[768]{0:T(1024)} %param.26) | copy-start | bytes 9220
  7.2 32.3 %all-gather.4.cloned.1.call-start = ((), (), s32[]{:S(2)}) async-start(), calls=%async_computation.2 | async-start | bytes 2359296 | tf_op jit(solution)/shard_map/all_gather | solution.py:219
  8.0 193.3 %reduce-scatter.7.cloned.1.call-start = ((), (), s32[]{:S(2)}) async-start(), calls=%async_computation.7 | async-start | bytes 2359296
  10.4 37.0 %copy-start.61 = (s32[2401]{0:T(1024)}, s32[2401]{0:T(1024)S(1)}, u32[]{:S(2)}) copy-start(s32[2401]{0:T(1024)S(1)} %eq.158) | copy-start | bytes 28816
  41.3 6.1 copy-start.43
  43.4 4.1 copy-start.49
  65.9 6.7 copy-start.16
  97.5 10.0 %copy-start.3 = (f32[12,512,640]{2,1,0:T(8,128)S(1)}, f32[12,512,640]{2,1,0:T(8,128)}, u32[]{:S(2)}) copy-start(f32[12,512,640]{2,1,0:T(8,128)} %get-tuple-element.865) | copy-start | bytes 47185924 | tf_op jit(solution)/shard_map/while
  119.5 6.7 copy-start.16
  151.1 10.0 %copy-start.3 = (f32[12,512,640]{2,1,0:T(8,128)S(1)}, f32[12,512,640]{2,1,0:T(8,128)}, u32[]{:S(2)}) copy-start(f32[12,512,640]{2,1,0:T(8,128)} %get-tuple-element.865) | copy-start | bytes 47185924 | tf_op jit(solution)/shard_map/while
  168.9 6.1 copy-start.65
  175.0 58.7 %all-gather.6.cloned.1.call-start = ((), (), s32[]{:S(2)}) async-start(), calls=%async_computation.3 | async-start | bytes 2359296 | tf_op jit(solution)/shard_map/all_gather | solution.py:249
  175.1 28.4 %copy-start.53 = (f32[384]{0:T(512)}, f32[384]{0:T(512)S(1)}, u32[]{:S(2)}) copy-start(f32[384]{0:T(512)S(1)} %dynamic_slice.115) | copy-start | bytes 4612
  206.3 31.2 %copy-start.45 = (f32[768]{0:T(1024)S(1)}, f32[768]{0:T(1024)}, u32[]{:S(2)}) copy-start(f32[768]{0:T(1024)} %param.33) | copy-start | bytes 9220
  206.3 31.2 %copy-start.69 = (f32[768]{0:T(1024)S(1)}, f32[768]{0:T(1024)}, u32[]{:S(2)}) copy-start(f32[768]{0:T(1024)} %param.34) | copy-start | bytes 9220
  206.3 56.0 %all-gather.8.cloned.1.call-start = ((), (), s32[]{:S(2)}) async-start(), calls=%async_computation.4 | async-start | bytes 2359296 | tf_op jit(solution)/shard_map/all_gather | solution.py:220
  206.9 132.5 %all-reduce.10.cloned.1.call-start = ((), (), s32[]{:S(2)}) async-start(), calls=%async_computation.5 | async-start | bytes 3145728 | tf_op jit(solution)/shard_map/psum | solution.py:272
  235.4 109.6 %copy-start.41 = (f32[1024]{0:T(1024)}, f32[1024]{0:T(1024)S(1)}, u32[]{:S(2)}) copy-start(f32[1024]{0:T(1024)S(1)} %broadcast_multiply_fusion) | copy-start | bytes 12292
  237.5 107.6 %copy-start.47 = (f32[1024]{0:T(1024)}, f32[1024]{0:T(1024)S(1)}, u32[]{:S(2)}) copy-start(f32[1024]{0:T(1024)S(1)} %fusion.85) | copy-start | bytes 12292
  237.5 24.7 %copy-start.63 = (f32[1536]{0:T(1024)S(1)}, f32[1536]{0:T(1024)}, u32[]{:S(2)}) copy-start(f32[1536]{0:T(1024)} %param.36) | copy-start | bytes 18436
  262.3 21.6 %copy-start.67 = (bf16[768,1536]{1,0:T(8,128)(2,1)S(1)}, bf16[768,1536]{1,0:T(8,128)(2,1)}, u32[]{:S(2)}) copy-start(bf16[768,1536]{1,0:T(8,128)(2,1)} %param.35) | copy-start | bytes 7077892
  287.6 276.3 %reduce-scatter.9.cloned.1.call-start = ((), (), s32[]{:S(2)}) async-start(), calls=%async_computation.8 | async-start | bytes 2359296
  299.2 40.1 %copy-start.9 = (bf16[1024,768]{1,0:T(8,128)(2,1)S(1)}, bf16[1024,768]{1,0:T(8,128)(2,1)}, u32[]{:S(2)}) copy-start(bf16[1024,768]{1,0:T(8,128)(2,1)} %all-gather.6.cloned.1.call-done) | copy-start | bytes 4718596
  302.0 292.4 %all-reduce.12.cloned.1.call-start = ((), (), s32[]{:S(2)}) async-start(), calls=%async_computation.6 | async-start | bytes 3145728 | tf_op jit(solution)/shard_map/psum | solution.py:290
  348.6 4.3 copy-start.13
  354.3 10.6 %copy-start.6 = (f32[12,49,49]{1,2,0:T(8,128)}, f32[12,49,49]{1,2,0:T(8,128)S(1)}, u32[]{:S(2)}) copy-start(f32[12,49,49]{1,2,0:T(8,128)S(1)} %get-tuple-element.987) | copy-start | bytes 345748 | tf_op jit(solution)/shard_map/while
  354.3 24.9 %copy-start.37 = (s32[1152]{0:T(1024)}, s32[1152]{0:T(1024)S(1)}, u32[]{:S(2)}) copy-start(s32[1152]{0:T(1024)S(1)} %get-tuple-element.984) | copy-start | bytes 13828 | tf_op jit(solution)/shard_map/while
  354.3 25.0 %copy-start.39 = (s32[1024]{0:T(1024)}, s32[1024]{0:T(1024)S(1)}, u32[]{:S(2)}) copy-start(s32[1024]{0:T(1024)S(1)} %get-tuple-element.983) | copy-start | bytes 12292 | tf_op jit(solution)/shard_map/while
  356.8 8.0 copy-start.4
  365.7 6.7 copy-start.17
  437.0 5.8 copy-start.20
  437.0 7.4 copy-start.7
  437.0 7.4 copy-start.38
  437.0 7.4 copy-start.40
  444.5 10.5 %copy-start.6 = (f32[12,49,49]{1,2,0:T(8,128)}, f32[12,49,49]{1,2,0:T(8,128)S(1)}, u32[]{:S(2)}) copy-start(f32[12,49,49]{1,2,0:T(8,128)S(1)} %get-tuple-element.987) | copy-start | bytes 345748 | tf_op jit(solution)/shard_map/while
  444.5 24.8 %copy-start.37 = (s32[1152]{0:T(1024)}, s32[1152]{0:T(1024)S(1)}, u32[]{:S(2)}) copy-start(s32[1152]{0:T(1024)S(1)} %get-tuple-element.984) | copy-start | bytes 13828 | tf_op jit(solution)/shard_map/while
  444.5 24.9 %copy-start.39 = (s32[1024]{0:T(1024)}, s32[1024]{0:T(1024)S(1)}, u32[]{:S(2)}) copy-start(s32[1024]{0:T(1024)S(1)} %get-tuple-element.983) | copy-start | bytes 12292 | tf_op jit(solution)/shard_map/while
  447.0 8.0 copy-start.4
  455.8 6.7 copy-start.17
  527.1 5.8 copy-start.20
  527.1 7.4 copy-start.7
  527.1 7.4 copy-start.38
  527.1 7.4 copy-start.40
  534.8 4.4 copy-start.28
  534.8 4.4 copy-start.68
  536.4 6.2 copy-start.32
  542.6 314.2 %all-reduce.14.cloned.1.call-start = ((), (), s32[]{:S(2)}) async-start(), calls=%async_computation.9 | async-start | bytes 28311552 | tf_op jit(solution)/shard_map/psum | solution.py:309
  542.7 6.6 copy-start.25
  542.8 6.6 copy-start.29
  549.4 4.4 copy-start.14
  549.4 4.4 copy-start.31
  562.7 34.4 %copy-start.55 = (f32[768]{0:T(1024)S(1)}, f32[768]{0:T(1024)}, u32[]{:S(2)}) copy-start(f32[768]{0:T(1024)} %get-tuple-element.611) | copy-start | bytes 9220
  562.7 34.4 %copy-start.56 = (f32[768]{0:T(1024)S(1)}, f32[768]{0:T(1024)}, u32[]{:S(2)}) copy-start(f32[768]{0:T(1024)} %get-tuple-element.607) | copy-start | bytes 9220
  562.7 34.4 %copy-start.57 = (f32[768]{0:T(1024)S(1)}, f32[768]{0:T(1024)}, u32[]{:S(2)}) copy-start(f32[768]{0:T(1024)} %get-tuple-element.689) | copy-start | bytes 9220
  562.7 34.4 %copy-start.58 = (f32[768]{0:T(1024)S(1)}, f32[768]{0:T(1024)}, u32[]{:S(2)}) copy-start(f32[768]{0:T(1024)} %get-tuple-element.703) | copy-start | bytes 9220
  562.8 34.4 %copy-start.64 = (f32[1536]{0:T(1024)S(1)}, f32[1536]{0:T(1024)}, u32[]{:S(2)}) copy-start(f32[1536]{0:T(1024)} %get-tuple-element.686) | copy-start | bytes 18436
  562.8 99.2 %copy-start.50 = (f32[1024]{0:T(1024)S(1)}, f32[1024]{0:T(1024)}, u32[]{:S(2)}) copy-start(f32[1024]{0:T(1024)} %copy-done.49) | copy-start | bytes 12292
  856.8 5.2 slice-start.2
  856.8 4.2 copy-start.30
  856.8 5.2 slice-start.3
  861.0 4.1 slice-start
  862.0 5.6 copy-start.1
  (38 other events, 95.2 us)
Sparse Core Ops, SparseCore 0:
  9.6 29.9 all-gather.3
  175.1 26.1 reduce-scatter.6
  206.4 27.1 all-gather.5
  235.0 27.1 all-gather.7
  287.8 51.5 all-reduce.9
  341.4 26.1 reduce-scatter.8
  542.8 51.5 all-reduce.11
  600.0 256.7 all-reduce.13
where the time goes:
time: 882 us; the launch traced here: 875 us
  waiting for transfers between devices  347 us (39%)
  matrix products  272 us (31%)
  local copies, waits for them, and re-layouts  92.3 us (10%)
  other arithmetic  80.1 us (9%)
  blocking collectives  64.8 us (7%)
  between operations  15.8 us (2%)
    psum x1, waiting for transfers between devices, body(): lax.psum((grad_g1, grad_c1, grad_w_qkv, grad_qv_bias, grad_table, grad_w_...  188 us
    dot_general x4, matrix products, block_scores(): jnp.einsum('hqm,km->hqk', left_rest, key_hot, preferred_element_type=f32)  81.6 us
    psum x1, blocking collectives, body(): lax.psum((grad_g1, grad_c1, grad_w_qkv, grad_qv_bias, grad_table, grad_w_...  64.8 us
    psum x1, waiting for transfers between devices, body(): lax.psum(hidden_terms.astype(jnp.bfloat16), 'mp').astype(jnp.float32)  37.3 us
    unnamed x136, local copies, waits for them, and re-layouts  33.4 us
    psum x1, waiting for transfers between devices, body(): lax.psum(mixer_terms.astype(jnp.bfloat16), 'mp').astype(jnp.float32)  28.9 us
    dot_general x4, matrix products, block_scores(): jnp.einsum('qhd,khd->hqk', query_block, key_block, preferred_element_type...  27 us
    dot_general x4, matrix products, block_scores(): jnp.einsum('hqm,km->hqk', left_high, key_hot, preferred_element_type=f32)  26.9 us
  transfers between devices with their start and end apart: 8, of which 7 were waited for; matrix products, arithmetic and copies ran while one was open for 30% of the time, Pallas kernels for 0%

commit v1 on v0

v1 whole, which is shorter than its diff:
```python
from functools import partial

import jax
import jax.numpy as jnp
from jax import lax
from jax.experimental import pallas as pl
from jax.experimental.pallas import tpu as pltpu
from jax.sharding import PartitionSpec as P

HEAD_DIM = 32
SIDE = 7
LOCAL_SIDE = 3
CELLS = 49
OFFSETS = 169
CROP_MAX = 8
QB = 128
HALO = 64
SPAN = QB + 2 * HALO
CP = 64
GROUP = 4
SCALE = HEAD_DIM ** (-0.5)
EPS = 1e-05
NEG = -1e30
F32 = jnp.float32
BF16 = jnp.bfloat16


def layout(counts, patches, row_count):
    live_crop = jnp.arange(CROP_MAX, dtype=jnp.int32)[None, :] < counts[:, None]
    crop_rows = jnp.where(live_crop, patches, 0).reshape(-1)
    crop_ends = jnp.cumsum(crop_rows)
    used_rows = crop_ends[-1]
    row_ids = jnp.arange(row_count, dtype=jnp.int32)
    passed = crop_ends[None, :] <= row_ids[:, None]
    window = jnp.sum(passed.astype(jnp.int32), axis=1)
    starts = jnp.max(jnp.where(passed, crop_ends[None, :], 0), axis=1)
    finish = jnp.min(jnp.where(passed, row_count + used_rows + 1, crop_ends[None, :]), axis=1)
    length = finish - starts
    offset = row_ids - starts
    grid_side = jnp.where(length >= CELLS, SIDE, LOCAL_SIDE).astype(jnp.int32)
    cell_index = offset // grid_side * SIDE + offset % grid_side
    inside = row_ids < used_rows
    cell_ids = jnp.where(inside, cell_index, 0)
    windows = jnp.where(inside, window, crop_rows.shape[0] + row_ids - used_rows)
    return (cell_ids, windows)


def layer_norm(values, gain, shift):
    center = values - jnp.mean(values, axis=-1, keepdims=True)
    spread = jnp.mean(center * center, axis=-1, keepdims=True)
    return center * lax.rsqrt(spread + EPS) * gain + shift


def dot(a, b):
    return jnp.dot(a, b, preferred_element_type=F32)


def dot_nt(a, b):
    return lax.dot_general(a, b, (((1,), (1,)), ((), ())), preferred_element_type=F32)


def stack_heads(rows_t):
    cols = []
    for j in range(GROUP):
        parts = []
        if j > 0:
            parts.append(jnp.zeros((HEAD_DIM * j, QB), BF16))
        parts.append(rows_t[HEAD_DIM * j : HEAD_DIM * (j + 1)])
        if j < GROUP - 1:
            parts.append(jnp.zeros((HEAD_DIM * (GROUP - 1 - j), QB), BF16))
        cols.append(jnp.concatenate(parts, axis=0))
    return jnp.concatenate(cols, axis=1)


def bias_rows(table, g, cells):
    tall = dot(table[2 * CP * GROUP * g : 2 * CP * GROUP * (g + 1), :], cells).astype(BF16)
    return jnp.concatenate([tall[2 * CP * j : 2 * CP * (j + 1)] for j in range(GROUP)], axis=1)


def attn_fwd_kernel(
    groups, tok, gain, shift, wt, qb_col, vb_col, vb_row, khot, qhott, table, kwin, qwin,
    a_out, qt, kx, kt, vx, o_out, lse, a_pad, vt,
):
    step = pl.program_id(0)
    rows_all = tok.shape[0]
    width = qt.shape[0]

    @pl.when(step == 0)
    def _():
        zero = jnp.zeros((HALO, tok.shape[1]), BF16)
        a_pad[:HALO, :] = zero
        a_pad[HALO + rows_all :, :] = zero

        def norm_rows(i, carry):
            at = pl.multiple_of(i * QB, QB)
            a = layer_norm(tok[pl.ds(at, QB), :].astype(F32), gain[...], shift[...]).astype(BF16)
            a_out[pl.ds(at, QB), :] = a
            a_pad[pl.ds(pl.multiple_of(at + HALO, HALO), QB), :] = a
            return carry

        lax.fori_loop(0, rows_all // QB, norm_rows, 0)
        a_all = a_pad[...]
        wk = wt[width : 2 * width, :]
        wv = wt[2 * width :, :]
        qt[...] = (dot_nt(wt[:width, :], a_out[...]) + qb_col[...]).astype(BF16)
        kx[...] = dot_nt(a_all, wk).astype(BF16)
        kt[...] = dot_nt(wk, a_all).astype(BF16)
        vx[...] = (dot_nt(a_all, wv) + vb_row[...]).astype(BF16)
        vt[...] = (dot_nt(wv, a_all) + vb_col[...]).astype(BF16)

    start = pl.multiple_of(step * QB, QB)
    span = pl.ds(start, SPAN)
    mask = jnp.where(kwin[span, :] == qwin[...], 0.0, NEG)
    hot = khot[span, :]
    cells = qhott[...]
    for g in range(groups):
        lanes = slice(128 * g, 128 * (g + 1))
        right = jnp.concatenate(
            [stack_heads(qt[lanes, pl.ds(start, QB)]), bias_rows(table, g, cells)], axis=0
        )
        scores = dot(jnp.concatenate([kx[span, lanes], hot], axis=1), right)
        outs = []
        for j in range(GROUP):
            h = GROUP * g + j
            s = scores[:, QB * j : QB * (j + 1)] * SCALE + mask
            peak = jnp.max(s, axis=0, keepdims=True)
            e = jnp.exp(s - peak)
            mass = jnp.sum(e, axis=0, keepdims=True)
            outs.append(dot(vt[HEAD_DIM * h : HEAD_DIM * (h + 1), span], e.astype(BF16)) / mass)
            lse[h : h + 1, :] = peak + jnp.log(mass)
        o_out[:, lanes] = jnp.concatenate(outs, axis=0).T.astype(BF16)


def whole(a):
    return pl.BlockSpec(a.shape, lambda i: (0,) * len(a.shape))


def same(*shape):
    return pl.BlockSpec(shape, lambda i: (0,) * len(shape))


def cols(n):
    return pl.BlockSpec((n, QB), lambda i: (0, i))


def attn_fwd(tok, gain, shift, wt, qb_col, vb_col, vb_row, khot, qhott, table, kwin, qwin):
    rows, model = tok.shape
    width = wt.shape[0] // 3
    heads = width // HEAD_DIM
    ext = rows + 2 * HALO
    shape = jax.ShapeDtypeStruct
    return pl.pallas_call(
        partial(attn_fwd_kernel, heads // GROUP),
        grid=(rows // QB,),
        in_specs=[whole(x) for x in (tok, gain, shift, wt, qb_col, vb_col, vb_row, khot)]
        + [cols(CP), whole(table), whole(kwin), cols(1)],
        out_specs=[
            same(rows, model), same(width, rows), same(ext, width), same(width, ext), same(ext, width),
            pl.BlockSpec((QB, width), lambda i: (i, 0)), cols(heads),
        ],
        out_shape=[
            shape((rows, model), BF16), shape((width, rows), BF16), shape((ext, width), BF16),
            shape((width, ext), BF16), shape((ext, width), BF16), shape((rows, width), BF16),
            shape((heads, rows), F32),
        ],
        scratch_shapes=[pltpu.VMEM((ext, model), BF16), pltpu.VMEM((width, ext), BF16)],
        name="attn_fwd",
    )(tok, gain, shift, wt, qb_col, vb_col, vb_row, khot, qhott, table, kwin, qwin)


def attn_bwd_kernel(
    groups, qt, kx, kt, vx, dot_t, khot, khott, qhott, qhot, table, kwin, qwin, lse,
    dq, dk, dv, gcell, dk_acc, dv_acc,
):
    step = pl.program_id(0)
    rows_all = dk.shape[0]

    @pl.when(step == 0)
    def _():
        dk_acc[...] = jnp.zeros_like(dk_acc)
        dv_acc[...] = jnp.zeros_like(dv_acc)
        gcell[...] = jnp.zeros_like(gcell)

    start = pl.multiple_of(step * QB, QB)
    span = pl.ds(start, SPAN)
    mask = jnp.where(kwin[span, :] == qwin[...], 0.0, NEG)
    hot = khot[span, :]
    hot_t = khott[:, span]
    cells = qhott[...]
    cells_r = qhot[...]
    for g in range(groups):
        lanes = slice(128 * g, 128 * (g + 1))
        q_stack = stack_heads(qt[lanes, :])
        do_stack = stack_heads(dot_t[lanes, :])
        right = jnp.concatenate([q_stack, bias_rows(table, g, cells)], axis=0)
        scores = dot(jnp.concatenate([kx[span, lanes], hot], axis=1), right)
        dprob = dot(vx[span, lanes], do_stack)
        ps, dss, dqs = [], [], []
        for j in range(GROUP):
            h = GROUP * g + j
            cut = slice(QB * j, QB * (j + 1))
            p = jnp.exp(scores[:, cut] * SCALE + mask - lse[h : h + 1, :])
            t = p * dprob[:, cut]
            inner = jnp.sum(t, axis=0, keepdims=True)
            ds = (t - p * inner).astype(BF16)
            ps.append(p.astype(BF16))
            dss.append(ds)
            both = dot(jnp.concatenate([kt[HEAD_DIM * h : HEAD_DIM * (h + 1), span], hot_t], axis=0), ds)
            dqs.append(both[:HEAD_DIM])
            gcell[CP * h : CP * (h + 1), :] += dot(both[HEAD_DIM:].astype(BF16), cells_r)
        dq[:, lanes] = (jnp.concatenate(dqs, axis=0) * SCALE).T.astype(BF16)
        dk_acc[span, lanes] += dot_nt(jnp.concatenate(dss, axis=1), q_stack)
        dv_acc[span, lanes] += dot_nt(jnp.concatenate(ps, axis=1), do_stack)

    @pl.when(step == pl.num_programs(0) - 1)
    def _():
        own = pl.ds(HALO, rows_all)
        dk[...] = (dk_acc[own, :] * SCALE).astype(BF16)
        dv[...] = dv_acc[own, :].astype(BF16)


def attn_bwd(qt, kx, kt, vx, dot_t, khot, khott, qhott, qhot, table, kwin, qwin, lse):
    width, rows = qt.shape
    heads = width // HEAD_DIM
    ext = rows + 2 * HALO
    shape = jax.ShapeDtypeStruct
    rblk = lambda n: pl.BlockSpec((QB, n), lambda i: (i, 0))
    return pl.pallas_call(
        partial(attn_bwd_kernel, heads // GROUP),
        grid=(rows // QB,),
        in_specs=[
            cols(width), whole(kx), whole(kt), whole(vx), cols(width), whole(khot), whole(khott),
            cols(CP), rblk(CP), whole(table), whole(kwin), cols(1), cols(heads),
        ],
        out_specs=[rblk(width), same(rows, width), same(rows, width), same(CP * heads, CP)],
        out_shape=[
            shape((rows, width), BF16), shape((rows, width), BF16), shape((rows, width), BF16),
            shape((CP * heads, CP), F32),
        ],
        scratch_shapes=[pltpu.VMEM((ext, width), F32), pltpu.VMEM((ext, width), F32)],
        name="attn_bwd",
    )(qt, kx, kt, vx, dot_t, khot, khott, qhott, qhot, table, kwin, qwin, lse)


def window_data(crop_counts, crop_patches, rel_index, rel_table, rows):
    highest = lax.Precision.HIGHEST
    heads = rel_table.shape[1]
    cells, wins = layout(crop_counts, crop_patches, rows)
    kcells = jnp.pad(cells, (HALO, HALO))
    kwin = jnp.pad(wins, (HALO, HALO), constant_values=-1)[:, None]
    span_cells = jnp.arange(CP, dtype=jnp.int32)
    wide_cells = jnp.arange(2 * CP, dtype=jnp.int32) % CP
    khot = (kcells[:, None] == wide_cells[None, :]).astype(BF16)
    khott = (span_cells[:, None] == kcells[None, :]).astype(BF16)
    qhott = (span_cells[:, None] == cells[None, :]).astype(BF16)
    qhot = (cells[:, None] == span_cells[None, :]).astype(BF16)
    rel_t = jnp.pad(rel_index.T, ((0, CP - CELLS), (0, CP - CELLS)), constant_values=-1).reshape(-1)
    offset_hot = (rel_t[:, None] == jnp.arange(OFFSETS, dtype=jnp.int32)[None, :]).astype(F32)
    bias = jnp.einsum("pm,mh->hp", offset_hot, rel_table, precision=highest) / SCALE
    high = bias.astype(BF16)
    rest = (bias - high.astype(F32)).astype(BF16)
    table = jnp.stack([high.reshape(heads, CP, CP), rest.reshape(heads, CP, CP)], axis=1)
    return (khot, khott, qhott, qhot, table.reshape(heads * 2 * CP, CP), kwin, wins[None, :], offset_hot)


def body(
    tokens,
    crop_counts,
    crop_patches,
    rel_index,
    ln1_gain,
    ln1_shift,
    w_qkv,
    qv_bias,
    rel_table,
    w_out,
    b_out,
    ln2_gain,
    ln2_shift,
    w_in,
    b_in,
    w_back,
    b_back,
    cotangent,
):
    highest = lax.Precision.HIGHEST
    rows, part_width = tokens.shape
    model = ln1_gain.shape[0]
    width = w_qkv.shape[2]
    heads = width // HEAD_DIM
    khot, khott, qhott, qhot, table, kwin, qwin, offset_hot = window_data(
        crop_counts, crop_patches, rel_index, rel_table, rows
    )
    column_start = lax.axis_index("mp") * part_width
    whole_in = lax.all_gather(tokens, "mp", axis=1, tiled=True)
    w_out_all = lax.all_gather(w_out, "mp", axis=0, tiled=True)
    whole_cot = lax.all_gather(cotangent, "mp", axis=1, tiled=True)
    wt = jnp.transpose(w_qkv, (1, 2, 0)).reshape(3 * width, model)
    mixer_in, qt, kx, kt, vx, heads_out, lse = attn_fwd(
        whole_in, ln1_gain[None, :], ln1_shift[None, :], wt, qv_bias[0][:, None], qv_bias[1][:, None],
        qv_bias[1][None, :], khot, qhott, table, kwin, qwin,
    )
    block_input = whole_in.astype(F32)
    heads_all = lax.all_gather(heads_out, "mp", axis=1, tiled=True)
    residual = block_input + dot(heads_all, w_out_all) + b_out
    hidden_in = layer_norm(residual, ln2_gain, ln2_shift).astype(BF16)
    hidden_pre = dot(hidden_in, w_in) + b_in
    activated = jax.nn.gelu(hidden_pre, approximate=False).astype(BF16)
    back_terms = dot(activated, w_back)
    grad_w_back = jnp.einsum("tf,td->fd", activated, whole_cot, preferred_element_type=F32)
    grad_act = jnp.einsum("td,fd->tf", whole_cot, w_back, preferred_element_type=F32)
    unused_gelu, gelu_pull = jax.vjp(partial(jax.nn.gelu, approximate=False), hidden_pre)
    grad_pre = gelu_pull(grad_act)[0].astype(BF16)
    hidden_terms = jnp.einsum("tf,df->td", grad_pre, w_in, preferred_element_type=F32)
    grad_normed_two = lax.psum(hidden_terms.astype(BF16), "mp").astype(F32)
    grad_b_back = jnp.sum(whole_cot.astype(F32), axis=0)
    grad_b_in = jnp.sum(grad_pre.astype(F32), axis=0)
    grad_w_in = jnp.einsum("td,tf->df", hidden_in, grad_pre, preferred_element_type=F32)
    unused_two, norm_two_pull = jax.vjp(layer_norm, residual, ln2_gain, ln2_shift)
    grad_resid_norm, grad_g2, grad_c2 = norm_two_pull(grad_normed_two)
    grad_resid = whole_cot.astype(F32) + grad_resid_norm
    grad_mixer = grad_resid.astype(BF16)
    grad_b_out = jnp.sum(grad_mixer.astype(F32), axis=0)
    grad_w_out = jnp.einsum("tf,td->fd", heads_out, grad_mixer, preferred_element_type=F32)
    grad_heads_t = jnp.einsum("fd,td->ft", w_out, grad_mixer, preferred_element_type=F32).astype(BF16)
    grad_query, grad_key, grad_value, gcell = attn_bwd(
        qt, kx, kt, vx, grad_heads_t, khot, khott, qhott, qhot, table, kwin, qwin, lse
    )
    grad_table = jnp.einsum(
        "pm,hp->mh", offset_hot, gcell.reshape(heads, CP * CP), precision=highest
    )
    grad_qkv = jnp.concatenate([grad_query, grad_key, grad_value], axis=1)
    mixer_terms = dot(grad_qkv, wt)
    grad_normed_one = lax.psum(mixer_terms.astype(BF16), "mp").astype(F32)
    grad_wt = jnp.einsum("tf,td->fd", grad_qkv, mixer_in, preferred_element_type=F32)
    grad_qv_bias = jnp.stack(
        [jnp.sum(grad_query.astype(F32), axis=0), jnp.sum(grad_value.astype(F32), axis=0)]
    )
    out_half = (
        lax.psum_scatter(back_terms.astype(BF16), "mp", scatter_dimension=1, tiled=True).astype(F32)
        + lax.dynamic_slice_in_dim(b_back, column_start, part_width, 0)
        + lax.dynamic_slice_in_dim(residual, column_start, part_width, 1)
    ).astype(BF16)
    unused_one, norm_one_pull = jax.vjp(layer_norm, block_input, ln1_gain, ln1_shift)
    grad_input_norm, grad_g1, grad_c1 = norm_one_pull(grad_normed_one)
    grad_input = grad_resid + grad_input_norm
    grad_half = lax.dynamic_slice_in_dim(grad_input, column_start, part_width, 1).astype(BF16)

    vectors = [grad_g1, grad_c1, grad_b_out, grad_g2, grad_c2, grad_b_back]
    packed = jnp.concatenate(
        [item.reshape(-1) for item in vectors + [grad_qv_bias, grad_b_in, grad_table]]
    )
    early = lax.psum((grad_w_in.astype(BF16), grad_w_back.astype(BF16)), "dp")
    early, late = lax.optimization_barrier(
        (early, (grad_wt.astype(BF16), grad_w_out.astype(BF16), packed.astype(BF16)))
    )
    late = lax.optimization_barrier(lax.psum(late, "dp"))
    grad_w_in, grad_w_back = (item.astype(F32) for item in early)
    grad_wt, grad_w_out, packed = (item.astype(F32) for item in late)
    grad_w_qkv = jnp.transpose(grad_wt.reshape(3, width, model), (2, 0, 1))
    at = 0
    outs = []
    for item in vectors + [grad_qv_bias, grad_b_in, grad_table]:
        outs.append(packed[at : at + item.size].reshape(item.shape))
        at += item.size
    grad_g1, grad_c1, grad_b_out, grad_g2, grad_c2, grad_b_back, grad_qv_bias, grad_b_in, grad_table = outs
    return (
        out_half,
        grad_half,
        grad_g1,
        grad_c1,
        grad_w_qkv,
        grad_qv_bias,
        grad_table,
        grad_w_out,
        grad_b_out,
        grad_g2,
        grad_c2,
        grad_w_in,
        grad_b_in,
        grad_w_back,
        grad_b_back,
    )


def solution(mesh):
    return jax.shard_map(
        body,
        mesh=mesh,
        in_specs=(
            P("dp", "mp"),
            P("dp"),
            P("dp", None),
            P(),
            P(),
            P(),
            P(None, None, "mp"),
            P(None, "mp"),
            P(None, "mp"),
            P("mp", None),
            P(),
            P(),
            P(),
            P(None, "mp"),
            P("mp"),
            P("mp", None),
            P(),
            P("dp", "mp"),
        ),
        out_specs=(
            P("dp", "mp"),
            P("dp", "mp"),
            P(),
            P(),
            P(None, None, "mp"),
            P(None, "mp"),
            P(None, "mp"),
            P("mp", None),
            P(),
            P(),
            P(),
            P(None, "mp"),
            P("mp"),
            P("mp", None),
            P(),
        ),
        check_vma=False,
    )
```

time: 882 us -> 577 us (0.65)
  matrix products: 272 us -> 62.7 us
  waiting for transfers between devices: 347 us -> 286 us
  Pallas kernels: 0 us -> 54.6 us
  local copies, waits for them, and re-layouts: 92.3 us -> 40.4 us
  other arithmetic: 80.1 us -> 48.3 us
    dot_general x44 -> x13, matrix products: 272 us -> 62.7 us  [the longest x1 19.9 us: body(): jnp.einsum('td,fd->tf', whole_cot, w_back, preferred_element_type=F32)]
    psum x3 -> x4, waiting for transfers between devices: 255 us -> 200 us  [the longest x1 114 us: body(): early = lax.psum((grad_w_in.astype(BF16), grad_w_back.astype(BF16)), 'dp')]
    pallas_call x0 -> x2, Pallas kernels: none -> 54.6 us  [the longest x1 31.4 us: attn_bwd(): pl.pallas_call(partial(attn_bwd_kernel, heads // GROUP), grid=(rows // QB...]
    dynamic_slice x42 -> x1, local copies, waits for them, and re-layouts: 20.4 us -> 0.65 us  [body(): lax.dynamic_slice_in_dim(b_back, column_start, part_width, 0)]
    convert_element_type x7 -> x9, other arithmetic: 36.4 us -> 18.9 us  [the longest x2 7.19 us: body(): grad_w_in, grad_w_back = (item.astype(F32) for item in early)]
    unnamed x136 -> x91, local copies, waits for them, and re-layouts: 33.4 us -> 18.1 us
    reduce_sum x5 -> x4, other arithmetic: 20.3 us -> 5.73 us  [the longest x1 2.66 us: body(): grad_b_out = jnp.sum(grad_mixer.astype(F32), axis=0)]
    dynamic_update_slice x14 -> x0, local copies, waits for them, and re-layouts: 13 us -> none  [the longest x4 7.77 us: backward_block(): lax.dynamic_update_slice_in_dim(grad_value_ext, value_now + grad_value_bl...]
  transfers between devices with their start and end apart: 8 -> 9, of which waited for: 7 -> 8; matrix products, arithmetic and copies ran while one was open for 30% -> 16% of each run, Pallas kernels for 0% -> 4%
where the time goes in v1:
time: 577 us; the launch traced here: 571 us
  waiting for transfers between devices  286 us (50%)
  matrix products  62.7 us (11%)
  blocking collectives  61.9 us (11%)
  Pallas kernels  54.6 us (9%)
  other arithmetic  48.3 us (8%)
  local copies, waits for them, and re-layouts  40.4 us (7%)
  between operations  15.2 us (3%)
    psum x1, waiting for transfers between devices, body(): early = lax.psum((grad_w_in.astype(BF16), grad_w_back.astype(BF16)), 'dp')  114 us
    psum x1, blocking collectives, body(): late = lax.optimization_barrier(lax.psum(late, 'dp'))  61.9 us
    psum x1, waiting for transfers between devices, body(): grad_normed_two = lax.psum(hidden_terms.astype(BF16), 'mp').astype(F32)  49.9 us
    pallas_call x1, Pallas kernels, attn_bwd(): pl.pallas_call(partial(attn_bwd_kernel, heads // GROUP), grid=(rows // QB...  31.4 us
    unnamed x10, waiting for transfers between devices  30.8 us
    all_gather x1, waiting for transfers between devices, body(): heads_all = lax.all_gather(heads_out, 'mp', axis=1, tiled=True)  29.2 us
    psum x1, waiting for transfers between devices, body(): late = lax.optimization_barrier(lax.psum(late, 'dp'))  26.9 us
    pallas_call x1, Pallas kernels, attn_fwd(): pl.pallas_call(partial(attn_fwd_kernel, heads // GROUP), grid=(rows // QB...  23.2 us
  transfers between devices with their start and end apart: 9, of which 8 were waited for; matrix products, arithmetic and copies ran while one was open for 16% of the time, Pallas kernels for 4%

profile of v1, /device:TPU:0, one launch (start us, length us, event | category | flops | bytes accessed | tf_op | source)
XLA Modules:
  0.0 571.0 jit_solution(16540079639510436289)
XLA Ops:
  10.3 0.8 copy.86
  13.5 1.8 subtract_convert_fusion
  15.2 1.3 fusion.50
  16.6 1.3 broadcast_in_dim.50.gain
  17.8 1.3 broadcast_in_dim.51.shift
  19.1 3.9 copy.68
  23.0 0.8 copy.73.qb_col
  23.8 0.8 copy.74.vb_col
  25.2 1.0 broadcast_in_dim.98.kwin
  26.3 0.8 pad_maximum_fusion
  27.1 1.2 compare_select_fusion.qwin
  29.0 0.9 compare_convert_fusion.khot
  30.0 9.5 %all-gather.5.cloned.1.call-done.tok = bf16[1024,768]{1,0:T(8,128)(2,1)} async-done(((bf16[1024,384]{1,0:T(8,128)(2,1)}), bf16[1024,768]{1,0:T(8,128)(2,1)}) %all-gather.5.cloned.1.call-update) | async-done | bytes 1572880 | tf_op jit(solution)/shard_map/all_gather | solution.py:295
  39.5 23.2 %attn_fwd.1 = (bf16[1024,768]{1,0:T(8,128)(2,1)}, bf16[384,1024]{1,0:T(8,128)(2,1)}, bf16[1152,384]{1,0:T(8,128)(2,1)}, bf16[384,1152]{1,0:T(8,128)(2,1)}, bf16[...) custom-call(bf16[1024,768]{1,0:T(8,128)(2,1)} %all-gather.5.cloned.1.call-done.tok, ...), custom_call_target="tpu_custom_call" | custom-call | tf_op jit(solution)/shard_map/attn_fwd/pallas_call | solution.py:152
  63.9 29.2 %all-gather.7.cloned.1.call-done = bf16[1024,768]{1,0:T(8,128)(2,1)} async-done(((bf16[1024,384]{1,0:T(8,128)(2,1)}), bf16[1024,768]{1,0:T(8,128)(2,1)}) %all-gather.7.cloned.1.call-update) | async-done | bytes 1572880 | tf_op jit(solution)/shard_map/all_gather | solution.py:304
  93.2 3.8 fusion.51
  97.5 1.1 copy-done.1
  98.6 1.2 copy-done.32
  99.8 5.0 fusion.43
  104.8 17.0 %all-gather.11.cloned.1.call-done = bf16[1024,768]{1,0:T(8,128)(2,1)} async-done(((bf16[1024,384]{1,0:T(8,128)(2,1)}), bf16[1024,768]{1,0:T(8,128)(2,1)}) %all-gather.11.cloned.1.call-update) | async-done | bytes 1572880 | tf_op jit(solution)/shard_map/all_gather | solution.py:297
  121.8 19.9 %fusion.44 = (bf16[1536]{0:T(1024)(128)(2,1)}, bf16[1024,1536]{1,0:T(8,128)(2,1)S(1)}, f32[1024,1536]{1,0:T(8,128)}) fusion(f32[1024,1536]{1,0:T(8,128)} %fusion.43, f32[1536]{0:T(1024)S(1)} %copy-done.24, bf16[1024,768]{1,0:T(8,128)(2,1)} %all-gather.11.cloned.1.call-done, bf16[1536,768]{1,0:T(8,128)(2,1)S(1)} %copy-done), kind=kOutput, calls=%fused_computation.118 | convolution fusion | flops 2532309504 | bytes 19670016 | tf_op jit(solution)/shard_map/td,fd->tf/dot_general | solution.py:311
  141.7 1.7 copy-done.37
  143.4 3.8 convolution_convert_fusion.4
  147.4 0.9 fusion.26.qhot
  149.0 49.9 %all-reduce.10.cloned.1.call-done = bf16[1024,768]{1,0:T(8,128)(2,1)} async-done(((bf16[1024,768]{1,0:T(8,128)(2,1)}), bf16[1024,768]{1,0:T(8,128)(2,1)}) %all-reduce.10.cloned.1.call-update) | async-done | bytes 1572880 | tf_op jit(solution)/shard_map/psum | solution.py:315
  198.9 3.3 fusion.14
  202.6 1.8 fusion.15
  204.5 2.7 convert_reduce_fusion.2
  207.2 1.7 copy-done.5
  208.9 1.7 fusion.24.dot_t
  210.6 31.4 %attn_bwd.1 = (bf16[1024,384]{1,0:T(8,128)(2,1)}, bf16[1024,384]{1,0:T(8,128)(2,1)}, bf16[1024,384]{1,0:T(8,128)(2,1)}, f32[768,64]{1,0:T(8,128)}) custom-call(bf16[384,1024]{1,0:T(8,128)(2,1)} %get-tuple-element.35.qt, bf16[1152,384]{1,0:T(8,128)(2,1)} %get-tuple-element.36.kx, bf16[384,1152]{1,0:T(8,128)(2,1)} %get-tuple-element.37.kt, ...), custom_call_target="tpu_custom_call" | custom-call | tf_op jit(solution)/shard_map/attn_bwd/pallas_call | solution.py:228
  242.0 2.1 fusion.47
  244.1 1.3 constant_dynamic-update-slice_fusion.1
  245.4 0.8 fusion.48
  246.2 1.4 copy-done.18
  247.6 3.4 convolution_convert_fusion.3
  251.4 6.3 %multiply_convert_fusion = bf16[1024,1536]{1,0:T(8,128)(2,1)S(1)} fusion(f32[1024,1536]{1,0:T(8,128)} %get-tuple-element.111, f32[1024,1536]{1,0:T(8,128)} %fusion.43, f32[1536]{0:T(1024)S(1)} %copy-done.24), kind=kLoop, calls=%fused_computation.3 | loop fusion | flops 6291456 | bytes 15734784 | tf_op jit(solution)/shard_map/convert_element_type | solution.py:308
  257.7 4.0 convolution_convert_fusion
  262.5 4.2 convolution_convert_fusion.1
  266.8 5.7 convolution_convert_fusion.5
  272.5 2.6 copy.84
  276.1 1.7 convert_reduce_fusion
  277.8 2.0 fusion.17
  281.8 1.3 reshape.242
  283.1 0.9 reshape.243
  283.9 2.4 fusion.25
  286.6 3.7 convolution_convert_fusion.7
  290.3 3.4 convolution_convert_fusion.2
  293.7 9.0 %all-reduce.12.cloned.1.call-done = bf16[1024,768]{1,0:T(8,128)(2,1)} async-done(((bf16[1024,768]{1,0:T(8,128)(2,1)}), bf16[1024,768]{1,0:T(8,128)(2,1)}) %all-reduce.12.cloned.1.call-update) | async-done | bytes 1572880 | tf_op jit(solution)/shard_map/psum | solution.py:334
  302.8 3.3 fusion.16
  306.4 1.7 reduce
  309.9 113.9 %all-reduce.16.cloned.1.call-done = (bf16[768,1536]{1,0:T(8,128)(2,1)}, bf16[1536,768]{1,0:T(8,128)(2,1)}) async-done(((bf16[768,1536]{1,0:T(8,128)(2,1)}, bf16[1536,768]{1,0:T(8,128)(2,1)}), (bf16[768,1536]{1,0:T(8,128)(2,1)}, bf16[1536,768]{1,0:T(8,128)(2,1)})) %all-reduce.16.cloned.1.call-update) | async-done | bytes 4718608 | tf_op jit(solution)/shard_map/psum | solution.py:353
  423.9 28.8 %reduce-scatter.4.cloned.1.call-done = bf16[384,1024]{1,0:T(8,128)(2,1)} async-done(((bf16[768,1024]{1,0:T(8,128)(2,1)}), bf16[384,1024]{1,0:T(8,128)(2,1)}) %reduce-scatter.4.cloned.1.call-update) | async-done | bytes 786448
  452.6 1.5 copy.85
  454.1 4.6 convert_element_type.145
  458.8 2.5 convert_element_type.146
  461.3 61.9 %psum.55 = bf16[8940]{0:T(1024)(128)(2,1)S(1)} all-reduce(bf16[8940]{0:T(1024)(128)(2,1)S(1)} %dynamic-update-slice.8), channel_id=1, replica_groups=mesh['dp'=16,'mp'=2] {'dp'}, use_global_device_ids=true, to_apply=%region_28.29 | all-reduce | flops 8940 | bytes 35760 | tf_op jit(solution)/shard_map/psum | solution.py:357
  523.3 3.0 fusion.46
  526.3 1.1 fusion.21
  527.4 1.0 copy-done.4
  528.4 1.1 add_convert_fusion.2
  529.5 26.9 %all-reduce.14.cloned.1.call-done = (bf16[1152,768]{1,0:T(8,128)(2,1)}, bf16[384,768]{1,0:T(8,128)(2,1)}) async-done(((bf16[1152,768]{1,0:T(8,128)(2,1)}, bf16[384,768]{1,0:T(8,128)(2,1)}), (bf16[1152,768]{1,0:T(8,128)(2,1)}, bf16[384,768]{1,0:T(8,128)(2,1)})) %all-reduce.14.cloned.1.call-update) | async-done | bytes 2359312 | tf_op jit(solution)/shard_map/psum | solution.py:357
  557.7 4.0 copy.80
  563.1 1.1 convert_element_type.144
  (139 shorter events, 18.2 us)
Async XLA Ops:
  7.2 114.6 %copy-start = (bf16[1536,768]{1,0:T(8,128)(2,1)S(1)}, bf16[1536,768]{1,0:T(8,128)(2,1)}, u32[]{:S(2)}) copy-start(bf16[1536,768]{1,0:T(8,128)(2,1)} %param.33) | copy-start | bytes 7077892
  7.2 32.3 %all-gather.5.cloned.1.call-start = ((), (), s32[]{:S(2)}) async-start(), calls=%async_computation.1 | async-start | bytes 2359296 | tf_op jit(solution)/shard_map/all_gather | solution.py:295
  7.9 56.0 %all-gather.9.cloned.1.call-start = ((), (), s32[]{:S(2)}) async-start(), calls=%async_computation.3 | async-start | bytes 1769472 | tf_op jit(solution)/shard_map/all_gather | solution.py:296
  8.7 84.5 %all-gather.7.cloned.1.call-start = ((), (), s32[]{:S(2)}) async-start(), calls=%async_computation.2 | async-start | bytes 2359296 | tf_op jit(solution)/shard_map/all_gather | solution.py:304
  11.2 13.7 %copy-start.23 = (s32[4096]{0:T(1024)}, s32[4096]{0:T(1024)S(1)}, u32[]{:S(2)}) copy-start(s32[4096]{0:T(1024)S(1)} %eq.88) | copy-start | bytes 49156
  39.5 53.7 %copy-start.35 = (f32[768]{0:T(1024)S(1)}, f32[768]{0:T(1024)}, u32[]{:S(2)}) copy-start(f32[768]{0:T(1024)} %param.28) | copy-start | bytes 9220
  62.7 59.0 %all-gather.11.cloned.1.call-start = ((), (), s32[]{:S(2)}) async-start(), calls=%async_computation.4 | async-start | bytes 2359296 | tf_op jit(solution)/shard_map/all_gather | solution.py:297
  63.3 135.5 %all-reduce.10.cloned.1.call-start = ((), (), s32[]{:S(2)}) async-start(), calls=%async_computation.5 | async-start | bytes 3145728 | tf_op jit(solution)/shard_map/psum | solution.py:315
  96.9 1.7 copy-start.1
  97.0 1.7 copy-start.20
  97.0 2.8 copy-start.32
  97.0 2.8 copy-start.36
  99.8 22.0 %copy-start.24 = (f32[1536]{0:T(1024)S(1)}, f32[1536]{0:T(1024)}, u32[]{:S(2)}) copy-start(f32[1536]{0:T(1024)} %param.32) | copy-start | bytes 18436
  121.8 21.6 %copy-start.33 = (bf16[768,1536]{1,0:T(8,128)(2,1)S(1)}, bf16[768,1536]{1,0:T(8,128)(2,1)}, u32[]{:S(2)}) copy-start(bf16[768,1536]{1,0:T(8,128)(2,1)} %param.31) | copy-start | bytes 7077892
  141.7 1.7 copy-start.37
  147.2 155.6 %all-reduce.12.cloned.1.call-start = ((), (), s32[]{:S(2)}) async-start(), calls=%async_computation.6 | async-start | bytes 3145728 | tf_op jit(solution)/shard_map/psum | solution.py:334
  198.9 3.3 copy-start.2
  198.9 3.8 copy-start.7
  202.1 2.4 copy-start.13
  204.5 4.4 copy-start.11
  207.2 1.7 copy-start.5
  242.0 3.4 copy-start.15
  242.0 5.6 copy-start.8
  246.2 1.4 copy-start.18
  251.1 172.7 %all-reduce.16.cloned.1.call-start = ((), (), s32[]{:S(2)}) async-start(), calls=%async_computation.9 | async-start | bytes 9437184 | tf_op jit(solution)/shard_map/psum | solution.py:353
  251.4 6.3 %copy-start.14 = (bf16[1024,768]{1,0:T(8,128)(2,1)S(1)}, bf16[1024,768]{1,0:T(8,128)(2,1)}, u32[]{:S(2)}) copy-start(bf16[1024,768]{1,0:T(8,128)(2,1)} %all-gather.11.cloned.1.call-done) | copy-start | bytes 4718596
  257.7 4.0 copy-start.9
  257.7 4.0 copy-start.3
  257.7 4.8 copy-start.38
  266.7 185.9 %reduce-scatter.4.cloned.1.call-start = ((), (), s32[]{:S(2)}) async-start(), calls=%async_computation.7 | async-start | bytes 2359296
  272.5 3.0 copy-start.31
  275.1 8.0 %copy-start.17 = (f32[768,64]{1,0:T(8,128)S(1)}, f32[768,64]{1,0:T(8,128)}, u32[]{:S(2)}) copy-start(f32[768,64]{1,0:T(8,128)} %get-tuple-element.44) | copy-start | bytes 589828
  275.1 11.5 %copy-start.10 = (bf16[1024,384]{1,0:T(8,128)(2,1)S(1)}, bf16[1024,384]{1,0:T(8,128)(2,1)}, u32[]{:S(2)}) copy-start(bf16[1024,384]{1,0:T(8,128)(2,1)} %get-tuple-element.34) | copy-start | bytes 2359300
  275.1 281.3 %all-reduce.14.cloned.1.call-start = ((), (), s32[]{:S(2)}) async-start(), calls=%async_computation.8 | async-start | bytes 4718592 | tf_op jit(solution)/shard_map/psum | solution.py:357
  286.6 3.7 copy-start.19
  286.6 3.7 copy-start.34
  290.3 12.5 %copy-start.21 = (f32[768]{0:T(1024)S(1)}, f32[768]{0:T(1024)}, u32[]{:S(2)}) copy-start(f32[768]{0:T(1024)} %param.22) | copy-start | bytes 9220
  293.7 12.4 %copy-start.22 = (bf16[8940]{0:T(1024)(128)(2,1)S(1)}, bf16[8940]{0:T(1024)(128)(2,1)}, u32[]{:S(2)}) copy-start(bf16[8940]{0:T(1024)(128)(2,1)} %custom-call) | copy-start | bytes 53644
  293.7 14.6 %copy-start.28 = (bf16[768]{0:T(1024)(128)(2,1)S(1)}, bf16[768]{0:T(1024)(128)(2,1)}, u32[]{:S(2)}) copy-start(bf16[768]{0:T(1024)(128)(2,1)} %get-tuple-element.112) | copy-start | bytes 4612
  293.7 15.0 %copy-start.27 = (bf16[768]{0:T(1024)(128)(2,1)S(1)}, bf16[768]{0:T(1024)(128)(2,1)}, u32[]{:S(2)}) copy-start(bf16[768]{0:T(1024)(128)(2,1)} %get-tuple-element.119) | copy-start | bytes 4612
  293.7 15.2 %copy-start.26 = (bf16[768]{0:T(1024)(128)(2,1)S(1)}, bf16[768]{0:T(1024)(128)(2,1)}, u32[]{:S(2)}) copy-start(bf16[768]{0:T(1024)(128)(2,1)} %get-tuple-element.118) | copy-start | bytes 4612
  293.7 15.4 %copy-start.29 = (bf16[768]{0:T(1024)(128)(2,1)S(1)}, bf16[768]{0:T(1024)(128)(2,1)}, u32[]{:S(2)}) copy-start(bf16[768]{0:T(1024)(128)(2,1)} %reshape.242) | copy-start | bytes 4612
  293.7 15.6 %copy-start.30 = (bf16[1536]{0:T(1024)(128)(2,1)S(1)}, bf16[1536]{0:T(1024)(128)(2,1)}, u32[]{:S(2)}) copy-start(bf16[1536]{0:T(1024)(128)(2,1)} %get-tuple-element.109) | copy-start | bytes 9220
  454.1 4.7 copy-start.12
  523.3 3.0 copy-start.6
  526.3 2.2 copy-start.4
  526.3 2.2 copy-start.25
  556.4 6.6 %copy-start.16 = (bf16[384,768]{1,0:T(8,128)(2,1)S(1)}, bf16[384,768]{1,0:T(8,128)(2,1)}, u32[]{:S(2)}) copy-start(bf16[384,768]{1,0:T(8,128)(2,1)} %get-tuple-element.50) | copy-start | bytes 1769476
Sparse Core Ops, SparseCore 0:
  9.5 29.9 all-gather.4
  41.0 22.7 all-gather.8
  65.9 27.1 all-gather.6
  94.6 27.1 all-gather.10
  147.3 51.5 all-reduce.9
  251.2 51.5 all-reduce.11
  307.0 116.7 all-reduce.15
  426.6 25.9 reduce-scatter.3
  456.8 99.5 all-reduce.13

commit v2 on v1

--- a/solution.py
+++ b/solution.py
@@ -21,6 +21,8 @@
 SCALE = HEAD_DIM ** (-0.5)
 EPS = 1e-05
 NEG = -1e30
+CHUNK = 256
+MESH = pl.DeviceIdType.MESH
 F32 = jnp.float32
 BF16 = jnp.bfloat16
 
@@ -77,16 +79,53 @@
     return jnp.concatenate([tall[2 * CP * j : 2 * CP * (j + 1)] for j in range(GROUP)], axis=1)
 
 
+def dot_tn(a, b):
+    return lax.dot_general(a, b, (((0,), (0,)), ((), ())), preferred_element_type=F32)
+
+
+def peer_of():
+    return 1 - lax.axis_index("mp")
+
+
+def greet():
+    barrier = pltpu.get_barrier_semaphore()
+    pl.semaphore_signal(barrier, inc=1, device_id={"mp": peer_of()}, device_id_type=MESH)
+    pl.semaphore_wait(barrier, 1)
+
+
+def to_peer(src, dst, send_sem, recv_sem):
+    return pltpu.make_async_remote_copy(
+        src_ref=src,
+        dst_ref=dst,
+        send_sem=send_sem,
+        recv_sem=recv_sem,
+        device_id={"mp": peer_of()},
+        device_id_type=MESH,
+    )
+
+
+def rows_copy(src, dst, size, sems, i):
+    at = pl.ds(pl.multiple_of(i * size, size), size)
+    return to_peer(src.at[at], dst.at[at], sems[0].at[i], sems[1].at[i])
+
+
+def half_lanes(index, half):
+    return pl.ds(pl.multiple_of(index * half, 128), half)
+
+
 def attn_fwd_kernel(
     groups, tok, gain, shift, wt, qb_col, vb_col, vb_row, khot, qhott, table, kwin, qwin,
-    a_out, qt, kx, kt, vx, o_out, lse, a_pad, vt,
+    a_out, qt, kx, kt, vx, o_out, peer_out, lse, a_pad, vt, o_all, o_peer, send_sem, recv_sem,
 ):
     step = pl.program_id(0)
+    last = tok.shape[0] // QB - 1
     rows_all = tok.shape[0]
     width = qt.shape[0]
+    sems = (send_sem, recv_sem)
 
     @pl.when(step == 0)
     def _():
+        greet()
         zero = jnp.zeros((HALO, tok.shape[1]), BF16)
         a_pad[:HALO, :] = zero
         a_pad[HALO + rows_all :, :] = zero
@@ -128,7 +167,24 @@
             mass = jnp.sum(e, axis=0, keepdims=True)
             outs.append(dot(vt[HEAD_DIM * h : HEAD_DIM * (h + 1), span], e.astype(BF16)) / mass)
             lse[h : h + 1, :] = peak + jnp.log(mass)
-        o_out[:, lanes] = jnp.concatenate(outs, axis=0).T.astype(BF16)
+        o_all[pl.ds(start, QB), lanes] = jnp.concatenate(outs, axis=0).T.astype(BF16)
+
+    @pl.when(step > 0)
+    def _():
+        rows_copy(o_all, o_peer, QB, sems, step - 1).start()
+
+    @pl.when(step == last)
+    def _():
+        o_out[...] = o_all[...]
+        rows_copy(o_all, o_peer, QB, sems, last).start()
+
+        def finish(i, carry):
+            copy = rows_copy(o_all, o_peer, QB, sems, i)
+            copy.wait()
+            return carry
+
+        lax.fori_loop(0, last + 1, finish, 0)
+        peer_out[...] = o_peer[...]
 
 
 def whole(a):
@@ -141,6 +197,10 @@
 
 def cols(n):
     return pl.BlockSpec((n, QB), lambda i: (0, i))
+
+
+def two_sems(n):
+    return [pltpu.SemaphoreType.DMA((n,)), pltpu.SemaphoreType.DMA((n,))]
 
 
 def attn_fwd(tok, gain, shift, wt, qb_col, vb_col, vb_row, khot, qhott, table, kwin, qwin):
@@ -156,27 +216,144 @@
         + [cols(CP), whole(table), whole(kwin), cols(1)],
         out_specs=[
             same(rows, model), same(width, rows), same(ext, width), same(width, ext), same(ext, width),
-            pl.BlockSpec((QB, width), lambda i: (i, 0)), cols(heads),
+            same(rows, width), same(rows, width), cols(heads),
         ],
         out_shape=[
             shape((rows, model), BF16), shape((width, rows), BF16), shape((ext, width), BF16),
             shape((width, ext), BF16), shape((ext, width), BF16), shape((rows, width), BF16),
-            shape((heads, rows), F32),
-        ],
-        scratch_shapes=[pltpu.VMEM((ext, model), BF16), pltpu.VMEM((width, ext), BF16)],
+            shape((rows, width), BF16), shape((heads, rows), F32),
+        ],
+        scratch_shapes=[
+            pltpu.VMEM((ext, model), BF16), pltpu.VMEM((width, ext), BF16),
+            pltpu.VMEM((rows, width), BF16), pltpu.VMEM((rows, width), BF16),
+        ] + two_sems(rows // QB),
+        compiler_params=pltpu.CompilerParams(collective_id=0, has_side_effects=True),
         name="attn_fwd",
     )(tok, gain, shift, wt, qb_col, vb_col, vb_row, khot, qhott, table, kwin, qwin)
 
 
+def ffn_kernel(
+    tok, o_own, o_peer, w_own, w_peer, bo, gain, shift, w_in, b_in, w_back, bb, cot,
+    keep, give, gr, dot_t, g_out, g_in, g_back, vec, vec_in,
+    n_s, r_s, h_s, z_s, du_s, gh_s, gh_p, go_s, wide_a, wide_b, send_sem, recv_sem,
+):
+    rows_all, model = tok.shape
+    half = keep.shape[1]
+    chunks = rows_all // CHUNK
+    sems = (send_sem, recv_sem)
+    me = lax.axis_index("mp")
+    own = half_lanes(me, half)
+    other = half_lanes(1 - me, half)
+    greet()
+    vec[...] = jnp.zeros_like(vec)
+    vec_in[...] = jnp.zeros_like(vec_in)
+
+    def forward(c, carry):
+        at = pl.ds(pl.multiple_of(c * CHUNK, CHUNK), CHUNK)
+        x1 = tok[at, :].astype(F32) + dot(o_own[at, :], w_own[...]) + dot(o_peer[at, :], w_peer[...])
+        x1 = x1 + bo[...]
+        center = x1 - jnp.mean(x1, axis=-1, keepdims=True)
+        r = lax.rsqrt(jnp.mean(center * center, axis=-1, keepdims=True) + EPS)
+        n = center * r
+        h = (n * gain[...] + shift[...]).astype(BF16)
+        wide_b[...] = x1
+        n_s[at, :] = n
+        r_s[at, :] = r
+        h_s[at, :] = h
+        u = dot(h, w_in[...]) + b_in[...]
+        cdf = 0.5 * (1.0 + lax.erf(u * (0.5**0.5)))
+        slope = cdf + u * (jnp.exp(-0.5 * u * u) * 0.3989422804014327)
+        z = (u * cdf).astype(BF16)
+        z_s[at, :] = z
+        du = (dot_nt(cot[at, :], w_back[...]) * slope).astype(BF16)
+        du_s[at, :] = du
+        gh_s[at, :] = dot_nt(du, w_in[...]).astype(BF16)
+        vec_in[...] += jnp.sum(du.astype(F32), axis=0, keepdims=True)
+        wide_a[...] = dot(z, w_back[...])
+        rows_copy(gh_s, gh_p, CHUNK, sems, c).start()
+        keep[at, :] = wide_a[:, own] + wide_b[:, own] + bb[:, own]
+        give[at, :] = wide_a[:, other].astype(BF16)
+        return carry
+
+    lax.fori_loop(0, chunks, forward, 0)
+
+    def back_block(i, carry):
+        at = pl.ds(pl.multiple_of(i * CHUNK, CHUNK), CHUNK)
+        g_back[at, :] = dot_tn(z_s[:, at], cot[...]).astype(BF16)
+        return carry
+
+    lax.fori_loop(0, z_s.shape[1] // CHUNK, back_block, 0)
+
+    def in_block(i, carry):
+        at = pl.ds(pl.multiple_of(i * CHUNK, CHUNK), CHUNK)
+        g_in[at, :] = dot_tn(h_s[:, at], du_s[...]).astype(BF16)
+        return carry
+
+    lax.fori_loop(0, model // CHUNK, in_block, 0)
+
+    def backward(c, carry):
+        at = pl.ds(pl.multiple_of(c * CHUNK, CHUNK), CHUNK)
+        rows_copy(gh_s, gh_p, CHUNK, sems, c).wait()
+        gh = gh_s[at, :].astype(F32) + gh_p[at, :].astype(F32)
+        n = n_s[at, :]
+        e = gh * gain[...]
+        gy = cot[at, :].astype(F32)
+        mean_e = jnp.mean(e, axis=-1, keepdims=True)
+        mean_n = jnp.mean(e * n, axis=-1, keepdims=True)
+        gx1 = gy + r_s[at, :] * (e - mean_e - n * mean_n)
+        wide_a[...] = gx1
+        go = gx1.astype(BF16)
+        go_s[at, :] = go
+        dot_t[:, at] = dot_nt(w_own[...], go).astype(BF16)
+        vec[0:1, :] += jnp.sum(gh * n, axis=0, keepdims=True)
+        vec[1:2, :] += jnp.sum(gh, axis=0, keepdims=True)
+        vec[2:3, :] += jnp.sum(go.astype(F32), axis=0, keepdims=True)
+        vec[3:4, :] += jnp.sum(gy, axis=0, keepdims=True)
+        gr[at, :] = wide_a[:, own]
+        return carry
+
+    lax.fori_loop(0, chunks, backward, 0)
+    g_out[...] = dot_tn(o_own[...], go_s[...]).astype(BF16)
+
+
+def ffn(tok, o_own, o_peer, w_own, w_peer, bo, gain, shift, w_in, b_in, w_back, bb, cot):
+    rows, model = tok.shape
+    width = o_own.shape[1]
+    hidden = w_in.shape[1]
+    half = model // 2
+    shape = jax.ShapeDtypeStruct
+    vm = pltpu.VMEM
+    return pl.pallas_call(
+        ffn_kernel,
+        in_specs=[pl.BlockSpec(memory_space=pltpu.VMEM)] * 13,
+        out_specs=[pl.BlockSpec(memory_space=pltpu.VMEM)] * 9,
+        out_shape=[
+            shape((rows, half), F32), shape((rows, half), BF16), shape((rows, half), F32),
+            shape((width, rows), BF16), shape((width, model), BF16), shape((model, hidden), BF16),
+            shape((hidden, model), BF16), shape((8, model), F32), shape((1, hidden), F32),
+        ],
+        scratch_shapes=[
+            vm((rows, model), F32), vm((rows, 1), F32), vm((rows, model), BF16), vm((rows, hidden), BF16),
+            vm((rows, hidden), BF16), vm((rows, model), BF16), vm((rows, model), BF16),
+            vm((rows, model), BF16), vm((CHUNK, model), F32), vm((CHUNK, model), F32),
+        ] + two_sems(rows // CHUNK),
+        compiler_params=pltpu.CompilerParams(collective_id=1, has_side_effects=True),
+        name="ffn",
+    )(tok, o_own, o_peer, w_own, w_peer, bo, gain, shift, w_in, b_in, w_back, bb, cot)
+
+
 def attn_bwd_kernel(
-    groups, qt, kx, kt, vx, dot_t, khot, khott, qhott, qhot, table, kwin, qwin, lse,
-    dq, dk, dv, gcell, dk_acc, dv_acc,
+    groups, keep, give, qt, kx, kt, vx, dot_t, khot, khott, qhott, qhot, table, kwin, qwin, lse,
+    out, dq, dk, dv, gcell, dk_acc, dv_acc, got, send_sem, recv_sem,
 ):
     step = pl.program_id(0)
     rows_all = dk.shape[0]
+    swap = to_peer(give, got, send_sem.at[0], recv_sem.at[0])
 
     @pl.when(step == 0)
     def _():
+        greet()
+        swap.start()
         dk_acc[...] = jnp.zeros_like(dk_acc)
         dv_acc[...] = jnp.zeros_like(dv_acc)
         gcell[...] = jnp.zeros_like(gcell)
@@ -212,34 +389,135 @@
         dk_acc[span, lanes] += dot_nt(jnp.concatenate(dss, axis=1), q_stack)
         dv_acc[span, lanes] += dot_nt(jnp.concatenate(ps, axis=1), do_stack)
 
-    @pl.when(step == pl.num_programs(0) - 1)
+    @pl.when(step == rows_all // QB - 1)
     def _():
-        own = pl.ds(HALO, rows_all)
-        dk[...] = (dk_acc[own, :] * SCALE).astype(BF16)
-        dv[...] = dv_acc[own, :].astype(BF16)
-
-
-def attn_bwd(qt, kx, kt, vx, dot_t, khot, khott, qhott, qhot, table, kwin, qwin, lse):
+        inner_rows = pl.ds(HALO, rows_all)
+        dk[...] = (dk_acc[inner_rows, :] * SCALE).astype(BF16)
+        dv[...] = dv_acc[inner_rows, :].astype(BF16)
+        swap.wait()
+        out[...] = (keep[...] + got[...].astype(F32)).astype(BF16)
+
+
+def attn_bwd(keep, give, qt, kx, kt, vx, dot_t, khot, khott, qhott, qhot, table, kwin, qwin, lse):
     width, rows = qt.shape
     heads = width // HEAD_DIM
     ext = rows + 2 * HALO
+    half = keep.shape[1]
     shape = jax.ShapeDtypeStruct
     rblk = lambda n: pl.BlockSpec((QB, n), lambda i: (i, 0))
     return pl.pallas_call(
         partial(attn_bwd_kernel, heads // GROUP),
         grid=(rows // QB,),
         in_specs=[
+            whole(keep), pl.BlockSpec(memory_space=pltpu.VMEM),
             cols(width), whole(kx), whole(kt), whole(vx), cols(width), whole(khot), whole(khott),
             cols(CP), rblk(CP), whole(table), whole(kwin), cols(1), cols(heads),
         ],
-        out_specs=[rblk(width), same(rows, width), same(rows, width), same(CP * heads, CP)],
+        out_specs=[
+            same(rows, half), rblk(width), same(rows, width), same(rows, width), same(CP * heads, CP),
+        ],
         out_shape=[
-            shape((rows, width), BF16), shape((rows, width), BF16), shape((rows, width), BF16),
-            shape((CP * heads, CP), F32),
-        ],
-        scratch_shapes=[pltpu.VMEM((ext, width), F32), pltpu.VMEM((ext, width), F32)],
+            shape((rows, half), BF16), shape((rows, width), BF16), shape((rows, width), BF16),
+            shape((rows, width), BF16), shape((CP * heads, CP), F32),
+        ],
+        scratch_shapes=[
+            pltpu.VMEM((ext, width), F32), pltpu.VMEM((ext, width), F32), pltpu.VMEM((rows, half), BF16),
+        ] + two_sems(1),
+        compiler_params=pltpu.CompilerParams(collective_id=2, has_side_effects=True),
         name="attn_bwd",
-    )(qt, kx, kt, vx, dot_t, khot, khott, qhott, qhot, table, kwin, qwin, lse)
+    )(keep, give, qt, kx, kt, vx, dot_t, khot, khott, qhott, qhot, table, kwin, qwin, lse)
+
+
+def close_kernel(
+    tok, a, dq, dk, dv, wt, gain, gr, out, g_wt, vec, vec_qv,
+    ga_s, give, got, stat, stat_p, r_s, wide, vec_s, vec_p, send_sem, recv_sem,
+):
+    rows_all, model = tok.shape
+    width = dq.shape[1]
+    half = out.shape[1]
+    chunks = rows_all // CHUNK
+    me = lax.axis_index("mp")
+    own = half_lanes(me, half)
+    other = half_lanes(1 - me, half)
+    greet()
+    vec_s[...] = jnp.zeros_like(vec_s)
+    main = lambda c: rows_copy(give, got, CHUNK, (send_sem.at[0], recv_sem.at[0]), c)
+    side = lambda c: rows_copy(stat, stat_p, CHUNK, (send_sem.at[1], recv_sem.at[1]), c)
+    lane = lax.broadcasted_iota(jnp.int32, (CHUNK, 128), 1)
+
+    def norms(at):
+        x = tok[at, :].astype(F32)
+        center = x - jnp.mean(x, axis=-1, keepdims=True)
+        r = lax.rsqrt(jnp.mean(center * center, axis=-1, keepdims=True) + EPS)
+        return center * r, r
+
+    def forward(c, carry):
+        at = pl.ds(pl.multiple_of(c * CHUNK, CHUNK), CHUNK)
+        ga = dot(dq[at, :], wt[:width, :]) + dot(dk[at, :], wt[width : 2 * width, :])
+        ga = ga + dot(dv[at, :], wt[2 * width :, :])
+        wide[...] = ga
+        give[at, :] = wide[:, other].astype(BF16)
+        ga_s[at, :] = wide[:, own]
+        n, r = norms(at)
+        e = ga * gain[...]
+        first = jnp.mean(e, axis=-1, keepdims=True)
+        second = jnp.mean(e * n, axis=-1, keepdims=True)
+        stat[at, :] = jnp.where(lane == 0, first, jnp.where(lane == 1, second, 0.0))
+        vec_s[0:1, :] += jnp.sum(ga * n, axis=0, keepdims=True)
+        vec_s[1:2, :] += jnp.sum(ga, axis=0, keepdims=True)
+        main(c).start()
+        side(c).start()
+        return carry
+
+    lax.fori_loop(0, chunks, forward, 0)
+    vectors = to_peer(vec_s, vec_p, send_sem.at[2, 0], recv_sem.at[2, 0])
+    for k, item in enumerate((dq, dk, dv)):
+        g_wt[width * k : width * (k + 1), :] = dot_tn(item[...], a[...]).astype(BF16)
+    vectors.start()
+    vec_qv[0:1, :] = jnp.sum(dq[...].astype(F32), axis=0, keepdims=True)
+    vec_qv[1:2, :] = jnp.sum(dv[...].astype(F32), axis=0, keepdims=True)
+
+    def backward(c, carry):
+        at = pl.ds(pl.multiple_of(c * CHUNK, CHUNK), CHUNK)
+        main(c).wait()
+        side(c).wait()
+        sums = stat[at, :] + stat_p[at, :]
+        n, r = norms(at)
+        wide[...] = n
+        e = (ga_s[at, :] + got[at, :].astype(F32)) * gain[:, own]
+        gx = gr[at, :] + r * (e - sums[:, 0:1] - wide[:, own] * sums[:, 1:2])
+        out[at, :] = gx.astype(BF16)
+        return carry
+
+    lax.fori_loop(0, chunks, backward, 0)
+    vectors.wait()
+    vec[...] = vec_s[...] + vec_p[...]
+
+
+def close(tok, a, dq, dk, dv, wt, gain, gr):
+    rows, model = tok.shape
+    width = dq.shape[1]
+    half = gr.shape[1]
+    chunks = rows // CHUNK
+    shape = jax.ShapeDtypeStruct
+    vm = pltpu.VMEM
+    sems = pltpu.SemaphoreType.DMA((3, chunks))
+    return pl.pallas_call(
+        close_kernel,
+        in_specs=[pl.BlockSpec(memory_space=pltpu.VMEM)] * 8,
+        out_specs=[pl.BlockSpec(memory_space=pltpu.VMEM)] * 4,
+        out_shape=[
+            shape((rows, half), BF16), shape((3 * width, model), BF16), shape((8, model), F32),
+            shape((8, width), F32),
+        ],
+        scratch_shapes=[
+            vm((rows, half), F32), vm((rows, half), BF16), vm((rows, half), BF16), vm((rows, 128), F32),
+            vm((rows, 128), F32), vm((rows, 1), F32), vm((CHUNK, model), F32), vm((8, model), F32),
+            vm((8, model), F32), sems, sems,
+        ],
+        compiler_params=pltpu.CompilerParams(collective_id=3, has_side_effects=True),
+        name="close",
+    )(tok, a, dq, dk, dv, wt, gain, gr)
 
 
 def window_data(crop_counts, crop_patches, rel_index, rel_table, rows):
@@ -291,78 +569,49 @@
     khot, khott, qhott, qhot, table, kwin, qwin, offset_hot = window_data(
         crop_counts, crop_patches, rel_index, rel_table, rows
     )
-    column_start = lax.axis_index("mp") * part_width
+    me = lax.axis_index("mp")
     whole_in = lax.all_gather(tokens, "mp", axis=1, tiled=True)
     w_out_all = lax.all_gather(w_out, "mp", axis=0, tiled=True)
+    w_peer = lax.dynamic_slice_in_dim(w_out_all, (1 - me) * width, width, 0)
     whole_cot = lax.all_gather(cotangent, "mp", axis=1, tiled=True)
     wt = jnp.transpose(w_qkv, (1, 2, 0)).reshape(3 * width, model)
-    mixer_in, qt, kx, kt, vx, heads_out, lse = attn_fwd(
+    mixer_in, qt, kx, kt, vx, heads_out, heads_peer, lse = attn_fwd(
         whole_in, ln1_gain[None, :], ln1_shift[None, :], wt, qv_bias[0][:, None], qv_bias[1][:, None],
         qv_bias[1][None, :], khot, qhott, table, kwin, qwin,
     )
-    block_input = whole_in.astype(F32)
-    heads_all = lax.all_gather(heads_out, "mp", axis=1, tiled=True)
-    residual = block_input + dot(heads_all, w_out_all) + b_out
-    hidden_in = layer_norm(residual, ln2_gain, ln2_shift).astype(BF16)
-    hidden_pre = dot(hidden_in, w_in) + b_in
-    activated = jax.nn.gelu(hidden_pre, approximate=False).astype(BF16)
-    back_terms = dot(activated, w_back)
-    grad_w_back = jnp.einsum("tf,td->fd", activated, whole_cot, preferred_element_type=F32)
-    grad_act = jnp.einsum("td,fd->tf", whole_cot, w_back, preferred_element_type=F32)
-    unused_gelu, gelu_pull = jax.vjp(partial(jax.nn.gelu, approximate=False), hidden_pre)
-    grad_pre = gelu_pull(grad_act)[0].astype(BF16)
-    hidden_terms = jnp.einsum("tf,df->td", grad_pre, w_in, preferred_element_type=F32)
-    grad_normed_two = lax.psum(hidden_terms.astype(BF16), "mp").astype(F32)
-    grad_b_back = jnp.sum(whole_cot.astype(F32), axis=0)
-    grad_b_in = jnp.sum(grad_pre.astype(F32), axis=0)
-    grad_w_in = jnp.einsum("td,tf->df", hidden_in, grad_pre, preferred_element_type=F32)
-    unused_two, norm_two_pull = jax.vjp(layer_norm, residual, ln2_gain, ln2_shift)
-    grad_resid_norm, grad_g2, grad_c2 = norm_two_pull(grad_normed_two)
-    grad_resid = whole_cot.astype(F32) + grad_resid_norm
-    grad_mixer = grad_resid.astype(BF16)
-    grad_b_out = jnp.sum(grad_mixer.astype(F32), axis=0)
-    grad_w_out = jnp.einsum("tf,td->fd", heads_out, grad_mixer, preferred_element_type=F32)
-    grad_heads_t = jnp.einsum("fd,td->ft", w_out, grad_mixer, preferred_element_type=F32).astype(BF16)
-    grad_query, grad_key, grad_value, gcell = attn_bwd(
-        qt, kx, kt, vx, grad_heads_t, khot, khott, qhott, qhot, table, kwin, qwin, lse
+    keep, give, gr, dot_t, grad_w_out, grad_w_in, grad_w_back, vec2, grad_b_in = ffn(
+        whole_in, heads_out, heads_peer, w_out, w_peer, b_out[None, :], ln2_gain[None, :], ln2_shift[None, :],
+        w_in, b_in[None, :], w_back, b_back[None, :], whole_cot,
+    )
+    early = lax.psum((grad_w_in, grad_w_back), "dp")
+    out_half, grad_query, grad_key, grad_value, gcell = attn_bwd(
+        keep, give, qt, kx, kt, vx, dot_t, khot, khott, qhott, qhot, table, kwin, qwin, lse
     )
     grad_table = jnp.einsum(
         "pm,hp->mh", offset_hot, gcell.reshape(heads, CP * CP), precision=highest
     )
-    grad_qkv = jnp.concatenate([grad_query, grad_key, grad_value], axis=1)
-    mixer_terms = dot(grad_qkv, wt)
-    grad_normed_one = lax.psum(mixer_terms.astype(BF16), "mp").astype(F32)
-    grad_wt = jnp.einsum("tf,td->fd", grad_qkv, mixer_in, preferred_element_type=F32)
-    grad_qv_bias = jnp.stack(
-        [jnp.sum(grad_query.astype(F32), axis=0), jnp.sum(grad_value.astype(F32), axis=0)]
-    )
-    out_half = (
-        lax.psum_scatter(back_terms.astype(BF16), "mp", scatter_dimension=1, tiled=True).astype(F32)
-        + lax.dynamic_slice_in_dim(b_back, column_start, part_width, 0)
-        + lax.dynamic_slice_in_dim(residual, column_start, part_width, 1)
-    ).astype(BF16)
-    unused_one, norm_one_pull = jax.vjp(layer_norm, block_input, ln1_gain, ln1_shift)
-    grad_input_norm, grad_g1, grad_c1 = norm_one_pull(grad_normed_one)
-    grad_input = grad_resid + grad_input_norm
-    grad_half = lax.dynamic_slice_in_dim(grad_input, column_start, part_width, 1).astype(BF16)
-
-    vectors = [grad_g1, grad_c1, grad_b_out, grad_g2, grad_c2, grad_b_back]
-    packed = jnp.concatenate(
-        [item.reshape(-1) for item in vectors + [grad_qv_bias, grad_b_in, grad_table]]
-    )
-    early = lax.psum((grad_w_in.astype(BF16), grad_w_back.astype(BF16)), "dp")
-    early, late = lax.optimization_barrier(
-        (early, (grad_wt.astype(BF16), grad_w_out.astype(BF16), packed.astype(BF16)))
-    )
+    grad_half, grad_wt, vec1, vec_qv = close(
+        whole_in, mixer_in, grad_query, grad_key, grad_value, wt, ln1_gain[None, :], gr
+    )
+    small = [vec1[0], vec1[1], vec2[2], vec2[0], vec2[1], vec2[3], vec_qv[:2], grad_b_in[0], grad_table]
+    sizes = [item.shape for item in small]
+    packed = jnp.concatenate([item.reshape(-1) for item in small])
+    pad_rows = -(-packed.size // (16 * model)) * 16
+    packed = jnp.pad(packed, (0, pad_rows * model - packed.size)).reshape(pad_rows, model).astype(BF16)
+    early, late = lax.optimization_barrier((early, (grad_wt, grad_w_out, packed)))
     late = lax.optimization_barrier(lax.psum(late, "dp"))
     grad_w_in, grad_w_back = (item.astype(F32) for item in early)
     grad_wt, grad_w_out, packed = (item.astype(F32) for item in late)
     grad_w_qkv = jnp.transpose(grad_wt.reshape(3, width, model), (2, 0, 1))
+    packed = packed.reshape(-1)
     at = 0
     outs = []
-    for item in vectors + [grad_qv_bias, grad_b_in, grad_table]:
-        outs.append(packed[at : at + item.size].reshape(item.shape))
-        at += item.size
+    for shape in sizes:
+        size = 1
+        for extent in shape:
+            size *= extent
+        outs.append(packed[at : at + size].reshape(shape))
+        at += size
     grad_g1, grad_c1, grad_b_out, grad_g2, grad_c2, grad_b_back, grad_qv_bias, grad_b_in, grad_table = outs
     return (
         out_half,

time: 577 us -> 397 us (0.69); the launches traced: 571 us -> 397 us
  waiting for transfers between devices: 286 us -> 110 us
  Pallas kernels: 54.6 us -> 166 us
  matrix products: 62.7 us -> 2.45 us
  other arithmetic: 48.3 us -> 15.1 us
  local copies, waits for them, and re-layouts: 40.4 us -> 27.5 us
    psum x3 -> x1, waiting for transfers between devices: 173 us -> 40.1 us  [body(): early = lax.psum((grad_w_in, grad_w_back), 'dp')]
    pallas_call x0 -> x2, Pallas kernels: none -> 84.8 us  [the longest x1 48.2 us: ffn(): pl.pallas_call(ffn_kernel, in_specs=[pl.BlockSpec(memory_space=pltpu.VMEM...]
    dot_general x11 -> x0, matrix products: 58.6 us -> none  [the longest x1 19.9 us: body(): jnp.einsum('td,fd->tf', whole_cot, w_back, preferred_element_type=F32)]
    all_gather x1 -> x0, waiting for transfers between devices: 29.2 us -> none  [body(): heads_all = lax.all_gather(heads_out, 'mp', axis=1, tiled=True)]
    unnamed x10 -> x5, waiting for transfers between devices: 30.8 us -> 2.09 us
    pallas_call x1, Pallas kernels: 23.2 us -> 48.3 us  [attn_fwd(): pl.pallas_call(partial(attn_fwd_kernel, heads // GROUP), grid=(rows // QB...]
    reduce_sum x11 -> x0, other arithmetic: 23 us -> none  [the longest x4 10.2 us: layer_norm(): return center * lax.rsqrt(spread + EPS) * gain + shift]
    all_gather x1, waiting for transfers between devices: 9.54 us -> 26.8 us  [body(): whole_in = lax.all_gather(tokens, 'mp', axis=1, tiled=True)]
  transfers between devices with their start and end apart: 9 -> 5, of which waited for: 8 -> 4; matrix products, arithmetic and copies ran while one was open for 16% -> 8% of each run, Pallas kernels for 4% -> 30%
where the time goes in v2:
time: 397 us
  Pallas kernels  166 us (42%)
  waiting for transfers between devices  110 us (28%)
  blocking collectives  60.6 us (15%)
  local copies, waits for them, and re-layouts  27.5 us (7%)
  other arithmetic  15.1 us (4%)
  between operations  14.7 us (4%)
    psum x1, blocking collectives, body(): late = lax.optimization_barrier(lax.psum(late, 'dp'))  60.6 us
    pallas_call x1, Pallas kernels, attn_fwd(): pl.pallas_call(partial(attn_fwd_kernel, heads // GROUP), grid=(rows // QB...  48.3 us
    pallas_call x1, Pallas kernels, ffn(): pl.pallas_call(ffn_kernel, in_specs=[pl.BlockSpec(memory_space=pltpu.VMEM...  48.2 us
    psum x1, waiting for transfers between devices, body(): early = lax.psum((grad_w_in, grad_w_back), 'dp')  40.1 us
    pallas_call x1, Pallas kernels, close(): pl.pallas_call(close_kernel, in_specs=[pl.BlockSpec(memory_space=pltpu.VM...  36.6 us
    psum x1, waiting for transfers between devices, body(): late = lax.optimization_barrier(lax.psum(late, 'dp'))  35 us
    pallas_call x1, Pallas kernels, attn_bwd(): pl.pallas_call(partial(attn_bwd_kernel, heads // GROUP), grid=(rows // QB...  33.2 us
    all_gather x1, waiting for transfers between devices, body(): whole_in = lax.all_gather(tokens, 'mp', axis=1, tiled=True)  26.8 us
  transfers between devices with their start and end apart: 5, of which 4 were waited for; matrix products, arithmetic and copies ran while one was open for 8% of the time, Pallas kernels for 30%

profile of v2, /device:TPU:0, one launch (start us, length us, event | category | flops | bytes accessed | tf_op | source)
XLA Modules:
  0.0 396.9 jit_solution(4354139079209857417)
XLA Ops:
  7.3 0.7 all-gather.6.cloned.1.call-update
  8.0 0.7 all-gather.4.cloned.1.call-update
  8.7 0.7 all-gather.8.cloned.1.call-update
  9.5 0.8 fusion.14
  10.4 0.5 slice.118
  11.0 0.8 copy.62
  12.6 0.2 convert_reduce_fusion
  12.8 0.8 fusion.11
  13.6 1.1 subtract_convert_fusion
  14.6 0.6 subtract_select_fusion
  15.4 1.0 broadcast_in_dim.90.kwin
  16.5 0.2 stack_reshape.6
  16.7 0.2 stack_reshape.7
  16.9 0.6 fusion.17
  17.5 0.8 copy.55.qb_col
  18.3 0.8 copy.56.vb_col
  19.1 2.2 copy.50
  21.4 0.6 broadcast_in_dim.77.gain
  21.9 0.6 broadcast_in_dim.78.shift
  22.5 0.6 broadcast_in_dim.88.b_in
  23.1 0.6 broadcast_in_dim.85.bo
  23.7 0.6 broadcast_in_dim.86.gain
  24.3 0.6 broadcast_in_dim.87.shift
  24.9 0.6 broadcast_in_dim.89.bb
  25.5 0.8 pad_maximum_fusion
  26.3 1.2 compare_select_fusion.qwin
  27.5 0.7 fusion.7.qhott
  28.2 0.9 compare_convert_fusion.khot
  29.2 6.0 %all-gather.6.cloned.1.call-done = bf16[768,768]{1,0:T(8,128)(2,1)} async-done(((bf16[384,768]{1,0:T(8,128)(2,1)}), bf16[768,768]{1,0:T(8,128)(2,1)}) %all-gather.6.cloned.1.call-update) | async-done | bytes 1179664 | tf_op jit(solution)/shard_map/all_gather | solution.py:574
  35.1 1.9 constant_dynamic-slice_fusion.w_peer
  37.0 26.8 %all-gather.4.cloned.1.call-done.tok = bf16[1024,768]{1,0:T(8,128)(2,1)} async-done(((bf16[1024,384]{1,0:T(8,128)(2,1)}), bf16[1024,768]{1,0:T(8,128)(2,1)}) %all-gather.4.cloned.1.call-update) | async-done | bytes 1572880 | tf_op jit(solution)/shard_map/all_gather | solution.py:573
  63.9 48.3 %attn_fwd.1 = (bf16[1024,768]{1,0:T(8,128)(2,1)}, bf16[384,1024]{1,0:T(8,128)(2,1)}, bf16[1152,384]{1,0:T(8,128)(2,1)}, bf16[384,1152]{1,0:T(8,128)(2,1)}, bf16[...) custom-call(bf16[1024,768]{1,0:T(8,128)(2,1)} %all-gather.4.cloned.1.call-done, ...), custom_call_target="tpu_custom_call" | custom-call | tf_op jit(solution)/shard_map/attn_fwd/pallas_call | solution.py:212
  112.2 48.2 %ffn.1 = (f32[1024,384]{1,0:T(8,128)}, bf16[1024,384]{1,0:T(8,128)(2,1)}, f32[1024,384]{1,0:T(8,128)}, bf16[384,1024]{1,0:T(8,128)(2,1)}, bf16[384,768]{1,0:T(8,...) custom-call(bf16[1024,768]{1,0:T(8,128)(2,1)} %all-gather.4.cloned.1.ca, ...), custom_call_target="tpu_custom_call" | custom-call | tf_op jit(solution)/shard_map/ffn/pallas_call | solution.py:326
  160.5 0.9 fusion.5.qhot
  161.5 0.7 fusion.6.khott
  162.1 33.2 %attn_bwd.1 = (bf16[1024,384]{1,0:T(8,128)(2,1)}, bf16[1024,384]{1,0:T(8,128)(2,1)}, bf16[1024,384]{1,0:T(8,128)(2,1)}, bf16[1024,384]{1,0:T(8,128)(2,1)}, f32[768,64]{1,0:T(8,128)}) custom-call(f32[1024,384]{1,0:T(8,128)} %get-tuple-element.51.keep, bf16[1024,384]{1,0:T(8,128)(2,1)} %get-tuple-element.52.give, bf16[384,1024]{1,0:T(8,128)(2,1)} %get-tuple-element.53.qt, ...), custom_call_target="tpu_custom_call" | custom-call | tf_op jit(solution)/shard_map/attn_bwd/pallas_call | solution.py:408
  195.4 36.6 %close.1 = (bf16[1024,384]{1,0:T(8,128)(2,1)}, bf16[1152,768]{1,0:T(8,128)(2,1)}, f32[8,768]{1,0:T(8,128)}, f32[8,384]{1,0:T(8,128)}) custom-call(bf16[1024,768]{1,0:T(8,128)(2,1)} %all-gather.4.cloned.1.call-done.tok, bf16[1024,768]{1,0:T(8,128)(2,1)} %get-tuple-element.60.a, bf16[1024,384]{1,0:T(8,128)(2,1)} %get-tuple-element.61.dq, ...), custom_call_target="tpu_custom_call" | custom-call | tf_op jit(solution)/shard_map/close/pallas_call | solution.py:505
  231.9 0.7 convert.39
  232.7 0.7 slice.151
  233.6 1.4 fusion.4
  235.3 0.2 dynamic-update-slice
  235.5 0.2 dynamic-update-slice.1
  235.8 0.2 dynamic-update-slice.2
  236.0 0.2 dynamic-update-slice.3
  236.2 0.2 dynamic-update-slice.4
  236.4 0.2 dynamic-update-slice.5
  236.6 0.2 dynamic-update-slice.6
  236.8 0.3 dynamic-update-slice.7
  237.1 0.3 dynamic-update-slice.8
  237.4 40.1 %all-reduce.11.cloned.1.call-done = (bf16[768,1536]{1,0:T(8,128)(2,1)}, bf16[1536,768]{1,0:T(8,128)(2,1)}) async-done(((bf16[768,1536]{1,0:T(8,128)(2,1)}, bf16[1536,768]{1,0:T(8,128)(2,1)}), (bf16[768,1536]{1,0:T(8,128)(2,1)}, bf16[1536,768]{1,0:T(8,128)(2,1)})) %all-reduce.11.cloned.1.call-update) | async-done | bytes 4718608 | tf_op jit(solution)/shard_map/psum | solution.py:586
  277.6 1.6 copy-done.2
  279.2 2.8 convert_element_type.55
  282.1 2.5 convert_element_type.56
  284.6 60.6 %psum.39 = bf16[16,768]{1,0:T(8,128)(2,1)S(1)} all-reduce(bf16[16,768]{1,0:T(8,128)(2,1)S(1)} %convert_element_type.52), channel_id=1, replica_groups=mesh['dp'=16,'mp'=2] {'dp'}, use_global_device_ids=true, to_apply=%region_8.9 | all-reduce | flops 12288 | bytes 49152 | tf_op jit(solution)/shard_map/psum | solution.py:602
  345.2 35.0 %all-reduce.9.cloned.1.call-done = (bf16[1152,768]{1,0:T(8,128)(2,1)}, bf16[384,768]{1,0:T(8,128)(2,1)}) async-done(((bf16[1152,768]{1,0:T(8,128)(2,1)}, bf16[384,768]{1,0:T(8,128)(2,1)}), (bf16[1152,768]{1,0:T(8,128)(2,1)}, bf16[384,768]{1,0:T(8,128)(2,1)})) %all-reduce.9.cloned.1.call-update) | async-done | bytes 2359312 | tf_op jit(solution)/shard_map/psum | solution.py:602
  380.3 0.5 slice.106
  380.9 4.1 %copy.60 = f32[3,384,768]{1,2,0:T(8,128)} copy(bf16[3,384,768]{2,1,0:T(8,128)(2,1)} %bitcast.25) | data formatting | bytes 5308416 | tf_op jit(solution)/shard_map/transpose | solution.py:605
  385.0 1.1 convert_element_type.54
  386.1 0.7 copy.61
  386.8 0.7 slice_reduce_fusion
  387.4 0.6 reshape.186
  388.0 0.6 slice.115
  388.6 0.9 copy.78
  389.5 0.9 copy.79
  (65 shorter events, 1.4 us)
Async XLA Ops:
  7.2 6.4 %copy-start = (f32[169,12]{0,1:T(8,128)S(1)}, f32[169,12]{0,1:T(8,128)}, u32[]{:S(2)}) copy-start(f32[169,12]{0,1:T(8,128)} %param.26) | copy-start | bytes 24340
  7.2 9.7 %copy-start.17 = (f32[2,384]{1,0:T(2,128)S(1)}, f32[2,384]{1,0:T(2,128)}, u32[]{:S(2)}) copy-start(f32[2,384]{1,0:T(2,128)} %param.25) | copy-start | bytes 9220
  7.2 27.9 %all-gather.6.cloned.1.call-start = ((), (), s32[]{:S(2)}) async-start(), calls=%async_computation.1 | async-start | bytes 1769472 | tf_op jit(solution)/shard_map/all_gather | solution.py:574
  7.9 11.2 %copy-start.3 = (bf16[768,3,384]{2,0,1:T(8,128)(2,1)S(1)}, bf16[768,3,384]{2,0,1:T(8,128)(2,1)}, u32[]{:S(2)}) copy-start(bf16[768,3,384]{2,0,1:T(8,128)(2,1)} %param.24) | copy-start | bytes 5308420
  8.0 55.9 %all-gather.4.cloned.1.call-start = ((), (), s32[]{:S(2)}) async-start(), calls=%async_computation | async-start | bytes 2359296 | tf_op jit(solution)/shard_map/all_gather | solution.py:573
  8.7 103.5 %all-gather.8.cloned.1.call-start = ((), (), s32[]{:S(2)}) async-start(), calls=%async_computation.2 | async-start | bytes 2359296 | tf_op jit(solution)/shard_map/all_gather | solution.py:576
  9.4 268.1 %all-reduce.11.cloned.1.call-start = ((), (), s32[]{:S(2)}) async-start(), calls=%async_computation.4 | async-start | bytes 9437184 | tf_op jit(solution)/shard_map/psum | solution.py:586
  16.5 4.9 %copy-start.11 = (f32[768]{0:T(1024)S(1)}, f32[768]{0:T(1024)}, u32[]{:S(2)}) copy-start(f32[768]{0:T(1024)} %param.22) | copy-start | bytes 9220
  16.5 5.5 %copy-start.12 = (f32[768]{0:T(1024)S(1)}, f32[768]{0:T(1024)}, u32[]{:S(2)}) copy-start(f32[768]{0:T(1024)} %param.23) | copy-start | bytes 9220
  16.5 6.1 %copy-start.9 = (f32[1536]{0:T(1024)S(1)}, f32[1536]{0:T(1024)}, u32[]{:S(2)}) copy-start(f32[1536]{0:T(1024)} %param.32) | copy-start | bytes 18436
  16.5 6.7 %copy-start.13 = (f32[768]{0:T(1024)S(1)}, f32[768]{0:T(1024)}, u32[]{:S(2)}) copy-start(f32[768]{0:T(1024)} %param.28) | copy-start | bytes 9220
  16.5 7.2 %copy-start.14 = (f32[768]{0:T(1024)S(1)}, f32[768]{0:T(1024)}, u32[]{:S(2)}) copy-start(f32[768]{0:T(1024)} %param.29) | copy-start | bytes 9220
  16.5 7.8 %copy-start.15 = (f32[768]{0:T(1024)S(1)}, f32[768]{0:T(1024)}, u32[]{:S(2)}) copy-start(f32[768]{0:T(1024)} %param.30) | copy-start | bytes 9220
  16.5 8.4 %copy-start.16 = (f32[768]{0:T(1024)S(1)}, f32[768]{0:T(1024)}, u32[]{:S(2)}) copy-start(f32[768]{0:T(1024)} %param.34) | copy-start | bytes 9220
  160.5 219.8 %all-reduce.9.cloned.1.call-start = ((), (), s32[]{:S(2)}) async-start(), calls=%async_computation.3 | async-start | bytes 4718592 | tf_op jit(solution)/shard_map/psum | solution.py:602
  195.4 37.3 %copy-start.8 = (f32[8,768]{1,0:T(8,128)S(1)}, f32[8,768]{1,0:T(8,128)}, u32[]{:S(2)}) copy-start(f32[8,768]{1,0:T(8,128)} %get-tuple-element.71) | copy-start | bytes 73732
  195.4 38.1 %copy-start.7 = (f32[768,64]{1,0:T(8,128)S(1)}, f32[768,64]{1,0:T(8,128)}, u32[]{:S(2)}) copy-start(f32[768,64]{1,0:T(8,128)} %get-tuple-element.74) | copy-start | bytes 589828
  195.4 41.4 %copy-start.10 = (f32[1,1536]{1,0:T(1,128)S(1)}, f32[1,1536]{1,0:T(1,128)}, u32[]{:S(2)}) copy-start(f32[1,1536]{1,0:T(1,128)} %get-tuple-element.73) | copy-start | bytes 18436
  277.6 1.7 copy-start.2
  279.2 2.8 copy-start.1
  380.9 4.1 %copy-start.6 = (bf16[384,768]{1,0:T(8,128)(2,1)S(1)}, bf16[384,768]{1,0:T(8,128)(2,1)}, u32[]{:S(2)}) copy-start(bf16[384,768]{1,0:T(8,128)(2,1)} %get-tuple-element.80) | copy-start | bytes 1769476
  385.0 3.6 copy-start.4
  385.0 4.5 %copy-start.5 = (bf16[1024,384]{1,0:T(8,128)(2,1)S(1)}, bf16[1024,384]{1,0:T(8,128)(2,1)}, u32[]{:S(2)}) copy-start(bf16[1024,384]{1,0:T(8,128)(2,1)} %get-tuple-element.154) | copy-start | bytes 2359300
Sparse Core Ops, SparseCore 0:
  9.6 25.5 all-gather.5
  36.6 27.1 all-gather.3
  65.4 41.4 all-gather.7
  160.6 116.8 all-reduce.10
  281.0 99.2 all-reduce.8

commit v3 on v2

--- a/solution.py
+++ b/solution.py
@@ -22,6 +22,7 @@
 EPS = 1e-05
 NEG = -1e30
 CHUNK = 256
+SMALL = 16
 MESH = pl.DeviceIdType.MESH
 F32 = jnp.float32
 BF16 = jnp.bfloat16
@@ -114,18 +115,20 @@
 
 
 def attn_fwd_kernel(
-    groups, tok, gain, shift, wt, qb_col, vb_col, vb_row, khot, qhott, table, kwin, qwin,
-    a_out, qt, kx, kt, vx, o_out, peer_out, lse, a_pad, vt, o_all, o_peer, send_sem, recv_sem,
+    groups, w_own, tok, gain, shift, wt, qb_col, vb_col, vb_row, khot, qhott, table, kwin, qwin,
+    a_out, qt, kx, kt, vx, o_out, peer_out, w_out, lse, a_pad, vt, o_all, o_peer, w_got, send_sem, recv_sem,
 ):
     step = pl.program_id(0)
     last = tok.shape[0] // QB - 1
     rows_all = tok.shape[0]
     width = qt.shape[0]
     sems = (send_sem, recv_sem)
+    weight = to_peer(w_own, w_got, send_sem.at[last + 1], recv_sem.at[last + 1])
 
     @pl.when(step == 0)
     def _():
         greet()
+        weight.start()
         zero = jnp.zeros((HALO, tok.shape[1]), BF16)
         a_pad[:HALO, :] = zero
         a_pad[HALO + rows_all :, :] = zero
@@ -184,6 +187,8 @@
             return carry
 
         lax.fori_loop(0, last + 1, finish, 0)
+        weight.wait()
+        w_out[...] = w_got[...]
         peer_out[...] = o_peer[...]
 
 
@@ -203,7 +208,7 @@
     return [pltpu.SemaphoreType.DMA((n,)), pltpu.SemaphoreType.DMA((n,))]
 
 
-def attn_fwd(tok, gain, shift, wt, qb_col, vb_col, vb_row, khot, qhott, table, kwin, qwin):
+def attn_fwd(w_own, tok, gain, shift, wt, qb_col, vb_col, vb_row, khot, qhott, table, kwin, qwin):
     rows, model = tok.shape
     width = wt.shape[0] // 3
     heads = width // HEAD_DIM
@@ -212,24 +217,26 @@
     return pl.pallas_call(
         partial(attn_fwd_kernel, heads // GROUP),
         grid=(rows // QB,),
-        in_specs=[whole(x) for x in (tok, gain, shift, wt, qb_col, vb_col, vb_row, khot)]
+        in_specs=[pl.BlockSpec(memory_space=pltpu.VMEM)]
+        + [whole(x) for x in (tok, gain, shift, wt, qb_col, vb_col, vb_row, khot)]
         + [cols(CP), whole(table), whole(kwin), cols(1)],
         out_specs=[
             same(rows, model), same(width, rows), same(ext, width), same(width, ext), same(ext, width),
-            same(rows, width), same(rows, width), cols(heads),
+            same(rows, width), same(rows, width), same(width, model), cols(heads),
         ],
         out_shape=[
             shape((rows, model), BF16), shape((width, rows), BF16), shape((ext, width), BF16),
             shape((width, ext), BF16), shape((ext, width), BF16), shape((rows, width), BF16),
-            shape((rows, width), BF16), shape((heads, rows), F32),
+            shape((rows, width), BF16), shape((width, model), BF16), shape((heads, rows), F32),
         ],
         scratch_shapes=[
             pltpu.VMEM((ext, model), BF16), pltpu.VMEM((width, ext), BF16),
             pltpu.VMEM((rows, width), BF16), pltpu.VMEM((rows, width), BF16),
-        ] + two_sems(rows // QB),
+            pltpu.VMEM((width, model), BF16),
+        ] + two_sems(rows // QB + 1),
         compiler_params=pltpu.CompilerParams(collective_id=0, has_side_effects=True),
         name="attn_fwd",
-    )(tok, gain, shift, wt, qb_col, vb_col, vb_row, khot, qhott, table, kwin, qwin)
+    )(w_own, tok, gain, shift, wt, qb_col, vb_col, vb_row, khot, qhott, table, kwin, qwin)
 
 
 def ffn_kernel(
@@ -429,8 +436,8 @@
 
 
 def close_kernel(
-    tok, a, dq, dk, dv, wt, gain, gr, out, g_wt, vec, vec_qv,
-    ga_s, give, got, stat, stat_p, r_s, wide, vec_s, vec_p, send_sem, recv_sem,
+    tok, a, dq, dk, dv, wt, gain, gr, vec2, vec_in, table, out, late,
+    ga_s, give, got, stat, stat_p, wide, vec_s, vec_p, send_sem, recv_sem,
 ):
     rows_all, model = tok.shape
     width = dq.shape[1]
@@ -472,10 +479,9 @@
     lax.fori_loop(0, chunks, forward, 0)
     vectors = to_peer(vec_s, vec_p, send_sem.at[2, 0], recv_sem.at[2, 0])
     for k, item in enumerate((dq, dk, dv)):
-        g_wt[width * k : width * (k + 1), :] = dot_tn(item[...], a[...]).astype(BF16)
+        late[width * k : width * (k + 1), :] = dot_tn(item[...], a[...]).astype(BF16)
     vectors.start()
-    vec_qv[0:1, :] = jnp.sum(dq[...].astype(F32), axis=0, keepdims=True)
-    vec_qv[1:2, :] = jnp.sum(dv[...].astype(F32), axis=0, keepdims=True)
+    qv = [jnp.sum(item[...].astype(F32), axis=0, keepdims=True) for item in (dq, dv)]
 
     def backward(c, carry):
         at = pl.ds(pl.multiple_of(c * CHUNK, CHUNK), CHUNK)
@@ -491,10 +497,18 @@
 
     lax.fori_loop(0, chunks, backward, 0)
     vectors.wait()
-    vec[...] = vec_s[...] + vec_p[...]
-
-
-def close(tok, a, dq, dk, dv, wt, gain, gr):
+    first = vec_s[0:2, :] + vec_p[0:2, :]
+    parts = [first[0:1], first[1:2]] + [vec2[k : k + 1, :] for k in range(4)]
+    parts.append(jnp.concatenate(qv, axis=1))
+    parts += [vec_in[:, model * k : model * (k + 1)] for k in range(vec_in.shape[1] // model)]
+    parts += [table[k : k + 1, :] for k in range(table.shape[0])]
+    parts.append(jnp.zeros((SMALL - len(parts), model), F32))
+    late[3 * width : 3 * width + SMALL, :] = jnp.concatenate(parts, axis=0).astype(BF16)
+    spare = late.shape[0] - 3 * width - SMALL
+    late[3 * width + SMALL :, :] = jnp.zeros((spare, model), BF16)
+
+
+def close(late_rows, tok, a, dq, dk, dv, wt, gain, gr, vec2, vec_in, table):
     rows, model = tok.shape
     width = dq.shape[1]
     half = gr.shape[1]
@@ -504,20 +518,109 @@
     sems = pltpu.SemaphoreType.DMA((3, chunks))
     return pl.pallas_call(
         close_kernel,
-        in_specs=[pl.BlockSpec(memory_space=pltpu.VMEM)] * 8,
-        out_specs=[pl.BlockSpec(memory_space=pltpu.VMEM)] * 4,
-        out_shape=[
-            shape((rows, half), BF16), shape((3 * width, model), BF16), shape((8, model), F32),
-            shape((8, width), F32),
-        ],
+        in_specs=[pl.BlockSpec(memory_space=pltpu.VMEM)] * 11,
+        out_specs=[pl.BlockSpec(memory_space=pltpu.VMEM)] * 2,
+        out_shape=[shape((rows, half), BF16), shape((late_rows, model), BF16)],
         scratch_shapes=[
             vm((rows, half), F32), vm((rows, half), BF16), vm((rows, half), BF16), vm((rows, 128), F32),
-            vm((rows, 128), F32), vm((rows, 1), F32), vm((CHUNK, model), F32), vm((8, model), F32),
-            vm((8, model), F32), sems, sems,
+            vm((rows, 128), F32), vm((CHUNK, model), F32), vm((8, model), F32), vm((8, model), F32),
+            sems, sems,
         ],
         compiler_params=pltpu.CompilerParams(collective_id=3, has_side_effects=True),
         name="close",
-    )(tok, a, dq, dk, dv, wt, gain, gr)
+    )(tok, a, dq, dk, dv, wt, gain, gr, vec2, vec_in, table)
+
+
+def dp_copy(src, dst, partner, send_sem, recv_sem):
+    return pltpu.make_async_remote_copy(
+        src_ref=src,
+        dst_ref=dst,
+        send_sem=send_sem,
+        recv_sem=recv_sem,
+        device_id={"dp": partner},
+        device_id_type=MESH,
+    )
+
+
+def dp_sum_kernel(orders, x, out, acc, got, send_sem, recv_sem):
+    rows, wide = x.shape
+    part = wide // len(orders)
+    steps = len(orders[0])
+    place = lax.axis_index("dp")
+
+    def bit_of(b):
+        return lax.rem(lax.div(place, 1 << b), 2)
+
+    def partner_of(b):
+        return place + (1 - 2 * bit_of(b)) * (1 << b)
+
+    barrier = pltpu.get_barrier_semaphore()
+    for b in range(steps):
+        pl.semaphore_signal(barrier, inc=1, device_id={"dp": partner_of(b)}, device_id_type=MESH)
+    pl.semaphore_wait(barrier, steps)
+
+    state = [(x, 0)] * len(orders)
+    kept = [[] for _ in orders]
+    for s in range(steps):
+        size = rows >> (s + 1)
+        base = rows - (rows >> s)
+        copies = []
+        for k, order in enumerate(orders):
+            src, low = state[k]
+            lanes = pl.ds(part * k, part)
+            bit = bit_of(order[s])
+            mine = pl.multiple_of(low + bit * size, 16)
+            theirs = pl.multiple_of(low + (1 - bit) * size, 16)
+            copy = dp_copy(
+                src.at[pl.ds(theirs, size), lanes],
+                got.at[pl.ds(base, size), lanes],
+                partner_of(order[s]),
+                send_sem.at[k, s],
+                recv_sem.at[k, s],
+            )
+            copy.start()
+            copies.append(copy)
+            kept[k].append(low)
+            state[k] = (src, mine)
+        for k, order in enumerate(orders):
+            src, mine = state[k]
+            lanes = slice(part * k, part * (k + 1))
+            copies[k].wait()
+            total = src[pl.ds(mine, size), lanes].astype(F32) + got[base : base + size, lanes].astype(F32)
+            goal = out if s == steps - 1 else acc
+            goal[pl.ds(mine, size), lanes] = total.astype(BF16)
+            state[k] = (goal, mine)
+    for s in reversed(range(steps)):
+        size = rows >> (s + 1)
+        copies = []
+        for k, order in enumerate(orders):
+            low = state[k][1]
+            lanes = pl.ds(part * k, part)
+            region = out.at[pl.ds(pl.multiple_of(low, 16), size), lanes]
+            at = 2 * steps - 1 - s
+            copy = dp_copy(region, region, partner_of(order[s]), send_sem.at[k, at], recv_sem.at[k, at])
+            copy.start()
+            copies.append(copy)
+            state[k] = (out, kept[k][s])
+        for copy in copies:
+            copy.wait()
+
+
+def dp_sum(ranks, x):
+    rows, wide = x.shape
+    steps = ranks.bit_length() - 1
+    orders = [list(range(steps)), [0] + list(range(2, steps)) + [1]]
+    vm = pltpu.VMEM
+    sems = pltpu.SemaphoreType.DMA((2, 2 * steps))
+    return pl.pallas_call(
+        partial(dp_sum_kernel, orders),
+        in_specs=[pl.BlockSpec(memory_space=pltpu.VMEM)],
+        out_specs=pl.BlockSpec(memory_space=pltpu.VMEM),
+        out_shape=jax.ShapeDtypeStruct((rows, wide), BF16),
+        scratch_shapes=[vm((rows, wide), BF16), vm((rows, wide), BF16), sems, sems],
+        compiler_params=pltpu.CompilerParams(collective_id=4, has_side_effects=True),
+        name="dp_sum",
+    )(x)
 
 
 def window_data(crop_counts, crop_patches, rel_index, rel_table, rows):
@@ -569,13 +672,11 @@
     khot, khott, qhott, qhot, table, kwin, qwin, offset_hot = window_data(
         crop_counts, crop_patches, rel_index, rel_table, rows
     )
-    me = lax.axis_index("mp")
     whole_in = lax.all_gather(tokens, "mp", axis=1, tiled=True)
-    w_out_all = lax.all_gather(w_out, "mp", axis=0, tiled=True)
-    w_peer = lax.dynamic_slice_in_dim(w_out_all, (1 - me) * width, width, 0)
     whole_cot = lax.all_gather(cotangent, "mp", axis=1, tiled=True)
     wt = jnp.transpose(w_qkv, (1, 2, 0)).reshape(3 * width, model)
-    mixer_in, qt, kx, kt, vx, heads_out, heads_peer, lse = attn_fwd(
+    mixer_in, qt, kx, kt, vx, heads_out, heads_peer, w_peer, lse = attn_fwd(
+        w_out,
         whole_in, ln1_gain[None, :], ln1_shift[None, :], wt, qv_bias[0][:, None], qv_bias[1][:, None],
         qv_bias[1][None, :], khot, qhott, table, kwin, qwin,
     )
@@ -583,36 +684,33 @@
         whole_in, heads_out, heads_peer, w_out, w_peer, b_out[None, :], ln2_gain[None, :], ln2_shift[None, :],
         w_in, b_in[None, :], w_back, b_back[None, :], whole_cot,
     )
-    early = lax.psum((grad_w_in, grad_w_back), "dp")
+    early = lax.psum((grad_w_in, grad_w_back, grad_w_out), "dp")
     out_half, grad_query, grad_key, grad_value, gcell = attn_bwd(
         keep, give, qt, kx, kt, vx, dot_t, khot, khott, qhott, qhot, table, kwin, qwin, lse
     )
     grad_table = jnp.einsum(
         "pm,hp->mh", offset_hot, gcell.reshape(heads, CP * CP), precision=highest
     )
-    grad_half, grad_wt, vec1, vec_qv = close(
-        whole_in, mixer_in, grad_query, grad_key, grad_value, wt, ln1_gain[None, :], gr
-    )
-    small = [vec1[0], vec1[1], vec2[2], vec2[0], vec2[1], vec2[3], vec_qv[:2], grad_b_in[0], grad_table]
-    sizes = [item.shape for item in small]
-    packed = jnp.concatenate([item.reshape(-1) for item in small])
-    pad_rows = -(-packed.size // (16 * model)) * 16
-    packed = jnp.pad(packed, (0, pad_rows * model - packed.size)).reshape(pad_rows, model).astype(BF16)
-    early, late = lax.optimization_barrier((early, (grad_wt, grad_w_out, packed)))
-    late = lax.optimization_barrier(lax.psum(late, "dp"))
-    grad_w_in, grad_w_back = (item.astype(F32) for item in early)
-    grad_wt, grad_w_out, packed = (item.astype(F32) for item in late)
-    grad_w_qkv = jnp.transpose(grad_wt.reshape(3, width, model), (2, 0, 1))
-    packed = packed.reshape(-1)
-    at = 0
-    outs = []
-    for shape in sizes:
-        size = 1
-        for extent in shape:
-            size *= extent
-        outs.append(packed[at : at + size].reshape(shape))
-        at += size
-    grad_g1, grad_c1, grad_b_out, grad_g2, grad_c2, grad_b_back, grad_qv_bias, grad_b_in, grad_table = outs
+    table_rows = -(-grad_table.size // model)
+    table_flat = jnp.pad(grad_table.reshape(-1), (0, table_rows * model - grad_table.size))
+    ranks = lax.axis_size("dp")
+    late_rows = -(-(3 * width + SMALL) // (16 * ranks)) * 16 * ranks
+    grad_half, late = close(
+        late_rows, whole_in, mixer_in, grad_query, grad_key, grad_value, wt, ln1_gain[None, :], gr,
+        vec2, grad_b_in, table_flat.reshape(table_rows, model),
+    )
+    late = dp_sum(ranks, late)
+    early, late = lax.optimization_barrier((early, late))
+    grad_w_in, grad_w_back, grad_w_out = (item.astype(F32) for item in early)
+    late = late[: 3 * width + SMALL].astype(F32)
+    grad_w_qkv = jnp.transpose(late[: 3 * width].reshape(3, width, model), (2, 0, 1))
+    small = late[3 * width :]
+    grad_g1, grad_c1, grad_g2, grad_c2, grad_b_out, grad_b_back = (small[k] for k in range(6))
+    grad_qv_bias = small[6].reshape(2, width)
+    hidden_rows = w_in.shape[1] // model
+    grad_b_in = small[7 : 7 + hidden_rows].reshape(-1)
+    flat = small[7 + hidden_rows : 7 + hidden_rows + table_rows].reshape(-1)
+    grad_table = flat[: grad_table.size].reshape(grad_table.shape)
     return (
         out_half,
         grad_half,

time: 397 us -> 309 us (0.78)
  waiting for transfers between devices: 110 us -> 17.7 us
  Pallas kernels: 166 us -> 235 us
  blocking collectives: 60.6 us -> 0 us
  local copies, waits for them, and re-layouts: 27.5 us -> 21 us
    psum x2 -> x1, waiting for transfers between devices: 75.1 us -> 4.49 us  [body(): early = lax.psum((grad_w_in, grad_w_back, grad_w_out), 'dp')]
    pallas_call x0 -> x1, Pallas kernels: none -> 64 us  [dp_sum(): pl.pallas_call(partial(dp_sum_kernel, orders), in_specs=[pl.BlockSpec(mem...]
    psum x1 -> x0, blocking collectives: 60.6 us -> none  [body(): late = lax.optimization_barrier(lax.psum(late, 'dp'))]
    all_gather x1, waiting for transfers between devices: 26.8 us -> 11.8 us  [body(): whole_in = lax.all_gather(tokens, 'mp', axis=1, tiled=True)]
    pallas_call x1, Pallas kernels: 48.3 us -> 54.5 us  [attn_fwd(): pl.pallas_call(partial(attn_fwd_kernel, heads // GROUP), grid=(rows // QB...]
    all_gather x1 -> x0, waiting for transfers between devices: 5.95 us -> none  [body(): w_out_all = lax.all_gather(w_out, 'mp', axis=0, tiled=True)]
    unnamed x48 -> x38, local copies, waits for them, and re-layouts: 6.79 us -> 2.63 us
    transpose x1 -> x0, local copies, waits for them, and re-layouts: 4.09 us -> none  [body(): grad_w_qkv = jnp.transpose(grad_wt.reshape(3, width, model), (2, 0, 1))]
  transfers between devices with their start and end apart: 5 -> 3, of which waited for: 4 -> 2; matrix products, arithmetic and copies ran while one was open for 8% -> 7% of each run, Pallas kernels for 30% -> 61%
where the time goes in v3:
time: 309 us
  Pallas kernels  235 us (76%)
  local copies, waits for them, and re-layouts  21 us (7%)
  other arithmetic  17.8 us (6%)
  waiting for transfers between devices  17.7 us (6%)
  between operations  14.7 us (5%)
    pallas_call x1, Pallas kernels, dp_sum(): pl.pallas_call(partial(dp_sum_kernel, orders), in_specs=[pl.BlockSpec(mem...  64 us
    pallas_call x1, Pallas kernels, attn_fwd(): pl.pallas_call(partial(attn_fwd_kernel, heads // GROUP), grid=(rows // QB...  54.5 us
    pallas_call x1, Pallas kernels, ffn(): pl.pallas_call(ffn_kernel, in_specs=[pl.BlockSpec(memory_space=pltpu.VMEM...  47.4 us
    pallas_call x1, Pallas kernels, close(): pl.pallas_call(close_kernel, in_specs=[pl.BlockSpec(memory_space=pltpu.VM...  35.7 us
    pallas_call x1, Pallas kernels, attn_bwd(): pl.pallas_call(partial(attn_bwd_kernel, heads // GROUP), grid=(rows // QB...  33.5 us
    all_gather x1, waiting for transfers between devices, body(): whole_in = lax.all_gather(tokens, 'mp', axis=1, tiled=True)  11.8 us
    convert_element_type x3, other arithmetic, body(): grad_w_in, grad_w_back, grad_w_out = (item.astype(F32) for item in early)  8.28 us
  transfers between devices with their start and end apart: 3, of which 2 were waited for; matrix products, arithmetic and copies ran while one was open for 7% of the time, Pallas kernels for 61%

profile of v3, /device:TPU:0, one launch (start us, length us, event | category | flops | bytes accessed | tf_op | source)
XLA Modules:
  0.0 308.8 jit_solution(9718539853014138900)
XLA Ops:
  7.2 0.0 all-gather.3.cloned.1.call-start
  7.3 0.7 all-gather.3.cloned.1.call-update
  8.0 0.0 all-gather.5.cloned.1.call-start
  8.0 0.7 all-gather.5.cloned.1.call-update
  8.7 0.0 all-reduce.7.cloned.1.call-start
  8.8 0.8 fusion.13
  9.5 0.1 reshape.173
  9.6 0.1 reduce-window.4
  9.7 0.5 slice.76
  10.2 0.1 reduce
  11.0 0.2 convert_reduce_fusion
  11.1 0.8 fusion.10
  11.9 0.1 pad.15
  12.0 0.7 subtract_select_fusion
  12.6 0.1 pad.17
  12.7 1.0 broadcast_in_dim.90.kwin
  13.7 0.1 copy.64
  13.8 0.1 eq.88
  13.9 1.1 subtract_convert_fusion
  15.1 0.2 stack_reshape.6
  15.3 0.2 stack_reshape.7
  15.5 0.6 fusion.16
  16.0 0.8 copy.56.qb_col
  16.9 0.8 copy.57.vb_col
  17.7 2.2 copy.51
  19.9 0.6 broadcast_in_dim.77.gain
  20.5 0.6 broadcast_in_dim.78.shift
  21.1 0.6 broadcast_in_dim.88.b_in
  21.7 0.6 broadcast_in_dim.85.bo
  22.3 0.6 broadcast_in_dim.86.gain
  22.9 0.6 broadcast_in_dim.87.shift
  23.4 0.6 broadcast_in_dim.89.bb
  24.0 0.8 pad_maximum_fusion
  24.9 1.2 compare_select_fusion.qwin
  26.1 0.7 fusion.6.qhott
  26.8 0.9 compare_convert_fusion.khot
  27.7 11.8 %all-gather.3.cloned.1.call-done.tok = bf16[1024,768]{1,0:T(8,128)(2,1)} async-done(((bf16[1024,384]{1,0:T(8,128)(2,1)}), bf16[1024,768]{1,0:T(8,128)(2,1)}) %all-gather.3.cloned.1.call-update) | async-done | bytes 1572880 | tf_op jit(solution)/shard_map/all_gather | solution.py:675
  39.5 54.5 %attn_fwd.1 = (bf16[1024,768]{1,0:T(8,128)(2,1)}, bf16[384,1024]{1,0:T(8,128)(2,1)}, bf16[1152,384]{1,0:T(8,128)(2,1)}, bf16[384,1152]{1,0:T(8,128)(2,1)}, bf16[...) custom-call(bf16[384,768]{1,0:T(8,128)(2,1)} %w_own.3, ...), custom_call_target="tpu_custom_call" | custom-call | tf_op jit(solution)/shard_map/attn_fwd/pallas_call | solution.py:217
  94.0 0.0 all-gather.5.cloned.1.call-done.cot
  94.0 47.4 %ffn.1 = (f32[1024,384]{1,0:T(8,128)}, bf16[1024,384]{1,0:T(8,128)(2,1)}, f32[1024,384]{1,0:T(8,128)}, bf16[384,1024]{1,0:T(8,128)(2,1)}, bf16[384,768]{1,0:T(8,...) custom-call(bf16[1024,768]{1,0:T(8,128)(2,1)} %all-gather.3.cloned.1.ca, ...), custom_call_target="tpu_custom_call" | custom-call | tf_op jit(solution)/shard_map/ffn/pallas_call | solution.py:333
  141.4 0.9 fusion.4.qhot
  142.3 0.7 fusion.5.khott
  143.0 33.5 %attn_bwd.1 = (bf16[1024,384]{1,0:T(8,128)(2,1)}, bf16[1024,384]{1,0:T(8,128)(2,1)}, bf16[1024,384]{1,0:T(8,128)(2,1)}, bf16[1024,384]{1,0:T(8,128)(2,1)}, f32[768,64]{1,0:T(8,128)}) custom-call(f32[1024,384]{1,0:T(8,128)} %get-tuple-element.47.keep, bf16[1024,384]{1,0:T(8,128)(2,1)} %get-tuple-element.48.give, bf16[384,1024]{1,0:T(8,128)(2,1)} %get-tuple-element.49.qt, ...), custom_call_target="tpu_custom_call" | custom-call | tf_op jit(solution)/shard_map/attn_bwd/pallas_call | solution.py:415
  176.5 1.1 reshape.168
  177.7 1.4 fusion.1
  179.1 0.1 reshape.169
  179.2 0.6 reshape.170.table
  179.8 35.7 %close.1 = (bf16[1024,384]{1,0:T(8,128)(2,1)}, bf16[1280,768]{1,0:T(8,128)(2,1)}) custom-call(bf16[1024,768]{1,0:T(8,128)(2,1)} %all-gather.3.cloned.1.call-done.tok, bf16[1024,768]{1,0:T(8,128)(2,1)} %get-tuple-element.56.a, bf16[1024,384]{1,0:T(8,128)(2,1)} %get-tuple-element.57.dq, bf16[1024,384]{1,0:T(8,128)(2,1)} %get-tuple-element.58.dk, ...), custom_call_target="tpu_custom_call" | custom-call | tf_op jit(solution)/shard_map/close/pallas_call | solution.py:519
  215.5 64.0 %dp_sum.1 = bf16[1280,768]{1,0:T(8,128)(2,1)} custom-call(bf16[1280,768]{1,0:T(8,128)(2,1)} %get-tuple-element.68.x), custom_call_target="tpu_custom_call" | custom-call | tf_op jit(solution)/shard_map/dp_sum/pallas_call | solution.py:615
  279.5 4.5 %all-reduce.7.cloned.1.call-done = (bf16[768,1536]{1,0:T(8,128)(2,1)}, bf16[1536,768]{1,0:T(8,128)(2,1)}, bf16[384,768]{1,0:T(8,128)(2,1)}) async-done(((bf16[768,1536]{1,0:T(8,128)(2,1)}, bf16[1536,768]{1,0:T(8,128)(2,1)}, bf16[384,768]{1,0:T(8,128)(2,1)}), (bf16[768,1536]{1,0:T(8,128)(2,1)}, bf16[1536,768]{1,0:T(8,128)(2,1)}, bf16[384,768]{1,0:T(8,128)(2,1)})) %all-reduce.7.cloned.1.call-update) | async-done | bytes 5308432 | tf_op jit(solution)/shard_map/psum | solution.py:687
  284.0 1.7 slice_convert_fusion
  285.8 0.2 slice.79
  286.0 0.7 slice_reduce_fusion
  286.7 0.6 slice.86
  287.3 2.9 copy.61
  290.2 4.6 %convert_element_type.49 = f32[768,1536]{1,0:T(8,128)} convert(bf16[768,1536]{1,0:T(8,128)(2,1)} %get-tuple-element.71) | non-fusion elementwise | flops 1179648 | bytes 7077888 | tf_op jit(solution)/shard_map/convert_element_type | solution.py:704
  294.9 2.5 convert_element_type.50
  297.4 0.1 slice.69
  297.6 0.7 copy.62
  298.2 0.6 reshape_squeeze.3
  298.8 0.6 reshape.172
  299.4 1.1 convert_element_type.48
  300.5 0.9 copy.70
  301.4 0.9 copy.71
  (40 shorter events, 0.1 us)
Async XLA Ops:
  7.2 6.7 %copy-start = (f32[169,12]{0,1:T(8,128)S(1)}, f32[169,12]{0,1:T(8,128)}, u32[]{:S(2)}) copy-start(f32[169,12]{0,1:T(8,128)} %param.26) | copy-start | bytes 24340
  7.2 6.5 %copy-start.7 = (s32[49,49]{1,0:T(8,128)S(1)}, s32[49,49]{1,0:T(8,128)}, u32[]{:S(2)}) copy-start(s32[49,49]{1,0:T(8,128)} %param.21) | copy-start | bytes 28816
  7.2 8.2 %copy-start.16 = (f32[2,384]{1,0:T(2,128)S(1)}, f32[2,384]{1,0:T(2,128)}, u32[]{:S(2)}) copy-start(f32[2,384]{1,0:T(2,128)} %param.25) | copy-start | bytes 9220
  7.2 10.5 %copy-start.3 = (bf16[768,3,384]{2,0,1:T(8,128)(2,1)S(1)}, bf16[768,3,384]{2,0,1:T(8,128)(2,1)}, u32[]{:S(2)}) copy-start(bf16[768,3,384]{2,0,1:T(8,128)(2,1)} %param.24) | copy-start | bytes 5308420
  7.2 32.3 %all-gather.3.cloned.1.call-start = ((), (), s32[]{:S(2)}) async-start(), calls=%async_computation | async-start | bytes 2359296 | tf_op jit(solution)/shard_map/all_gather | solution.py:675
  8.0 86.1 %all-gather.5.cloned.1.call-start = ((), (), s32[]{:S(2)}) async-start(), calls=%async_computation.1 | async-start | bytes 2359296 | tf_op jit(solution)/shard_map/all_gather | solution.py:676
  8.7 275.3 %all-reduce.7.cloned.1.call-start = ((), (), s32[]{:S(2)}) async-start(), calls=%async_computation.2 | async-start | bytes 10616832 | tf_op jit(solution)/shard_map/psum | solution.py:687
  15.0 4.9 %copy-start.10 = (f32[768]{0:T(1024)S(1)}, f32[768]{0:T(1024)}, u32[]{:S(2)}) copy-start(f32[768]{0:T(1024)} %param.22) | copy-start | bytes 9220
  15.0 5.5 %copy-start.11 = (f32[768]{0:T(1024)S(1)}, f32[768]{0:T(1024)}, u32[]{:S(2)}) copy-start(f32[768]{0:T(1024)} %param.23) | copy-start | bytes 9220
  15.0 6.1 %copy-start.9 = (f32[1536]{0:T(1024)S(1)}, f32[1536]{0:T(1024)}, u32[]{:S(2)}) copy-start(f32[1536]{0:T(1024)} %param.32) | copy-start | bytes 18436
  15.0 6.7 %copy-start.12 = (f32[768]{0:T(1024)S(1)}, f32[768]{0:T(1024)}, u32[]{:S(2)}) copy-start(f32[768]{0:T(1024)} %param.28) | copy-start | bytes 9220
  15.0 7.3 %copy-start.13 = (f32[768]{0:T(1024)S(1)}, f32[768]{0:T(1024)}, u32[]{:S(2)}) copy-start(f32[768]{0:T(1024)} %param.29) | copy-start | bytes 9220
  15.0 7.8 %copy-start.14 = (f32[768]{0:T(1024)S(1)}, f32[768]{0:T(1024)}, u32[]{:S(2)}) copy-start(f32[768]{0:T(1024)} %param.30) | copy-start | bytes 9220
  15.0 8.4 %copy-start.15 = (f32[768]{0:T(1024)S(1)}, f32[768]{0:T(1024)}, u32[]{:S(2)}) copy-start(f32[768]{0:T(1024)} %param.34) | copy-start | bytes 9220
  290.2 4.7 %copy-start.2 = (bf16[1536,768]{1,0:T(8,128)(2,1)S(1)}, bf16[1536,768]{1,0:T(8,128)(2,1)}, u32[]{:S(2)}) copy-start(bf16[1536,768]{1,0:T(8,128)(2,1)} %get-tuple-element.72) | copy-start | bytes 7077892
  294.9 4.0 %copy-start.8 = (f32[2,768]{1,0:T(2,128)S(1)}, f32[2,768]{1,0:T(2,128)}, u32[]{:S(2)}) copy-start(f32[2,768]{1,0:T(2,128)} %slice.86) | copy-start | bytes 18436
  294.9 4.6 %copy-start.6 = (bf16[384,768]{1,0:T(8,128)(2,1)S(1)}, bf16[384,768]{1,0:T(8,128)(2,1)}, u32[]{:S(2)}) copy-start(bf16[384,768]{1,0:T(8,128)(2,1)} %get-tuple-element.70) | copy-start | bytes 1769476
  297.4 3.1 %copy-start.4 = (bf16[1024,384]{1,0:T(8,128)(2,1)S(1)}, bf16[1024,384]{1,0:T(8,128)(2,1)}, u32[]{:S(2)}) copy-start(bf16[1024,384]{1,0:T(8,128)(2,1)} %get-tuple-element.136) | copy-start | bytes 2359300
  297.4 4.0 %copy-start.5 = (bf16[1024,384]{1,0:T(8,128)(2,1)S(1)}, bf16[1024,384]{1,0:T(8,128)(2,1)}, u32[]{:S(2)}) copy-start(bf16[1024,384]{1,0:T(8,128)(2,1)} %get-tuple-element.137) | copy-start | bytes 2359300
  298.8 3.5 %copy-start.1 = (f32[169,12]{0,1:T(8,128)S(1)}, f32[169,12]{0,1:T(8,128)}, u32[]{:S(2)}) copy-start(f32[169,12]{0,1:T(8,128)} %param.26) | copy-start | bytes 24340
Sparse Core Ops, SparseCore 0:
  9.6 29.9 all-gather.2
  41.1 44.1 all-gather.4
  141.5 142.4 all-reduce.6

commit v4 on v3

--- a/solution.py
+++ b/solution.py
@@ -239,21 +239,20 @@
     )(w_own, tok, gain, shift, wt, qb_col, vb_col, vb_row, khot, qhott, table, kwin, qwin)
 
 
-def ffn_kernel(
-    tok, o_own, o_peer, w_own, w_peer, bo, gain, shift, w_in, b_in, w_back, bb, cot,
-    keep, give, gr, dot_t, g_out, g_in, g_back, vec, vec_in,
-    n_s, r_s, h_s, z_s, du_s, gh_s, gh_p, go_s, wide_a, wide_b, send_sem, recv_sem,
+def ffn_fwd_kernel(
+    tok, o_own, o_peer, w_own, w_peer, bo, gain, shift, w_in, b_in, w_back, bb, cot_own,
+    keep, give, n_out, r_out, h_out, slope_out, cot, g_back, z_s, cot_got, wide_a, wide_b, send_sem, recv_sem,
 ):
     rows_all, model = tok.shape
     half = keep.shape[1]
     chunks = rows_all // CHUNK
-    sems = (send_sem, recv_sem)
     me = lax.axis_index("mp")
     own = half_lanes(me, half)
     other = half_lanes(1 - me, half)
     greet()
-    vec[...] = jnp.zeros_like(vec)
-    vec_in[...] = jnp.zeros_like(vec_in)
+    swap = to_peer(cot_own, cot_got, send_sem.at[0], recv_sem.at[0])
+    swap.start()
+    cot[:, own] = cot_own[...]
 
     def forward(c, carry):
         at = pl.ds(pl.multiple_of(c * CHUNK, CHUNK), CHUNK)
@@ -264,25 +263,23 @@
         n = center * r
         h = (n * gain[...] + shift[...]).astype(BF16)
         wide_b[...] = x1
-        n_s[at, :] = n
-        r_s[at, :] = r
-        h_s[at, :] = h
+        n_out[at, :] = n.astype(BF16)
+        r_out[at, :] = r
+        h_out[at, :] = h
         u = dot(h, w_in[...]) + b_in[...]
         cdf = 0.5 * (1.0 + lax.erf(u * (0.5**0.5)))
         slope = cdf + u * (jnp.exp(-0.5 * u * u) * 0.3989422804014327)
+        slope_out[at, :] = slope.astype(BF16)
         z = (u * cdf).astype(BF16)
         z_s[at, :] = z
-        du = (dot_nt(cot[at, :], w_back[...]) * slope).astype(BF16)
-        du_s[at, :] = du
-        gh_s[at, :] = dot_nt(du, w_in[...]).astype(BF16)
-        vec_in[...] += jnp.sum(du.astype(F32), axis=0, keepdims=True)
         wide_a[...] = dot(z, w_back[...])
-        rows_copy(gh_s, gh_p, CHUNK, sems, c).start()
         keep[at, :] = wide_a[:, own] + wide_b[:, own] + bb[:, own]
         give[at, :] = wide_a[:, other].astype(BF16)
         return carry
 
     lax.fori_loop(0, chunks, forward, 0)
+    swap.wait()
+    cot[:, other] = cot_got[...]
 
     def back_block(i, carry):
         at = pl.ds(pl.multiple_of(i * CHUNK, CHUNK), CHUNK)
@@ -291,9 +288,57 @@
 
     lax.fori_loop(0, z_s.shape[1] // CHUNK, back_block, 0)
 
+
+def ffn_fwd(tok, o_own, o_peer, w_own, w_peer, bo, gain, shift, w_in, b_in, w_back, bb, cot_own):
+    rows, model = tok.shape
+    hidden = w_in.shape[1]
+    half = cot_own.shape[1]
+    shape = jax.ShapeDtypeStruct
+    vm = pltpu.VMEM
+    return pl.pallas_call(
+        ffn_fwd_kernel,
+        in_specs=[pl.BlockSpec(memory_space=pltpu.VMEM)] * 13,
+        out_specs=[pl.BlockSpec(memory_space=pltpu.VMEM)] * 8,
+        out_shape=[
+            shape((rows, half), F32), shape((rows, half), BF16), shape((rows, model), BF16),
+            shape((rows, 1), F32), shape((rows, model), BF16), shape((rows, hidden), BF16),
+            shape((rows, model), BF16), shape((hidden, model), BF16),
+        ],
+        scratch_shapes=[
+            vm((rows, hidden), BF16), vm((rows, half), BF16), vm((CHUNK, model), F32), vm((CHUNK, model), F32),
+        ] + two_sems(1),
+        compiler_params=pltpu.CompilerParams(collective_id=1, has_side_effects=True),
+        name="ffn_fwd",
+    )(tok, o_own, o_peer, w_own, w_peer, bo, gain, shift, w_in, b_in, w_back, bb, cot_own)
+
+
+def ffn_bwd_kernel(
+    n_in, r_in, h_in, slope, cot, w_in, w_back, w_own, gain, o_own,
+    gr, dot_t, g_out, g_in, vec, vec_in, du_s, gh_s, gh_p, go_s, wide_a, send_sem, recv_sem,
+):
+    rows_all, model = n_in.shape
+    half = gr.shape[1]
+    chunks = rows_all // CHUNK
+    sems = (send_sem, recv_sem)
+    own = half_lanes(lax.axis_index("mp"), half)
+    greet()
+    vec[...] = jnp.zeros_like(vec)
+    vec_in[...] = jnp.zeros_like(vec_in)
+
+    def forward(c, carry):
+        at = pl.ds(pl.multiple_of(c * CHUNK, CHUNK), CHUNK)
+        du = (dot_nt(cot[at, :], w_back[...]) * slope[at, :].astype(F32)).astype(BF16)
+        du_s[at, :] = du
+        gh_s[at, :] = dot_nt(du, w_in[...]).astype(BF16)
+        vec_in[...] += jnp.sum(du.astype(F32), axis=0, keepdims=True)
+        rows_copy(gh_s, gh_p, CHUNK, sems, c).start()
+        return carry
+
+    lax.fori_loop(0, chunks, forward, 0)
+
     def in_block(i, carry):
         at = pl.ds(pl.multiple_of(i * CHUNK, CHUNK), CHUNK)
-        g_in[at, :] = dot_tn(h_s[:, at], du_s[...]).astype(BF16)
+        g_in[at, :] = dot_tn(h_in[:, at], du_s[...]).astype(BF16)
         return carry
 
     lax.fori_loop(0, model // CHUNK, in_block, 0)
@@ -302,12 +347,12 @@
         at = pl.ds(pl.multiple_of(c * CHUNK, CHUNK), CHUNK)
         rows_copy(gh_s, gh_p, CHUNK, sems, c).wait()
         gh = gh_s[at, :].astype(F32) + gh_p[at, :].astype(F32)
-        n = n_s[at, :]
+        n = n_in[at, :].astype(F32)
         e = gh * gain[...]
         gy = cot[at, :].astype(F32)
         mean_e = jnp.mean(e, axis=-1, keepdims=True)
         mean_n = jnp.mean(e * n, axis=-1, keepdims=True)
-        gx1 = gy + r_s[at, :] * (e - mean_e - n * mean_n)
+        gx1 = gy + r_in[at, :] * (e - mean_e - n * mean_n)
         wide_a[...] = gx1
         go = gx1.astype(BF16)
         go_s[at, :] = go
@@ -323,30 +368,28 @@
     g_out[...] = dot_tn(o_own[...], go_s[...]).astype(BF16)
 
 
-def ffn(tok, o_own, o_peer, w_own, w_peer, bo, gain, shift, w_in, b_in, w_back, bb, cot):
-    rows, model = tok.shape
+def ffn_bwd(n_in, r_in, h_in, slope, cot, w_in, w_back, w_own, gain, o_own):
+    rows, model = n_in.shape
     width = o_own.shape[1]
     hidden = w_in.shape[1]
     half = model // 2
     shape = jax.ShapeDtypeStruct
     vm = pltpu.VMEM
     return pl.pallas_call(
-        ffn_kernel,
-        in_specs=[pl.BlockSpec(memory_space=pltpu.VMEM)] * 13,
-        out_specs=[pl.BlockSpec(memory_space=pltpu.VMEM)] * 9,
+        ffn_bwd_kernel,
+        in_specs=[pl.BlockSpec(memory_space=pltpu.VMEM)] * 10,
+        out_specs=[pl.BlockSpec(memory_space=pltpu.VMEM)] * 6,
         out_shape=[
-            shape((rows, half), F32), shape((rows, half), BF16), shape((rows, half), F32),
-            shape((width, rows), BF16), shape((width, model), BF16), shape((model, hidden), BF16),
-            shape((hidden, model), BF16), shape((8, model), F32), shape((1, hidden), F32),
+            shape((rows, half), F32), shape((width, rows), BF16), shape((width, model), BF16),
+            shape((model, hidden), BF16), shape((8, model), F32), shape((1, hidden), F32),
         ],
         scratch_shapes=[
-            vm((rows, model), F32), vm((rows, 1), F32), vm((rows, model), BF16), vm((rows, hidden), BF16),
             vm((rows, hidden), BF16), vm((rows, model), BF16), vm((rows, model), BF16),
-            vm((rows, model), BF16), vm((CHUNK, model), F32), vm((CHUNK, model), F32),
+            vm((rows, model), BF16), vm((CHUNK, model), F32),
         ] + two_sems(rows // CHUNK),
-        compiler_params=pltpu.CompilerParams(collective_id=1, has_side_effects=True),
-        name="ffn",
-    )(tok, o_own, o_peer, w_own, w_peer, bo, gain, shift, w_in, b_in, w_back, bb, cot)
+        compiler_params=pltpu.CompilerParams(collective_id=5, has_side_effects=True),
+        name="ffn_bwd",
+    )(n_in, r_in, h_in, slope, cot, w_in, w_back, w_own, gain, o_own)
 
 
 def attn_bwd_kernel(
@@ -673,18 +716,22 @@
         crop_counts, crop_patches, rel_index, rel_table, rows
     )
     whole_in = lax.all_gather(tokens, "mp", axis=1, tiled=True)
-    whole_cot = lax.all_gather(cotangent, "mp", axis=1, tiled=True)
     wt = jnp.transpose(w_qkv, (1, 2, 0)).reshape(3 * width, model)
     mixer_in, qt, kx, kt, vx, heads_out, heads_peer, w_peer, lse = attn_fwd(
         w_out,
         whole_in, ln1_gain[None, :], ln1_shift[None, :], wt, qv_bias[0][:, None], qv_bias[1][:, None],
         qv_bias[1][None, :], khot, qhott, table, kwin, qwin,
     )
-    keep, give, gr, dot_t, grad_w_out, grad_w_in, grad_w_back, vec2, grad_b_in = ffn(
+    keep, give, normed, spread, hidden_in, slope, whole_cot, grad_w_back = ffn_fwd(
         whole_in, heads_out, heads_peer, w_out, w_peer, b_out[None, :], ln2_gain[None, :], ln2_shift[None, :],
-        w_in, b_in[None, :], w_back, b_back[None, :], whole_cot,
-    )
-    early = lax.psum((grad_w_in, grad_w_back, grad_w_out), "dp")
+        w_in, b_in[None, :], w_back, b_back[None, :], cotangent,
+    )
+    ranks = lax.axis_size("dp")
+    grad_w_back = lax.psum(grad_w_back, "dp", axis_index_groups=[list(range(ranks))[::-1]])
+    gr, dot_t, grad_w_out, grad_w_in, vec2, grad_b_in = ffn_bwd(
+        normed, spread, hidden_in, slope, whole_cot, w_in, w_back, w_out, ln2_gain[None, :], heads_out
+    )
+    early = lax.psum((grad_w_in, grad_w_out), "dp")
     out_half, grad_query, grad_key, grad_value, gcell = attn_bwd(
         keep, give, qt, kx, kt, vx, dot_t, khot, khott, qhott, qhot, table, kwin, qwin, lse
     )
@@ -693,15 +740,15 @@
     )
     table_rows = -(-grad_table.size // model)
     table_flat = jnp.pad(grad_table.reshape(-1), (0, table_rows * model - grad_table.size))
-    ranks = lax.axis_size("dp")
     late_rows = -(-(3 * width + SMALL) // (16 * ranks)) * 16 * ranks
     grad_half, late = close(
         late_rows, whole_in, mixer_in, grad_query, grad_key, grad_value, wt, ln1_gain[None, :], gr,
         vec2, grad_b_in, table_flat.reshape(table_rows, model),
     )
     late = dp_sum(ranks, late)
-    early, late = lax.optimization_barrier((early, late))
-    grad_w_in, grad_w_back, grad_w_out = (item.astype(F32) for item in early)
+    grad_w_back, early, late = lax.optimization_barrier((grad_w_back, early, late))
+    grad_w_back = grad_w_back.astype(F32)
+    grad_w_in, grad_w_out = (item.astype(F32) for item in early)
     late = late[: 3 * width + SMALL].astype(F32)
     grad_w_qkv = jnp.transpose(late[: 3 * width].reshape(3, width, model), (2, 0, 1))
     small = late[3 * width :]

time: 309 us -> 346 us (1.12)
  waiting for transfers between devices: 17.7 us -> 53.3 us
    psum x1 -> x2, waiting for transfers between devices: 4.49 us -> 40.7 us  [the longest x1 40.7 us: body(): early = lax.psum((grad_w_in, grad_w_out), 'dp')]
    pallas_call x1 -> x2, Pallas kernels: 47.4 us -> 73.7 us  [the longest x1 43.6 us: ffn_bwd(): pl.pallas_call(ffn_bwd_kernel, in_specs=[pl.BlockSpec(memory_space=pltpu....]
    pallas_call x1, Pallas kernels: 54.5 us -> 37.7 us  [attn_fwd(): pl.pallas_call(partial(attn_fwd_kernel, heads // GROUP), grid=(rows // QB...]
    pallas_call x1, Pallas kernels: 64 us -> 55.8 us  [dp_sum(): pl.pallas_call(partial(dp_sum_kernel, orders), in_specs=[pl.BlockSpec(mem...]
  transfers between devices with their start and end apart: 3 -> 3, of which waited for: 2 -> 2; matrix products, arithmetic and copies ran while one was open for 7% -> 7% of each run, Pallas kernels for 61% -> 49%
where the time goes in v4:
time: 346 us
  Pallas kernels  236 us (68%)
  waiting for transfers between devices  53.3 us (15%)
  local copies, waits for them, and re-layouts  21.7 us (6%)
  other arithmetic  17.8 us (5%)
  between operations  14.7 us (4%)
    pallas_call x1, Pallas kernels, dp_sum(): pl.pallas_call(partial(dp_sum_kernel, orders), in_specs=[pl.BlockSpec(mem...  55.8 us
    pallas_call x1, Pallas kernels, ffn_bwd(): pl.pallas_call(ffn_bwd_kernel, in_specs=[pl.BlockSpec(memory_space=pltpu....  43.6 us
    psum x1, waiting for transfers between devices, body(): early = lax.psum((grad_w_in, grad_w_out), 'dp')  40.7 us
    pallas_call x1, Pallas kernels, attn_fwd(): pl.pallas_call(partial(attn_fwd_kernel, heads // GROUP), grid=(rows // QB...  37.7 us
    pallas_call x1, Pallas kernels, close(): pl.pallas_call(close_kernel, in_specs=[pl.BlockSpec(memory_space=pltpu.VM...  35.1 us
    pallas_call x1, Pallas kernels, attn_bwd(): pl.pallas_call(partial(attn_bwd_kernel, heads // GROUP), grid=(rows // QB...  33.5 us
    pallas_call x1, Pallas kernels, ffn_fwd(): pl.pallas_call(ffn_fwd_kernel, in_specs=[pl.BlockSpec(memory_space=pltpu....  30.1 us
    all_gather x1, waiting for transfers between devices, body(): whole_in = lax.all_gather(tokens, 'mp', axis=1, tiled=True)  11.8 us
  transfers between devices with their start and end apart: 3, of which 2 were waited for; matrix products, arithmetic and copies ran while one was open for 7% of the time, Pallas kernels for 49%

profile of v4, /device:TPU:0, one launch (start us, length us, event | category | flops | bytes accessed | tf_op | source)
XLA Modules:
  0.0 346.0 jit_solution(10303237633735452844)
XLA Ops:
  7.2 0.0 all-gather.2.cloned.1.call-start
  7.3 0.7 all-gather.2.cloned.1.call-update
  8.0 0.0 all-reduce.8.cloned.1.call-start
  8.0 0.8 fusion.13
  8.8 0.1 reshape.173
  8.8 0.1 reduce-window.4
  8.9 0.5 slice.76
  9.4 0.1 reduce
  10.2 0.2 convert_reduce_fusion
  10.4 0.8 fusion.10
  11.1 0.1 pad.15
  11.2 0.7 subtract_select_fusion
  11.9 0.1 pad.17
  11.9 1.0 broadcast_in_dim.91.kwin
  13.0 0.8 copy.64
  13.8 0.1 eq.88
  13.9 1.1 subtract_convert_fusion
  15.0 0.2 stack_reshape.6
  15.2 0.2 stack_reshape.7
  15.4 0.6 fusion.16
  16.0 0.8 copy.56.qb_col
  16.8 0.8 copy.57.vb_col
  17.7 2.2 copy.51
  19.9 0.6 broadcast_in_dim.78.gain
  20.5 0.6 broadcast_in_dim.79.shift
  21.1 0.6 broadcast_in_dim.87.gain
  21.7 0.6 broadcast_in_dim.89.b_in
  22.3 0.6 broadcast_in_dim.86.bo
  22.8 0.6 broadcast_in_dim.88.shift
  23.4 0.6 broadcast_in_dim.90.bb
  24.0 0.8 pad_maximum_fusion
  24.8 1.2 compare_select_fusion.qwin
  26.1 0.7 fusion.6.qhott
  26.8 0.9 compare_convert_fusion.khot
  27.7 11.8 %all-gather.2.cloned.1.call-done.tok = bf16[1024,768]{1,0:T(8,128)(2,1)} async-done(((bf16[1024,384]{1,0:T(8,128)(2,1)}), bf16[1024,768]{1,0:T(8,128)(2,1)}) %all-gather.2.cloned.1.call-update) | async-done | bytes 1572880 | tf_op jit(solution)/shard_map/all_gather | solution.py:718
  39.5 37.7 %attn_fwd.1 = (bf16[1024,768]{1,0:T(8,128)(2,1)}, bf16[384,1024]{1,0:T(8,128)(2,1)}, bf16[1152,384]{1,0:T(8,128)(2,1)}, bf16[384,1152]{1,0:T(8,128)(2,1)}, bf16[...) custom-call(bf16[384,768]{1,0:T(8,128)(2,1)} %w_own.5, ...), custom_call_target="tpu_custom_call" | custom-call | tf_op jit(solution)/shard_map/attn_fwd/pallas_call | solution.py:217
  77.2 30.1 %ffn_fwd.1 = (f32[1024,384]{1,0:T(8,128)}, bf16[1024,384]{1,0:T(8,128)(2,1)}, bf16[1024,768]{1,0:T(8,128)(2,1)}, f32[1024,1]{1,0:T(8,128)}, bf16[1024,768]{1,0:T...) custom-call(bf16[1024,768]{1,0:T(8,128)(2,1)} %all-gather.2.cloned.1.call-done.tok, ...), custom_call_target="tpu_custom_call" | custom-call | tf_op jit(solution)/shard_map/ffn_fwd/pallas_call | solution.py:298
  107.3 0.2 all-reduce.10.cloned.1.call-start
  107.5 43.6 %ffn_bwd.1 = (f32[1024,384]{1,0:T(8,128)}, bf16[384,1024]{1,0:T(8,128)(2,1)}, bf16[384,768]{1,0:T(8,128)(2,1)}, bf16[768,1536]{1,0:T(8,128)(2,1)}, f32[8,768]{1,0:T(8,128)}, /*index=5*/f32[1,1536]{1,0:T(1,128)}) custom-call(bf16[1024,768]{1,0:T(8,128)(2,1)} %get-tuple-element.58.n_in, f32[1024,1]{1,0:T(8,128)} %get-tuple-element.59.r_in, ...), custom_call_target="tpu_custom_call" | custom-call | tf_op jit(solution)/shard_map/ffn_bwd/pallas_call | solution.py:378
  151.1 0.9 fusion.4.qhot
  152.0 0.7 fusion.5.khott
  152.7 33.5 %attn_bwd.1 = (bf16[1024,384]{1,0:T(8,128)(2,1)}, bf16[1024,384]{1,0:T(8,128)(2,1)}, bf16[1024,384]{1,0:T(8,128)(2,1)}, bf16[1024,384]{1,0:T(8,128)(2,1)}, f32[768,64]{1,0:T(8,128)}) custom-call(f32[1024,384]{1,0:T(8,128)} %get-tuple-element.52.keep, bf16[1024,384]{1,0:T(8,128)(2,1)} %get-tuple-element.53.give, bf16[384,1024]{1,0:T(8,128)(2,1)} %get-tuple-element.54.qt, ...), custom_call_target="tpu_custom_call" | custom-call | tf_op jit(solution)/shard_map/attn_bwd/pallas_call | solution.py:458
  186.3 1.1 reshape.168
  187.4 1.4 fusion.1
  188.8 0.1 reshape.169
  188.9 0.6 reshape.170.table
  189.5 35.1 %close.1 = (bf16[1024,384]{1,0:T(8,128)(2,1)}, bf16[1280,768]{1,0:T(8,128)(2,1)}) custom-call(bf16[1024,768]{1,0:T(8,128)(2,1)} %all-gather.2.cloned.1.call-done.tok, bf16[1024,768]{1,0:T(8,128)(2,1)} %get-tuple-element.66.a, bf16[1024,384]{1,0:T(8,128)(2,1)} %get-tuple-element.67.dq, bf16[1024,384]{1,0:T(8,128)(2,1)} %get-tuple-element.68.dk, ...), custom_call_target="tpu_custom_call" | custom-call | tf_op jit(solution)/shard_map/close/pallas_call | solution.py:562
  224.7 55.8 %dp_sum.1 = bf16[1280,768]{1,0:T(8,128)(2,1)} custom-call(bf16[1280,768]{1,0:T(8,128)(2,1)} %get-tuple-element.78.x), custom_call_target="tpu_custom_call" | custom-call | tf_op jit(solution)/shard_map/dp_sum/pallas_call | solution.py:658
  280.4 0.0 all-reduce.8.cloned.1.call-done
  280.5 40.7 %all-reduce.10.cloned.1.call-done = (bf16[768,1536]{1,0:T(8,128)(2,1)}, bf16[384,768]{1,0:T(8,128)(2,1)}) async-done(((bf16[768,1536]{1,0:T(8,128)(2,1)}, bf16[384,768]{1,0:T(8,128)(2,1)}), (bf16[768,1536]{1,0:T(8,128)(2,1)}, bf16[384,768]{1,0:T(8,128)(2,1)})) %all-reduce.10.cloned.1.call-update) | async-done | bytes 2949136 | tf_op jit(solution)/shard_map/psum | solution.py:734
  321.2 1.7 slice_convert_fusion
  322.9 0.2 slice.79
  323.2 0.7 slice_reduce_fusion
  323.8 0.6 slice.86
  324.4 2.9 copy.61
  327.4 4.6 %convert_element_type.49 = f32[768,1536]{1,0:T(8,128)} convert(bf16[768,1536]{1,0:T(8,128)(2,1)} %get-tuple-element.81) | non-fusion elementwise | flops 1179648 | bytes 7077888 | tf_op jit(solution)/shard_map/convert_element_type | solution.py:751
  332.0 2.5 convert_element_type.50
  334.6 0.1 slice.69
  334.7 0.7 copy.62
  335.4 0.6 reshape_squeeze.3
  336.0 0.6 reshape.172
  336.6 1.1 convert_element_type.48
  337.7 0.9 copy.70
  338.6 0.9 copy.71
  (39 shorter events, 0.1 us)
Async XLA Ops:
  7.2 6.7 %copy-start = (f32[169,12]{0,1:T(8,128)S(1)}, f32[169,12]{0,1:T(8,128)}, u32[]{:S(2)}) copy-start(f32[169,12]{0,1:T(8,128)} %param.26) | copy-start | bytes 24340
  7.2 8.2 %copy-start.15 = (f32[2,384]{1,0:T(2,128)S(1)}, f32[2,384]{1,0:T(2,128)}, u32[]{:S(2)}) copy-start(f32[2,384]{1,0:T(2,128)} %param.25) | copy-start | bytes 9220
  7.2 10.5 %copy-start.3 = (bf16[768,3,384]{2,0,1:T(8,128)(2,1)S(1)}, bf16[768,3,384]{2,0,1:T(8,128)(2,1)}, u32[]{:S(2)}) copy-start(bf16[768,3,384]{2,0,1:T(8,128)(2,1)} %param.24) | copy-start | bytes 5308420
  7.2 32.3 %all-gather.2.cloned.1.call-start = ((), (), s32[]{:S(2)}) async-start(), calls=%async_computation | async-start | bytes 2359296 | tf_op jit(solution)/shard_map/all_gather | solution.py:718
  8.0 272.5 %all-reduce.8.cloned.1.call-start = ((), (), s32[]{:S(2)}) async-start(), calls=%async_computation.1 | async-start | bytes 4718592 | tf_op jit(solution)/shard_map/psum | solution.py:730
  15.0 4.9 %copy-start.9 = (f32[768]{0:T(1024)S(1)}, f32[768]{0:T(1024)}, u32[]{:S(2)}) copy-start(f32[768]{0:T(1024)} %param.22) | copy-start | bytes 9220
  15.0 5.5 %copy-start.10 = (f32[768]{0:T(1024)S(1)}, f32[768]{0:T(1024)}, u32[]{:S(2)}) copy-start(f32[768]{0:T(1024)} %param.23) | copy-start | bytes 9220
  15.0 6.1 %copy-start.11 = (f32[768]{0:T(1024)S(1)}, f32[768]{0:T(1024)}, u32[]{:S(2)}) copy-start(f32[768]{0:T(1024)} %param.29) | copy-start | bytes 9220
  15.0 6.7 %copy-start.8 = (f32[1536]{0:T(1024)S(1)}, f32[1536]{0:T(1024)}, u32[]{:S(2)}) copy-start(f32[1536]{0:T(1024)} %param.32) | copy-start | bytes 18436
  15.0 7.3 %copy-start.12 = (f32[768]{0:T(1024)S(1)}, f32[768]{0:T(1024)}, u32[]{:S(2)}) copy-start(f32[768]{0:T(1024)} %param.28) | copy-start | bytes 9220
  15.0 7.8 %copy-start.13 = (f32[768]{0:T(1024)S(1)}, f32[768]{0:T(1024)}, u32[]{:S(2)}) copy-start(f32[768]{0:T(1024)} %param.30) | copy-start | bytes 9220
  15.0 8.4 %copy-start.14 = (f32[768]{0:T(1024)S(1)}, f32[768]{0:T(1024)}, u32[]{:S(2)}) copy-start(f32[768]{0:T(1024)} %param.34) | copy-start | bytes 9220
  107.3 213.9 %all-reduce.10.cloned.1.call-start = ((), (), s32[]{:S(2)}) async-start(), calls=%async_computation.2 | async-start | bytes 5898240 | tf_op jit(solution)/shard_map/psum | solution.py:734
  327.4 4.7 %copy-start.2 = (bf16[1536,768]{1,0:T(8,128)(2,1)S(1)}, bf16[1536,768]{1,0:T(8,128)(2,1)}, u32[]{:S(2)}) copy-start(bf16[1536,768]{1,0:T(8,128)(2,1)} %all-reduce.8.cloned.1.call-done) | copy-start | bytes 7077892
  332.0 4.0 %copy-start.7 = (f32[2,768]{1,0:T(2,128)S(1)}, f32[2,768]{1,0:T(2,128)}, u32[]{:S(2)}) copy-start(f32[2,768]{1,0:T(2,128)} %slice.86) | copy-start | bytes 18436
  332.0 4.6 %copy-start.6 = (bf16[384,768]{1,0:T(8,128)(2,1)S(1)}, bf16[384,768]{1,0:T(8,128)(2,1)}, u32[]{:S(2)}) copy-start(bf16[384,768]{1,0:T(8,128)(2,1)} %get-tuple-element.80) | copy-start | bytes 1769476
  334.6 3.1 copy-start.4
  334.6 4.0 %copy-start.5 = (bf16[1024,384]{1,0:T(8,128)(2,1)S(1)}, bf16[1024,384]{1,0:T(8,128)(2,1)}, u32[]{:S(2)}) copy-start(bf16[1024,384]{1,0:T(8,128)(2,1)} %get-tuple-element.146) | copy-start | bytes 2359300
  336.0 3.5 %copy-start.1 = (f32[169,12]{0,1:T(8,128)S(1)}, f32[169,12]{0,1:T(8,128)}, u32[]{:S(2)}) copy-start(f32[169,12]{0,1:T(8,128)} %param.26) | copy-start | bytes 24340
Sparse Core Ops, SparseCore 0:
  9.6 29.9 all-gather.1
  107.4 99.4 all-reduce.7
  210.6 110.4 all-reduce.9

commit v5 on v3

--- a/solution.py
+++ b/solution.py
@@ -123,11 +123,20 @@
     rows_all = tok.shape[0]
     width = qt.shape[0]
     sems = (send_sem, recv_sem)
-    weight = to_peer(w_own, w_got, send_sem.at[last + 1], recv_sem.at[last + 1])
+    place = lax.axis_index("dp")
+    core = lax.rem(place, 2)
+    mate = place + 1 - 2 * core
+    fetched = w_own.shape[0] // 2
+    part = pl.ds(pl.multiple_of(core * fetched, 16), fetched)
+    weight = to_peer(w_own.at[part], w_got.at[part], send_sem.at[last + 1], recv_sem.at[last + 1])
+    handed = dp_copy(w_got.at[part], w_got.at[part], mate, send_sem.at[last + 2], recv_sem.at[last + 2])
 
     @pl.when(step == 0)
     def _():
-        greet()
+        barrier = pltpu.get_barrier_semaphore()
+        pl.semaphore_signal(barrier, inc=1, device_id={"mp": peer_of()}, device_id_type=MESH)
+        pl.semaphore_signal(barrier, inc=1, device_id={"dp": mate}, device_id_type=MESH)
+        pl.semaphore_wait(barrier, 2)
         weight.start()
         zero = jnp.zeros((HALO, tok.shape[1]), BF16)
         a_pad[:HALO, :] = zero
@@ -176,6 +185,11 @@
     def _():
         rows_copy(o_all, o_peer, QB, sems, step - 1).start()
 
+    @pl.when(step == last - 2)
+    def _():
+        weight.wait()
+        handed.start()
+
     @pl.when(step == last)
     def _():
         o_out[...] = o_all[...]
@@ -187,7 +201,7 @@
             return carry
 
         lax.fori_loop(0, last + 1, finish, 0)
-        weight.wait()
+        handed.wait()
         w_out[...] = w_got[...]
         peer_out[...] = o_peer[...]
 
@@ -233,7 +247,7 @@
             pltpu.VMEM((ext, model), BF16), pltpu.VMEM((width, ext), BF16),
             pltpu.VMEM((rows, width), BF16), pltpu.VMEM((rows, width), BF16),
             pltpu.VMEM((width, model), BF16),
-        ] + two_sems(rows // QB + 1),
+        ] + two_sems(rows // QB + 2),
         compiler_params=pltpu.CompilerParams(collective_id=0, has_side_effects=True),
         name="attn_fwd",
     )(w_own, tok, gain, shift, wt, qb_col, vb_col, vb_row, khot, qhott, table, kwin, qwin)
@@ -242,7 +256,7 @@
 def ffn_kernel(
     tok, o_own, o_peer, w_own, w_peer, bo, gain, shift, w_in, b_in, w_back, bb, cot,
     keep, give, gr, dot_t, g_out, g_in, g_back, vec, vec_in,
-    n_s, r_s, h_s, z_s, du_s, gh_s, gh_p, go_s, wide_a, wide_b, send_sem, recv_sem,
+    n_s, r_s, h_s, z_s, du_s, gh_s, gh_p, g_acc, wide_a, wide_b, send_sem, recv_sem,
 ):
     rows_all, model = tok.shape
     half = keep.shape[1]
@@ -276,13 +290,21 @@
         du_s[at, :] = du
         gh_s[at, :] = dot_nt(du, w_in[...]).astype(BF16)
         vec_in[...] += jnp.sum(du.astype(F32), axis=0, keepdims=True)
-        wide_a[...] = dot(z, w_back[...])
+        keep[at, :] = wide_b[:, own] + bb[:, own]
         rows_copy(gh_s, gh_p, CHUNK, sems, c).start()
-        keep[at, :] = wide_a[:, own] + wide_b[:, own] + bb[:, own]
+        return carry
+
+    lax.fori_loop(0, chunks, forward, 0)
+
+    def output(c, carry):
+        at = pl.ds(pl.multiple_of(c * CHUNK, CHUNK), CHUNK)
+        wide_a[...] = dot(z_s[at, :], w_back[...])
+        keep[at, :] += wide_a[:, own]
         give[at, :] = wide_a[:, other].astype(BF16)
         return carry
 
-    lax.fori_loop(0, chunks, forward, 0)
+    lax.fori_loop(0, chunks, output, 0)
+    g_acc[...] = jnp.zeros_like(g_acc)
 
     def back_block(i, carry):
         at = pl.ds(pl.multiple_of(i * CHUNK, CHUNK), CHUNK)
@@ -310,7 +332,7 @@
         gx1 = gy + r_s[at, :] * (e - mean_e - n * mean_n)
         wide_a[...] = gx1
         go = gx1.astype(BF16)
-        go_s[at, :] = go
+        g_acc[...] += dot_tn(o_own[at, :], go)
         dot_t[:, at] = dot_nt(w_own[...], go).astype(BF16)
         vec[0:1, :] += jnp.sum(gh * n, axis=0, keepdims=True)
         vec[1:2, :] += jnp.sum(gh, axis=0, keepdims=True)
@@ -320,7 +342,7 @@
         return carry
 
     lax.fori_loop(0, chunks, backward, 0)
-    g_out[...] = dot_tn(o_own[...], go_s[...]).astype(BF16)
+    g_out[...] = g_acc[...].astype(BF16)
 
 
 def ffn(tok, o_own, o_peer, w_own, w_peer, bo, gain, shift, w_in, b_in, w_back, bb, cot):
@@ -342,7 +364,7 @@
         scratch_shapes=[
             vm((rows, model), F32), vm((rows, 1), F32), vm((rows, model), BF16), vm((rows, hidden), BF16),
             vm((rows, hidden), BF16), vm((rows, model), BF16), vm((rows, model), BF16),
-            vm((rows, model), BF16), vm((CHUNK, model), F32), vm((CHUNK, model), F32),
+            vm((width, model), F32), vm((CHUNK, model), F32), vm((CHUNK, model), F32),
         ] + two_sems(rows // CHUNK),
         compiler_params=pltpu.CompilerParams(collective_id=1, has_side_effects=True),
         name="ffn",
@@ -478,8 +500,13 @@
 
     lax.fori_loop(0, chunks, forward, 0)
     vectors = to_peer(vec_s, vec_p, send_sem.at[2, 0], recv_sem.at[2, 0])
-    for k, item in enumerate((dq, dk, dv)):
-        late[width * k : width * (k + 1), :] = dot_tn(item[...], a[...]).astype(BF16)
+    grads = jnp.concatenate([dq[...], dk[...], dv[...]], axis=1)
+    for b in range(2):
+        block = dot_tn(a[:, width * b : width * (b + 1)], grads).astype(BF16)
+        for c in range(3):
+            k = 2 * c + b
+            goal = (width * (k % 3), width * (k // 3))
+            late[goal[0] : goal[0] + width, goal[1] : goal[1] + width] = block[:, width * c : width * (c + 1)]
     vectors.start()
     qv = [jnp.sum(item[...].astype(F32), axis=0, keepdims=True) for item in (dq, dv)]
 
@@ -542,7 +569,7 @@
     )
 
 
-def dp_sum_kernel(orders, x, out, acc, got, send_sem, recv_sem):
+def dp_sum_kernel(orders, x, big, small, out, acc, got, send_sem, recv_sem):
     rows, wide = x.shape
     part = wide // len(orders)
     steps = len(orders[0])
@@ -604,9 +631,13 @@
             state[k] = (out, kept[k][s])
         for copy in copies:
             copy.wait()
-
-
-def dp_sum(ranks, x):
+    tall = big.shape[0] // 2
+    for k in range(2):
+        big[tall * k : tall * (k + 1), :] = out[:tall, big.shape[1] * k : big.shape[1] * (k + 1)]
+    small[...] = out[tall : tall + small.shape[0], :].astype(F32)
+
+
+def dp_sum(ranks, big_shape, x):
     rows, wide = x.shape
     steps = ranks.bit_length() - 1
     orders = [list(range(steps)), [0] + list(range(2, steps)) + [1]]
@@ -615,9 +646,9 @@
     return pl.pallas_call(
         partial(dp_sum_kernel, orders),
         in_specs=[pl.BlockSpec(memory_space=pltpu.VMEM)],
-        out_specs=pl.BlockSpec(memory_space=pltpu.VMEM),
-        out_shape=jax.ShapeDtypeStruct((rows, wide), BF16),
-        scratch_shapes=[vm((rows, wide), BF16), vm((rows, wide), BF16), sems, sems],
+        out_specs=[pl.BlockSpec(memory_space=pltpu.VMEM)] * 2,
+        out_shape=[jax.ShapeDtypeStruct(big_shape, BF16), jax.ShapeDtypeStruct((SMALL, wide), F32)],
+        scratch_shapes=[vm((rows, wide), BF16)] * 3 + [sems, sems],
         compiler_params=pltpu.CompilerParams(collective_id=4, has_side_effects=True),
         name="dp_sum",
     )(x)
@@ -699,12 +730,10 @@
         late_rows, whole_in, mixer_in, grad_query, grad_key, grad_value, wt, ln1_gain[None, :], gr,
         vec2, grad_b_in, table_flat.reshape(table_rows, model),
     )
-    late = dp_sum(ranks, late)
-    early, late = lax.optimization_barrier((early, late))
+    big, small = dp_sum(ranks, (3 * model, width), late)
+    early, big = lax.optimization_barrier((early, big))
     grad_w_in, grad_w_back, grad_w_out = (item.astype(F32) for item in early)
-    late = late[: 3 * width + SMALL].astype(F32)
-    grad_w_qkv = jnp.transpose(late[: 3 * width].reshape(3, width, model), (2, 0, 1))
-    small = late[3 * width :]
+    grad_w_qkv = jnp.transpose(big.astype(F32).reshape(3, model, width), (1, 0, 2))
     grad_g1, grad_c1, grad_g2, grad_c2, grad_b_out, grad_b_back = (small[k] for k in range(6))
     grad_qv_bias = small[6].reshape(2, width)
     hidden_rows = w_in.shape[1] // model

time: 309 us -> 300 us (0.971)
  waiting for transfers between devices: 17.7 us -> 10.3 us
    pallas_call x1, Pallas kernels: 54.5 us -> 48.6 us  [attn_fwd(): pl.pallas_call(partial(attn_fwd_kernel, heads // GROUP), grid=(rows // QB...]
    psum x1, waiting for transfers between devices: 4.49 us -> 0.01 us  [body(): early = lax.psum((grad_w_in, grad_w_back, grad_w_out), 'dp')]
    transpose x0 -> x1, other arithmetic: none -> 3.65 us  [body(): jnp.transpose(big.astype(F32).reshape(3, model, width), (1, 0, 2))]
  transfers between devices with their start and end apart: 3 -> 3, of which waited for: 2 -> 1; matrix products, arithmetic and copies ran while one was open for 7% -> 10% of each run, Pallas kernels for 61% -> 61%
where the time goes in v5:
time: 300 us
  Pallas kernels  232 us (77%)
  local copies, waits for them, and re-layouts  22.8 us (8%)
  other arithmetic  17.9 us (6%)
  between operations  14.6 us (5%)
  waiting for transfers between devices  10.3 us (3%)
    pallas_call x1, Pallas kernels, dp_sum(): pl.pallas_call(partial(dp_sum_kernel, orders), in_specs=[pl.BlockSpec(mem...  64.9 us
    pallas_call x1, Pallas kernels, attn_fwd(): pl.pallas_call(partial(attn_fwd_kernel, heads // GROUP), grid=(rows // QB...  48.6 us
    pallas_call x1, Pallas kernels, ffn(): pl.pallas_call(ffn_kernel, in_specs=[pl.BlockSpec(memory_space=pltpu.VMEM...  47.8 us
    pallas_call x1, Pallas kernels, close(): pl.pallas_call(close_kernel, in_specs=[pl.BlockSpec(memory_space=pltpu.VM...  36.7 us
    pallas_call x1, Pallas kernels, attn_bwd(): pl.pallas_call(partial(attn_bwd_kernel, heads // GROUP), grid=(rows // QB...  33.6 us
    all_gather x1, waiting for transfers between devices, body(): whole_in = lax.all_gather(tokens, 'mp', axis=1, tiled=True)  8.85 us
    convert_element_type x3, other arithmetic, body(): grad_w_in, grad_w_back, grad_w_out = (item.astype(F32) for item in early)  6.46 us
  transfers between devices with their start and end apart: 3, of which 1 were waited for; matrix products, arithmetic and copies ran while one was open for 10% of the time, Pallas kernels for 61%

profile of v5, /device:TPU:0, one launch (start us, length us, event | category | flops | bytes accessed | tf_op | source)
XLA Modules:
  0.0 299.6 jit_solution(8579444084793931037)
XLA Ops:
  7.2 0.0 copy-start
  7.2 0.0 all-gather.3.cloned.1.call-start
  7.2 0.7 all-gather.3.cloned.1.call-update
  8.0 0.0 all-gather.5.cloned.1.call-start
  8.0 0.7 all-gather.5.cloned.1.call-update
  8.7 0.0 all-reduce.7.cloned.1.call-start
  8.7 0.8 fusion.13
  9.5 0.1 reshape.175
  9.6 0.1 reduce-window.4
  9.7 0.1 reduce
  9.8 0.5 slice.58
  10.3 1.3 broadcast_in_dim.77.gain
  11.6 1.3 broadcast_in_dim.78.shift
  12.9 3.9 %copy.49 = bf16[3,384,768]{2,1,0:T(8,128)(2,1)} copy(bf16[3,384,768]{1,2,0:T(8,128)(2,1)} %bitcast.24) | data formatting | bytes 3538944 | tf_op jit(solution)/shard_map/transpose | solution.py:708
  16.7 0.6 fusion.16
  17.3 0.8 copy.54.qb_col
  18.1 0.8 copy.55.vb_col
  19.6 0.2 convert_reduce_fusion
  19.8 0.8 fusion.10
  20.6 0.1 pad.15
  20.6 0.1 copy.61
  20.7 0.1 eq.88
  20.8 1.1 subtract_convert_fusion
  21.9 0.2 stack_reshape.7
  22.1 0.2 stack_reshape.6
  22.3 0.7 subtract_select_fusion
  22.9 0.1 pad.17
  23.0 1.0 broadcast_in_dim.90.kwin
  24.0 0.6 broadcast_in_dim.85.bo
  24.6 0.6 broadcast_in_dim.86.gain
  25.2 0.6 broadcast_in_dim.87.shift
  25.8 0.6 broadcast_in_dim.88.b_in
  26.4 0.6 broadcast_in_dim.89.bb
  27.0 0.8 pad_maximum_fusion
  27.8 1.2 compare_select_fusion.qwin
  29.0 0.7 fusion.6.qhott
  29.7 0.9 compare_convert_fusion.khot
  30.6 8.8 %all-gather.3.cloned.1.call-done.tok = bf16[1024,768]{1,0:T(8,128)(2,1)} async-done(((bf16[1024,384]{1,0:T(8,128)(2,1)}), bf16[1024,768]{1,0:T(8,128)(2,1)}) %all-gather.3.cloned.1.call-update) | async-done | bytes 1572880 | tf_op jit(solution)/shard_map/all_gather | solution.py:706
  39.5 48.6 %attn_fwd.1 = (bf16[1024,768]{1,0:T(8,128)(2,1)}, bf16[384,1024]{1,0:T(8,128)(2,1)}, bf16[1152,384]{1,0:T(8,128)(2,1)}, bf16[384,1152]{1,0:T(8,128)(2,1)}, bf16[...) custom-call(bf16[384,768]{1,0:T(8,128)(2,1)} %w_own.3, ...), custom_call_target="tpu_custom_call" | custom-call | tf_op jit(solution)/shard_map/attn_fwd/pallas_call | solution.py:231
  88.1 0.0 all-gather.5.cloned.1.call-done.cot
  88.1 47.8 %ffn.1 = (f32[1024,384]{1,0:T(8,128)}, bf16[1024,384]{1,0:T(8,128)(2,1)}, f32[1024,384]{1,0:T(8,128)}, bf16[384,1024]{1,0:T(8,128)(2,1)}, bf16[384,768]{1,0:T(8,...) custom-call(bf16[1024,768]{1,0:T(8,128)(2,1)} %all-gather.3.cloned.1.ca, ...), custom_call_target="tpu_custom_call" | custom-call | tf_op jit(solution)/shard_map/ffn/pallas_call | solution.py:355
  135.9 0.0 all-reduce.7.cloned.1.call-update
  135.9 0.9 fusion.4.qhot
  136.8 0.7 fusion.5.khott
  137.5 33.6 %attn_bwd.1 = (bf16[1024,384]{1,0:T(8,128)(2,1)}, bf16[1024,384]{1,0:T(8,128)(2,1)}, bf16[1024,384]{1,0:T(8,128)(2,1)}, bf16[1024,384]{1,0:T(8,128)(2,1)}, f32[768,64]{1,0:T(8,128)}) custom-call(f32[1024,384]{1,0:T(8,128)} %get-tuple-element.49.keep, bf16[1024,384]{1,0:T(8,128)(2,1)} %get-tuple-element.50.give, bf16[384,1024]{1,0:T(8,128)(2,1)} %get-tuple-element.51.qt, ...), custom_call_target="tpu_custom_call" | custom-call | tf_op jit(solution)/shard_map/attn_bwd/pallas_call | solution.py:437
  171.1 1.1 reshape.169
  172.2 1.4 fusion.1
  173.6 0.1 reshape.170
  173.8 0.6 reshape.171.table
  174.4 36.7 %close.1 = (bf16[1024,384]{1,0:T(8,128)(2,1)}, bf16[1280,768]{1,0:T(8,128)(2,1)}) custom-call(bf16[1024,768]{1,0:T(8,128)(2,1)} %all-gather.3.cloned.1.call-done.tok, bf16[1024,768]{1,0:T(8,128)(2,1)} %get-tuple-element.58.a, bf16[1024,384]{1,0:T(8,128)(2,1)} %get-tuple-element.59.dq, bf16[1024,384]{1,0:T(8,128)(2,1)} %get-tuple-element.60.dk, ...), custom_call_target="tpu_custom_call" | custom-call | tf_op jit(solution)/shard_map/close/pallas_call | solution.py:546
  211.1 64.9 %dp_sum.1 = (bf16[2304,384]{1,0:T(8,128)(2,1)}, f32[16,768]{1,0:T(8,128)}) custom-call(bf16[1280,768]{1,0:T(8,128)(2,1)} %get-tuple-element.67.x), custom_call_target="tpu_custom_call" | custom-call | tf_op jit(solution)/shard_map/dp_sum/pallas_call | solution.py:646
  276.0 0.7 slice.50
  276.7 0.8 slice.56
  277.5 1.7 slice_reduce_fusion
  279.2 0.6 reshape_squeeze.3
  279.8 0.1 slice.51
  279.9 0.7 copy.59
  280.6 0.6 reshape.173
  281.2 3.6 %convert_bitcast_fusion = f32[768,3,384]{2,0,1:T(8,128)} fusion(bf16[3,768,384]{2,1,0:T(8,128)(2,1)} %bitcast.25), kind=kLoop, calls=%fused_computation.2 | loop fusion | flops 884736 | bytes 5308416 | tf_op jit(solution)/shard_map/transpose | solution.py:736
  284.9 1.1 convert_element_type.45
  286.0 2.8 convert_element_type.46
  288.8 2.5 convert_element_type.47
  291.4 0.9 copy.67
  292.2 0.9 copy.68
  (30 shorter events, 0.1 us)
Async XLA Ops:
  7.2 13.6 %copy-start = (f32[169,12]{0,1:T(8,128)S(1)}, f32[169,12]{0,1:T(8,128)}, u32[]{:S(2)}) copy-start(f32[169,12]{0,1:T(8,128)} %param.26) | copy-start | bytes 24340
  7.2 32.3 %all-gather.3.cloned.1.call-start = ((), (), s32[]{:S(2)}) async-start(), calls=%async_computation | async-start | bytes 2359296 | tf_op jit(solution)/shard_map/all_gather | solution.py:706
  7.9 8.8 %copy-start.12 = (f32[2,384]{1,0:T(2,128)S(1)}, f32[2,384]{1,0:T(2,128)}, u32[]{:S(2)}) copy-start(f32[2,384]{1,0:T(2,128)} %param.25) | copy-start | bytes 9220
  7.9 12.7 %copy-start.6 = (s32[49,49]{1,0:T(8,128)S(1)}, s32[49,49]{1,0:T(8,128)}, u32[]{:S(2)}) copy-start(s32[49,49]{1,0:T(8,128)} %param.21) | copy-start | bytes 28816
  8.0 80.1 %all-gather.5.cloned.1.call-start = ((), (), s32[]{:S(2)}) async-start(), calls=%async_computation.1 | async-start | bytes 2359296 | tf_op jit(solution)/shard_map/all_gather | solution.py:707
  8.7 272.5 %all-reduce.7.cloned.1.call-start = ((), (), s32[]{:S(2)}) async-start(), calls=%async_computation.2 | async-start | bytes 10616832 | tf_op jit(solution)/shard_map/psum | solution.py:718
  12.8 11.2 %copy-start.8 = (f32[768]{0:T(1024)S(1)}, f32[768]{0:T(1024)}, u32[]{:S(2)}) copy-start(f32[768]{0:T(1024)} %param.28) | copy-start | bytes 9220
  12.8 11.8 %copy-start.9 = (f32[768]{0:T(1024)S(1)}, f32[768]{0:T(1024)}, u32[]{:S(2)}) copy-start(f32[768]{0:T(1024)} %param.29) | copy-start | bytes 9220
  12.8 12.4 %copy-start.10 = (f32[768]{0:T(1024)S(1)}, f32[768]{0:T(1024)}, u32[]{:S(2)}) copy-start(f32[768]{0:T(1024)} %param.30) | copy-start | bytes 9220
  12.8 12.9 %copy-start.7 = (f32[1536]{0:T(1024)S(1)}, f32[1536]{0:T(1024)}, u32[]{:S(2)}) copy-start(f32[1536]{0:T(1024)} %param.32) | copy-start | bytes 18436
  12.8 13.5 %copy-start.11 = (f32[768]{0:T(1024)S(1)}, f32[768]{0:T(1024)}, u32[]{:S(2)}) copy-start(f32[768]{0:T(1024)} %param.34) | copy-start | bytes 9220
  281.2 3.7 %copy-start.5 = (bf16[384,768]{1,0:T(8,128)(2,1)S(1)}, bf16[384,768]{1,0:T(8,128)(2,1)}, u32[]{:S(2)}) copy-start(bf16[384,768]{1,0:T(8,128)(2,1)} %get-tuple-element.74) | copy-start | bytes 1769476
  281.2 4.7 %copy-start.2 = (bf16[768,1536]{1,0:T(8,128)(2,1)S(1)}, bf16[768,1536]{1,0:T(8,128)(2,1)}, u32[]{:S(2)}) copy-start(bf16[768,1536]{1,0:T(8,128)(2,1)} %get-tuple-element.75) | copy-start | bytes 7077892
  286.0 2.8 copy-start.1
  288.8 2.6 copy-start.3
  288.8 3.4 %copy-start.4 = (bf16[1024,384]{1,0:T(8,128)(2,1)S(1)}, bf16[1024,384]{1,0:T(8,128)(2,1)}, u32[]{:S(2)}) copy-start(bf16[1024,384]{1,0:T(8,128)(2,1)} %get-tuple-element.141) | copy-start | bytes 2359300
Sparse Core Ops, SparseCore 0:
  9.5 29.9 all-gather.2
  41.0 41.2 all-gather.4
  136.1 143.6 all-reduce.6

commit v6 on v5

--- a/solution.py
+++ b/solution.py
@@ -21,7 +21,9 @@
 SCALE = HEAD_DIM ** (-0.5)
 EPS = 1e-05
 NEG = -1e30
-CHUNK = 256
+BLOCK = 256
+FFN_ROWS = 128
+CLOSE_ROWS = 128
 SMALL = 16
 MESH = pl.DeviceIdType.MESH
 F32 = jnp.float32
@@ -115,8 +117,9 @@
 
 
 def attn_fwd_kernel(
-    groups, w_own, tok, gain, shift, wt, qb_col, vb_col, vb_row, khot, qhott, table, kwin, qwin,
-    a_out, qt, kx, kt, vx, o_out, peer_out, w_out, lse, a_pad, vt, o_all, o_peer, w_got, send_sem, recv_sem,
+    groups, w_own, cot_own, tok, gain, shift, wt, qb_col, vb_col, vb_row, khot, qhott, table, kwin, qwin,
+    a_out, qt, kx, kt, vx, o_out, peer_out, w_out, cot, lse,
+    a_pad, vt, o_all, o_peer, w_got, cot_got, send_sem, recv_sem,
 ):
     step = pl.program_id(0)
     last = tok.shape[0] // QB - 1
@@ -129,6 +132,7 @@
     fetched = w_own.shape[0] // 2
     part = pl.ds(pl.multiple_of(core * fetched, 16), fetched)
     weight = to_peer(w_own.at[part], w_got.at[part], send_sem.at[last + 1], recv_sem.at[last + 1])
+    swap = to_peer(cot_own, cot_got, send_sem.at[last + 3], recv_sem.at[last + 3])
     handed = dp_copy(w_got.at[part], w_got.at[part], mate, send_sem.at[last + 2], recv_sem.at[last + 2])
 
     @pl.when(step == 0)
@@ -138,6 +142,7 @@
         pl.semaphore_signal(barrier, inc=1, device_id={"dp": mate}, device_id_type=MESH)
         pl.semaphore_wait(barrier, 2)
         weight.start()
+        swap.start()
         zero = jnp.zeros((HALO, tok.shape[1]), BF16)
         a_pad[:HALO, :] = zero
         a_pad[HALO + rows_all :, :] = zero
@@ -193,6 +198,11 @@
     @pl.when(step == last)
     def _():
         o_out[...] = o_all[...]
+        half = cot_own.shape[1]
+        me = lax.axis_index("mp")
+        cot[:, half_lanes(me, half)] = cot_own[...]
+        swap.wait()
+        cot[:, half_lanes(1 - me, half)] = cot_got[...]
         rows_copy(o_all, o_peer, QB, sems, last).start()
 
         def finish(i, carry):
@@ -222,7 +232,7 @@
     return [pltpu.SemaphoreType.DMA((n,)), pltpu.SemaphoreType.DMA((n,))]
 
 
-def attn_fwd(w_own, tok, gain, shift, wt, qb_col, vb_col, vb_row, khot, qhott, table, kwin, qwin):
+def attn_fwd(w_own, cot_own, tok, gain, shift, wt, qb_col, vb_col, vb_row, khot, qhott, table, kwin, qwin):
     rows, model = tok.shape
     width = wt.shape[0] // 3
     heads = width // HEAD_DIM
@@ -231,26 +241,28 @@
     return pl.pallas_call(
         partial(attn_fwd_kernel, heads // GROUP),
         grid=(rows // QB,),
-        in_specs=[pl.BlockSpec(memory_space=pltpu.VMEM)]
+        in_specs=[pl.BlockSpec(memory_space=pltpu.VMEM)] * 2
         + [whole(x) for x in (tok, gain, shift, wt, qb_col, vb_col, vb_row, khot)]
         + [cols(CP), whole(table), whole(kwin), cols(1)],
         out_specs=[
             same(rows, model), same(width, rows), same(ext, width), same(width, ext), same(ext, width),
-            same(rows, width), same(rows, width), same(width, model), cols(heads),
+            same(rows, width), same(rows, width), same(width, model), same(rows, model),
+            cols(heads),
         ],
         out_shape=[
             shape((rows, model), BF16), shape((width, rows), BF16), shape((ext, width), BF16),
             shape((width, ext), BF16), shape((ext, width), BF16), shape((rows, width), BF16),
-            shape((rows, width), BF16), shape((width, model), BF16), shape((heads, rows), F32),
+            shape((rows, width), BF16), shape((width, model), BF16), shape((rows, model), BF16),
+            shape((heads, rows), F32),
         ],
         scratch_shapes=[
             pltpu.VMEM((ext, model), BF16), pltpu.VMEM((width, ext), BF16),
             pltpu.VMEM((rows, width), BF16), pltpu.VMEM((rows, width), BF16),
-            pltpu.VMEM((width, model), BF16),
-        ] + two_sems(rows // QB + 2),
+            pltpu.VMEM((width, model), BF16), pltpu.VMEM(cot_own.shape, BF16),
+        ] + two_sems(rows // QB + 3),
         compiler_params=pltpu.CompilerParams(collective_id=0, has_side_effects=True),
         name="attn_fwd",
-    )(w_own, tok, gain, shift, wt, qb_col, vb_col, vb_row, khot, qhott, table, kwin, qwin)
+    )(w_own, cot_own, tok, gain, shift, wt, qb_col, vb_col, vb_row, khot, qhott, table, kwin, qwin)
 
 
 def ffn_kernel(
@@ -260,7 +272,7 @@
 ):
     rows_all, model = tok.shape
     half = keep.shape[1]
-    chunks = rows_all // CHUNK
+    chunks = rows_all // FFN_ROWS
     sems = (send_sem, recv_sem)
     me = lax.axis_index("mp")
     own = half_lanes(me, half)
@@ -270,7 +282,7 @@
     vec_in[...] = jnp.zeros_like(vec_in)
 
     def forward(c, carry):
-        at = pl.ds(pl.multiple_of(c * CHUNK, CHUNK), CHUNK)
+        at = pl.ds(pl.multiple_of(c * FFN_ROWS, FFN_ROWS), FFN_ROWS)
         x1 = tok[at, :].astype(F32) + dot(o_own[at, :], w_own[...]) + dot(o_peer[at, :], w_peer[...])
         x1 = x1 + bo[...]
         center = x1 - jnp.mean(x1, axis=-1, keepdims=True)
@@ -291,13 +303,13 @@
         gh_s[at, :] = dot_nt(du, w_in[...]).astype(BF16)
         vec_in[...] += jnp.sum(du.astype(F32), axis=0, keepdims=True)
         keep[at, :] = wide_b[:, own] + bb[:, own]
-        rows_copy(gh_s, gh_p, CHUNK, sems, c).start()
+        rows_copy(gh_s, gh_p, FFN_ROWS, sems, c).start()
         return carry
 
     lax.fori_loop(0, chunks, forward, 0)
 
     def output(c, carry):
-        at = pl.ds(pl.multiple_of(c * CHUNK, CHUNK), CHUNK)
+        at = pl.ds(pl.multiple_of(c * FFN_ROWS, FFN_ROWS), FFN_ROWS)
         wide_a[...] = dot(z_s[at, :], w_back[...])
         keep[at, :] += wide_a[:, own]
         give[at, :] = wide_a[:, other].astype(BF16)
@@ -307,22 +319,22 @@
     g_acc[...] = jnp.zeros_like(g_acc)
 
     def back_block(i, carry):
-        at = pl.ds(pl.multiple_of(i * CHUNK, CHUNK), CHUNK)
+        at = pl.ds(pl.multiple_of(i * BLOCK, BLOCK), BLOCK)
         g_back[at, :] = dot_tn(z_s[:, at], cot[...]).astype(BF16)
         return carry
 
-    lax.fori_loop(0, z_s.shape[1] // CHUNK, back_block, 0)
+    lax.fori_loop(0, z_s.shape[1] // BLOCK, back_block, 0)
 
     def in_block(i, carry):
-        at = pl.ds(pl.multiple_of(i * CHUNK, CHUNK), CHUNK)
+        at = pl.ds(pl.multiple_of(i * BLOCK, BLOCK), BLOCK)
         g_in[at, :] = dot_tn(h_s[:, at], du_s[...]).astype(BF16)
         return carry
 
-    lax.fori_loop(0, model // CHUNK, in_block, 0)
+    lax.fori_loop(0, model // BLOCK, in_block, 0)
 
     def backward(c, carry):
-        at = pl.ds(pl.multiple_of(c * CHUNK, CHUNK), CHUNK)
-        rows_copy(gh_s, gh_p, CHUNK, sems, c).wait()
+        at = pl.ds(pl.multiple_of(c * FFN_ROWS, FFN_ROWS), FFN_ROWS)
+        rows_copy(gh_s, gh_p, FFN_ROWS, sems, c).wait()
         gh = gh_s[at, :].astype(F32) + gh_p[at, :].astype(F32)
         n = n_s[at, :]
         e = gh * gain[...]
@@ -364,8 +376,8 @@
         scratch_shapes=[
             vm((rows, model), F32), vm((rows, 1), F32), vm((rows, model), BF16), vm((rows, hidden), BF16),
             vm((rows, hidden), BF16), vm((rows, model), BF16), vm((rows, model), BF16),
-            vm((width, model), F32), vm((CHUNK, model), F32), vm((CHUNK, model), F32),
-        ] + two_sems(rows // CHUNK),
+            vm((width, model), F32), vm((FFN_ROWS, model), F32), vm((FFN_ROWS, model), F32),
+        ] + two_sems(rows // FFN_ROWS),
         compiler_params=pltpu.CompilerParams(collective_id=1, has_side_effects=True),
         name="ffn",
     )(tok, o_own, o_peer, w_own, w_peer, bo, gain, shift, w_in, b_in, w_back, bb, cot)
@@ -464,15 +476,15 @@
     rows_all, model = tok.shape
     width = dq.shape[1]
     half = out.shape[1]
-    chunks = rows_all // CHUNK
+    chunks = rows_all // CLOSE_ROWS
     me = lax.axis_index("mp")
     own = half_lanes(me, half)
     other = half_lanes(1 - me, half)
     greet()
     vec_s[...] = jnp.zeros_like(vec_s)
-    main = lambda c: rows_copy(give, got, CHUNK, (send_sem.at[0], recv_sem.at[0]), c)
-    side = lambda c: rows_copy(stat, stat_p, CHUNK, (send_sem.at[1], recv_sem.at[1]), c)
-    lane = lax.broadcasted_iota(jnp.int32, (CHUNK, 128), 1)
+    main = lambda c: rows_copy(give, got, CLOSE_ROWS, (send_sem.at[0], recv_sem.at[0]), c)
+    side = lambda c: rows_copy(stat, stat_p, CLOSE_ROWS, (send_sem.at[1], recv_sem.at[1]), c)
+    lane = lax.broadcasted_iota(jnp.int32, (CLOSE_ROWS, 128), 1)
 
     def norms(at):
         x = tok[at, :].astype(F32)
@@ -481,7 +493,7 @@
         return center * r, r
 
     def forward(c, carry):
-        at = pl.ds(pl.multiple_of(c * CHUNK, CHUNK), CHUNK)
+        at = pl.ds(pl.multiple_of(c * CLOSE_ROWS, CLOSE_ROWS), CLOSE_ROWS)
         ga = dot(dq[at, :], wt[:width, :]) + dot(dk[at, :], wt[width : 2 * width, :])
         ga = ga + dot(dv[at, :], wt[2 * width :, :])
         wide[...] = ga
@@ -511,7 +523,7 @@
     qv = [jnp.sum(item[...].astype(F32), axis=0, keepdims=True) for item in (dq, dv)]
 
     def backward(c, carry):
-        at = pl.ds(pl.multiple_of(c * CHUNK, CHUNK), CHUNK)
+        at = pl.ds(pl.multiple_of(c * CLOSE_ROWS, CLOSE_ROWS), CLOSE_ROWS)
         main(c).wait()
         side(c).wait()
         sums = stat[at, :] + stat_p[at, :]
@@ -539,7 +551,7 @@
     rows, model = tok.shape
     width = dq.shape[1]
     half = gr.shape[1]
-    chunks = rows // CHUNK
+    chunks = rows // CLOSE_ROWS
     shape = jax.ShapeDtypeStruct
     vm = pltpu.VMEM
     sems = pltpu.SemaphoreType.DMA((3, chunks))
@@ -550,7 +562,7 @@
         out_shape=[shape((rows, half), BF16), shape((late_rows, model), BF16)],
         scratch_shapes=[
             vm((rows, half), F32), vm((rows, half), BF16), vm((rows, half), BF16), vm((rows, 128), F32),
-            vm((rows, 128), F32), vm((CHUNK, model), F32), vm((8, model), F32), vm((8, model), F32),
+            vm((rows, 128), F32), vm((CLOSE_ROWS, model), F32), vm((8, model), F32), vm((8, model), F32),
             sems, sems,
         ],
         compiler_params=pltpu.CompilerParams(collective_id=3, has_side_effects=True),
@@ -569,10 +581,9 @@
     )
 
 
-def dp_sum_kernel(orders, x, big, small, out, acc, got, send_sem, recv_sem):
-    rows, wide = x.shape
-    part = wide // len(orders)
-    steps = len(orders[0])
+def dp_sum_kernel(flows, x, big, small, out, acc, got, send_sem, recv_sem):
+    rows = x.shape[0]
+    steps = len(flows[0][0])
     place = lax.axis_index("dp")
 
     def bit_of(b):
@@ -586,51 +597,54 @@
         pl.semaphore_signal(barrier, inc=1, device_id={"dp": partner_of(b)}, device_id_type=MESH)
     pl.semaphore_wait(barrier, steps)
 
-    state = [(x, 0)] * len(orders)
-    kept = [[] for _ in orders]
-    for s in range(steps):
+    lows = [[0] for _ in flows]
+    for k, (order, _, _) in enumerate(flows):
+        for s in range(steps):
+            lows[k].append(lows[k][s] + bit_of(order[s]) * (rows >> (s + 1)))
+
+    def halve(k, s):
+        order, lane, count = flows[k]
+        size = rows >> (s + 1)
+        lanes = pl.ds(lane, count)
+        theirs = pl.multiple_of(lows[k][s] + (1 - bit_of(order[s])) * size, 16)
+        copy = dp_copy(
+            (x if s == 0 else acc).at[pl.ds(theirs, size), lanes],
+            got.at[pl.ds(rows - (rows >> s), size), lanes],
+            partner_of(order[s]),
+            send_sem.at[k, s],
+            recv_sem.at[k, s],
+        )
+        copy.start()
+        return copy
+
+    def add(k, s):
+        _, lane, count = flows[k]
         size = rows >> (s + 1)
         base = rows - (rows >> s)
-        copies = []
-        for k, order in enumerate(orders):
-            src, low = state[k]
-            lanes = pl.ds(part * k, part)
-            bit = bit_of(order[s])
-            mine = pl.multiple_of(low + bit * size, 16)
-            theirs = pl.multiple_of(low + (1 - bit) * size, 16)
-            copy = dp_copy(
-                src.at[pl.ds(theirs, size), lanes],
-                got.at[pl.ds(base, size), lanes],
-                partner_of(order[s]),
-                send_sem.at[k, s],
-                recv_sem.at[k, s],
-            )
-            copy.start()
-            copies.append(copy)
-            kept[k].append(low)
-            state[k] = (src, mine)
-        for k, order in enumerate(orders):
-            src, mine = state[k]
-            lanes = slice(part * k, part * (k + 1))
+        lanes = slice(lane, lane + count)
+        mine = pl.ds(pl.multiple_of(lows[k][s + 1], 16), size)
+        total = (x if s == 0 else acc)[mine, lanes].astype(F32) + got[base : base + size, lanes].astype(F32)
+        (out if s == steps - 1 else acc)[mine, lanes] = total.astype(BF16)
+
+    def double(k, s):
+        order, lane, count = flows[k]
+        at = 2 * steps - 1 - s
+        region = out.at[pl.ds(pl.multiple_of(lows[k][s + 1], 16), rows >> (s + 1)), pl.ds(lane, count)]
+        copy = dp_copy(region, region, partner_of(order[s]), send_sem.at[k, at], recv_sem.at[k, at])
+        copy.start()
+        return copy
+
+    copies = [halve(k, 0) for k in range(len(flows))]
+    for s in range(steps):
+        for k in range(len(flows)):
             copies[k].wait()
-            total = src[pl.ds(mine, size), lanes].astype(F32) + got[base : base + size, lanes].astype(F32)
-            goal = out if s == steps - 1 else acc
-            goal[pl.ds(mine, size), lanes] = total.astype(BF16)
-            state[k] = (goal, mine)
+            add(k, s)
+            copies[k] = halve(k, s + 1) if s + 1 < steps else double(k, s)
     for s in reversed(range(steps)):
-        size = rows >> (s + 1)
-        copies = []
-        for k, order in enumerate(orders):
-            low = state[k][1]
-            lanes = pl.ds(part * k, part)
-            region = out.at[pl.ds(pl.multiple_of(low, 16), size), lanes]
-            at = 2 * steps - 1 - s
-            copy = dp_copy(region, region, partner_of(order[s]), send_sem.at[k, at], recv_sem.at[k, at])
-            copy.start()
-            copies.append(copy)
-            state[k] = (out, kept[k][s])
-        for copy in copies:
-            copy.wait()
+        for k in range(len(flows)):
+            copies[k].wait()
+            if s > 0:
+                copies[k] = double(k, s - 1)
     tall = big.shape[0] // 2
     for k in range(2):
         big[tall * k : tall * (k + 1), :] = out[:tall, big.shape[1] * k : big.shape[1] * (k + 1)]
@@ -640,11 +654,12 @@
 def dp_sum(ranks, big_shape, x):
     rows, wide = x.shape
     steps = ranks.bit_length() - 1
-    orders = [list(range(steps)), [0] + list(range(2, steps)) + [1]]
+    first, second = list(range(steps)), [0] + list(range(2, steps)) + [1]
+    flows = [(first, 0, 256), (second, 256, 256), (first, 512, 128), (second, 640, 128)]
     vm = pltpu.VMEM
-    sems = pltpu.SemaphoreType.DMA((2, 2 * steps))
+    sems = pltpu.SemaphoreType.DMA((len(flows), 2 * steps))
     return pl.pallas_call(
-        partial(dp_sum_kernel, orders),
+        partial(dp_sum_kernel, flows),
         in_specs=[pl.BlockSpec(memory_space=pltpu.VMEM)],
         out_specs=[pl.BlockSpec(memory_space=pltpu.VMEM)] * 2,
         out_shape=[jax.ShapeDtypeStruct(big_shape, BF16), jax.ShapeDtypeStruct((SMALL, wide), F32)],
@@ -704,10 +719,9 @@
         crop_counts, crop_patches, rel_index, rel_table, rows
     )
     whole_in = lax.all_gather(tokens, "mp", axis=1, tiled=True)
-    whole_cot = lax.all_gather(cotangent, "mp", axis=1, tiled=True)
     wt = jnp.transpose(w_qkv, (1, 2, 0)).reshape(3 * width, model)
-    mixer_in, qt, kx, kt, vx, heads_out, heads_peer, w_peer, lse = attn_fwd(
-        w_out,
+    mixer_in, qt, kx, kt, vx, heads_out, heads_peer, w_peer, whole_cot, lse = attn_fwd(
+        w_out, cotangent,
         whole_in, ln1_gain[None, :], ln1_shift[None, :], wt, qv_bias[0][:, None], qv_bias[1][:, None],
         qv_bias[1][None, :], khot, qhott, table, kwin, qwin,
     )
@@ -731,9 +745,10 @@
         vec2, grad_b_in, table_flat.reshape(table_rows, model),
     )
     big, small = dp_sum(ranks, (3 * model, width), late)
+    big = big.astype(F32)
     early, big = lax.optimization_barrier((early, big))
     grad_w_in, grad_w_back, grad_w_out = (item.astype(F32) for item in early)
-    grad_w_qkv = jnp.transpose(big.astype(F32).reshape(3, model, width), (1, 0, 2))
+    grad_w_qkv = jnp.transpose(big.reshape(3, model, width), (1, 0, 2))
     grad_g1, grad_c1, grad_g2, grad_c2, grad_b_out, grad_b_back = (small[k] for k in range(6))
     grad_qv_bias = small[6].reshape(2, width)
     hidden_rows = w_in.shape[1] // model

time: 300 us -> 293 us (0.977)
  Pallas kernels: 232 us -> 218 us
  waiting for transfers between devices: 10.3 us -> 17.3 us
    pallas_call x1, Pallas kernels: 64.9 us -> 52.4 us  [dp_sum(): pl.pallas_call(partial(dp_sum_kernel, flows), in_specs=[pl.BlockSpec(memo...]
    psum x1, waiting for transfers between devices: 0.01 us -> 4.77 us  [body(): early = lax.psum((grad_w_in, grad_w_back, grad_w_out), 'dp')]
    transpose x1 -> x0, other arithmetic: 3.65 us -> none  [body(): jnp.transpose(big.astype(F32).reshape(3, model, width), (1, 0, 2))]
    convert_element_type x0 -> x1, other arithmetic: none -> 3.53 us  [body(): big = big.astype(F32)]
  transfers between devices with their start and end apart: 3 -> 2, of which waited for: 1 -> 2; matrix products, arithmetic and copies ran while one was open for 10% -> 11% of each run, Pallas kernels for 61% -> 42%
where the time goes in v6:
time: 293 us
  Pallas kernels  218 us (74%)
  local copies, waits for them, and re-layouts  20.5 us (7%)
  other arithmetic  19.6 us (7%)
  waiting for transfers between devices  17.3 us (6%)
  between operations  14.9 us (5%)
    pallas_call x1, Pallas kernels, dp_sum(): pl.pallas_call(partial(dp_sum_kernel, flows), in_specs=[pl.BlockSpec(memo...  52.4 us
    pallas_call x1, Pallas kernels, attn_fwd(): pl.pallas_call(partial(attn_fwd_kernel, heads // GROUP), grid=(rows // QB...  48.8 us
    pallas_call x1, Pallas kernels, ffn(): pl.pallas_call(ffn_kernel, in_specs=[pl.BlockSpec(memory_space=pltpu.VMEM...  46.4 us
    pallas_call x1, Pallas kernels, close(): pl.pallas_call(close_kernel, in_specs=[pl.BlockSpec(memory_space=pltpu.VM...  35.9 us
    pallas_call x1, Pallas kernels, attn_bwd(): pl.pallas_call(partial(attn_bwd_kernel, heads // GROUP), grid=(rows // QB...  34.4 us
    all_gather x1, waiting for transfers between devices, body(): whole_in = lax.all_gather(tokens, 'mp', axis=1, tiled=True)  11.8 us
    convert_element_type x3, other arithmetic, body(): grad_w_in, grad_w_back, grad_w_out = (item.astype(F32) for item in early)  8.28 us
  transfers between devices with their start and end apart: 2, of which 2 were waited for; matrix products, arithmetic and copies ran while one was open for 11% of the time, Pallas kernels for 42%

profile of v6, /device:TPU:0, one launch (start us, length us, event | category | flops | bytes accessed | tf_op | source)
XLA Modules:
  0.0 292.8 jit_solution(625477308763941727)
XLA Ops:
  7.2 0.0 copy-start
  7.2 0.0 all-gather.2.cloned.1.call-start
  7.3 0.7 all-gather.2.cloned.1.call-update
  8.0 0.0 all-reduce.7.cloned.1.call-start
  8.0 0.8 fusion.13
  8.8 0.1 reshape.173
  8.8 0.1 reduce-window.4
  8.9 0.5 slice.58
  9.4 0.1 reduce
  10.2 0.2 convert_reduce_fusion
  10.4 0.8 fusion.10
  11.1 0.1 pad.15
  11.2 0.7 subtract_select_fusion
  11.9 0.1 pad.17
  11.9 1.0 broadcast_in_dim.90.kwin
  13.0 0.8 copy.61
  13.8 0.1 eq.88
  13.9 1.1 subtract_convert_fusion
  15.0 0.0 copy-start.8
  15.0 0.0 copy-start.9
  15.0 0.2 stack_reshape.6
  15.2 0.2 stack_reshape.7
  15.4 0.6 fusion.16
  16.0 0.8 copy.54.qb_col
  16.8 0.8 copy.55.vb_col
  17.7 2.2 copy.49
  19.9 0.6 broadcast_in_dim.77.gain
  20.5 0.6 broadcast_in_dim.78.shift
  21.1 0.6 broadcast_in_dim.88.b_in
  21.7 0.6 broadcast_in_dim.85.bo
  22.3 0.6 broadcast_in_dim.86.gain
  22.8 0.6 broadcast_in_dim.87.shift
  23.4 0.6 broadcast_in_dim.89.bb
  24.0 0.8 pad_maximum_fusion
  24.8 1.2 compare_select_fusion.qwin
  26.1 0.7 fusion.6.qhott
  26.8 0.9 compare_convert_fusion.khot
  27.7 11.8 %all-gather.2.cloned.1.call-done.tok = bf16[1024,768]{1,0:T(8,128)(2,1)} async-done(((bf16[1024,384]{1,0:T(8,128)(2,1)}), bf16[1024,768]{1,0:T(8,128)(2,1)}) %all-gather.2.cloned.1.call-update) | async-done | bytes 1572880 | tf_op jit(solution)/shard_map/all_gather | solution.py:721
  39.5 48.8 %attn_fwd.1 = (bf16[1024,768]{1,0:T(8,128)(2,1)}, bf16[384,1024]{1,0:T(8,128)(2,1)}, bf16[1152,384]{1,0:T(8,128)(2,1)}, bf16[384,1152]{1,0:T(8,128)(2,1)}, bf16[...) custom-call(bf16[384,768]{1,0:T(8,128)(2,1)} %w_own.3, ...), custom_call_target="tpu_custom_call" | custom-call | tf_op jit(solution)/shard_map/attn_fwd/pallas_call | solution.py:241
  88.4 46.4 %ffn.1 = (f32[1024,384]{1,0:T(8,128)}, bf16[1024,384]{1,0:T(8,128)(2,1)}, f32[1024,384]{1,0:T(8,128)}, bf16[384,1024]{1,0:T(8,128)(2,1)}, bf16[384,768]{1,0:T(8,...) custom-call(bf16[1024,768]{1,0:T(8,128)(2,1)} %all-gather.2.cloned.1.ca, ...), custom_call_target="tpu_custom_call" | custom-call | tf_op jit(solution)/shard_map/ffn/pallas_call | solution.py:367
  134.7 0.0 all-reduce.7.cloned.1.call-update
  134.8 0.9 fusion.4.qhot
  135.7 0.7 fusion.5.khott
  136.4 34.4 %attn_bwd.1 = (bf16[1024,384]{1,0:T(8,128)(2,1)}, bf16[1024,384]{1,0:T(8,128)(2,1)}, bf16[1024,384]{1,0:T(8,128)(2,1)}, bf16[1024,384]{1,0:T(8,128)(2,1)}, f32[768,64]{1,0:T(8,128)}) custom-call(f32[1024,384]{1,0:T(8,128)} %get-tuple-element.51.keep, bf16[1024,384]{1,0:T(8,128)(2,1)} %get-tuple-element.52.give, bf16[384,1024]{1,0:T(8,128)(2,1)} %get-tuple-element.53.qt, ...), custom_call_target="tpu_custom_call" | custom-call | tf_op jit(solution)/shard_map/attn_bwd/pallas_call | solution.py:449
  170.8 1.1 reshape.168
  172.0 1.4 fusion.1
  173.4 0.1 reshape.169
  173.5 0.6 reshape.170.table
  174.1 35.9 %close.1 = (bf16[1024,384]{1,0:T(8,128)(2,1)}, bf16[1280,768]{1,0:T(8,128)(2,1)}) custom-call(bf16[1024,768]{1,0:T(8,128)(2,1)} %all-gather.2.cloned.1.call-done.tok, bf16[1024,768]{1,0:T(8,128)(2,1)} %get-tuple-element.60.a, bf16[1024,384]{1,0:T(8,128)(2,1)} %get-tuple-element.61.dq, bf16[1024,384]{1,0:T(8,128)(2,1)} %get-tuple-element.62.dk, ...), custom_call_target="tpu_custom_call" | custom-call | tf_op jit(solution)/shard_map/close/pallas_call | solution.py:558
  210.0 52.4 %dp_sum.1 = (bf16[2304,384]{1,0:T(8,128)(2,1)}, f32[16,768]{1,0:T(8,128)}) custom-call(bf16[1280,768]{1,0:T(8,128)(2,1)} %get-tuple-element.69.x), custom_call_target="tpu_custom_call" | custom-call | tf_op jit(solution)/shard_map/dp_sum/pallas_call | solution.py:661
  262.4 0.7 slice.50
  263.1 0.8 slice.56
  263.9 3.5 %convert_element_type.47 = f32[2304,384]{1,0:T(8,128)} convert(bf16[2304,384]{1,0:T(8,128)(2,1)} %get-tuple-element.74) | non-fusion elementwise | flops 884736 | bytes 5308416 | tf_op jit(solution)/shard_map/convert_element_type | solution.py:748
  267.5 0.1 slice.51
  267.6 0.7 copy.59
  268.3 1.7 slice_reduce_fusion
  270.0 0.6 reshape_squeeze.3
  270.6 0.6 reshape.172
  271.2 4.8 %all-reduce.7.cloned.1.call-done = (bf16[768,1536]{1,0:T(8,128)(2,1)}, bf16[1536,768]{1,0:T(8,128)(2,1)}, bf16[384,768]{1,0:T(8,128)(2,1)}) async-done(((bf16[768,1536]{1,0:T(8,128)(2,1)}, bf16[1536,768]{1,0:T(8,128)(2,1)}, bf16[384,768]{1,0:T(8,128)(2,1)}), (bf16[768,1536]{1,0:T(8,128)(2,1)}, bf16[1536,768]{1,0:T(8,128)(2,1)}, bf16[384,768]{1,0:T(8,128)(2,1)})) %all-reduce.7.cloned.1.call-update) | async-done | bytes 5308432 | tf_op jit(solution)/shard_map/psum | solution.py:732
  275.9 4.6 %convert_element_type.49 = f32[768,1536]{1,0:T(8,128)} convert(bf16[768,1536]{1,0:T(8,128)(2,1)} %get-tuple-element.77) | non-fusion elementwise | flops 1179648 | bytes 7077888 | tf_op jit(solution)/shard_map/convert_element_type | solution.py:750
  280.6 2.5 convert_element_type.50
  283.1 1.1 convert_element_type.48
  284.2 0.9 copy.67
  285.1 0.9 copy.68
  (29 shorter events, 0.1 us)
Async XLA Ops:
  7.2 6.7 %copy-start = (f32[169,12]{0,1:T(8,128)S(1)}, f32[169,12]{0,1:T(8,128)}, u32[]{:S(2)}) copy-start(f32[169,12]{0,1:T(8,128)} %param.26) | copy-start | bytes 24340
  7.2 8.2 %copy-start.13 = (f32[2,384]{1,0:T(2,128)S(1)}, f32[2,384]{1,0:T(2,128)}, u32[]{:S(2)}) copy-start(f32[2,384]{1,0:T(2,128)} %param.25) | copy-start | bytes 9220
  7.2 10.5 %copy-start.2 = (bf16[768,3,384]{2,0,1:T(8,128)(2,1)S(1)}, bf16[768,3,384]{2,0,1:T(8,128)(2,1)}, u32[]{:S(2)}) copy-start(bf16[768,3,384]{2,0,1:T(8,128)(2,1)} %param.24) | copy-start | bytes 5308420
  7.2 32.3 %all-gather.2.cloned.1.call-start = ((), (), s32[]{:S(2)}) async-start(), calls=%async_computation | async-start | bytes 2359296 | tf_op jit(solution)/shard_map/all_gather | solution.py:721
  8.0 268.0 %all-reduce.7.cloned.1.call-start = ((), (), s32[]{:S(2)}) async-start(), calls=%async_computation.1 | async-start | bytes 10616832 | tf_op jit(solution)/shard_map/psum | solution.py:732
  15.0 4.9 %copy-start.7 = (f32[768]{0:T(1024)S(1)}, f32[768]{0:T(1024)}, u32[]{:S(2)}) copy-start(f32[768]{0:T(1024)} %param.22) | copy-start | bytes 9220
  15.0 5.5 %copy-start.8 = (f32[768]{0:T(1024)S(1)}, f32[768]{0:T(1024)}, u32[]{:S(2)}) copy-start(f32[768]{0:T(1024)} %param.23) | copy-start | bytes 9220
  15.0 6.1 %copy-start.6 = (f32[1536]{0:T(1024)S(1)}, f32[1536]{0:T(1024)}, u32[]{:S(2)}) copy-start(f32[1536]{0:T(1024)} %param.32) | copy-start | bytes 18436
  15.0 6.7 %copy-start.9 = (f32[768]{0:T(1024)S(1)}, f32[768]{0:T(1024)}, u32[]{:S(2)}) copy-start(f32[768]{0:T(1024)} %param.28) | copy-start | bytes 9220
  15.0 7.3 %copy-start.10 = (f32[768]{0:T(1024)S(1)}, f32[768]{0:T(1024)}, u32[]{:S(2)}) copy-start(f32[768]{0:T(1024)} %param.29) | copy-start | bytes 9220
  15.0 7.8 %copy-start.11 = (f32[768]{0:T(1024)S(1)}, f32[768]{0:T(1024)}, u32[]{:S(2)}) copy-start(f32[768]{0:T(1024)} %param.30) | copy-start | bytes 9220
  15.0 8.4 %copy-start.12 = (f32[768]{0:T(1024)S(1)}, f32[768]{0:T(1024)}, u32[]{:S(2)}) copy-start(f32[768]{0:T(1024)} %param.34) | copy-start | bytes 9220
  275.9 4.7 %copy-start.1 = (bf16[1536,768]{1,0:T(8,128)(2,1)S(1)}, bf16[1536,768]{1,0:T(8,128)(2,1)}, u32[]{:S(2)}) copy-start(bf16[1536,768]{1,0:T(8,128)(2,1)} %get-tuple-element.78) | copy-start | bytes 7077892
  280.6 2.6 copy-start.5
  280.6 3.6 %copy-start.3 = (bf16[1024,384]{1,0:T(8,128)(2,1)S(1)}, bf16[1024,384]{1,0:T(8,128)(2,1)}, u32[]{:S(2)}) copy-start(bf16[1024,384]{1,0:T(8,128)(2,1)} %get-tuple-element.142) | copy-start | bytes 2359300
  283.1 2.0 copy-start.4
Sparse Core Ops, SparseCore 0:
  9.6 29.9 all-gather.1
  134.9 141.0 all-reduce.6

commit v7 on v6

--- a/solution.py
+++ b/solution.py
@@ -117,9 +117,9 @@
 
 
 def attn_fwd_kernel(
-    groups, w_own, cot_own, tok, gain, shift, wt, qb_col, vb_col, vb_row, khot, qhott, table, kwin, qwin,
-    a_out, qt, kx, kt, vx, o_out, peer_out, w_out, cot, lse,
-    a_pad, vt, o_all, o_peer, w_got, cot_got, send_sem, recv_sem,
+    groups, w_own, cot_own, tok_low, tok_own, gain, shift, wt, qb_col, vb_col, vb_row, khot, qhott, table, kwin, qwin,
+    tok, a_out, qt, kx, kt, vx, o_out, peer_out, w_out, cot, lse,
+    a_pad, vt, o_all, o_peer, w_got, cot_got, tok_got, send_sem, recv_sem,
 ):
     step = pl.program_id(0)
     last = tok.shape[0] // QB - 1
@@ -132,6 +132,8 @@
     fetched = w_own.shape[0] // 2
     part = pl.ds(pl.multiple_of(core * fetched, 16), fetched)
     weight = to_peer(w_own.at[part], w_got.at[part], send_sem.at[last + 1], recv_sem.at[last + 1])
+    low = tok_low.shape[0]
+    rest = to_peer(tok_own, tok_got, send_sem.at[last + 4], recv_sem.at[last + 4])
     swap = to_peer(cot_own, cot_got, send_sem.at[last + 3], recv_sem.at[last + 3])
     handed = dp_copy(w_got.at[part], w_got.at[part], mate, send_sem.at[last + 2], recv_sem.at[last + 2])
 
@@ -141,8 +143,13 @@
         pl.semaphore_signal(barrier, inc=1, device_id={"mp": peer_of()}, device_id_type=MESH)
         pl.semaphore_signal(barrier, inc=1, device_id={"dp": mate}, device_id_type=MESH)
         pl.semaphore_wait(barrier, 2)
+        rest.start()
         weight.start()
         swap.start()
+        half = tok_own.shape[1]
+        me = lax.axis_index("mp")
+        tok[:low, :] = tok_low[...]
+        tok[low:, half_lanes(me, half)] = tok_own[...]
         zero = jnp.zeros((HALO, tok.shape[1]), BF16)
         a_pad[:HALO, :] = zero
         a_pad[HALO + rows_all :, :] = zero
@@ -154,15 +161,25 @@
             a_pad[pl.ds(pl.multiple_of(at + HALO, HALO), QB), :] = a
             return carry
 
-        lax.fori_loop(0, rows_all // QB, norm_rows, 0)
-        a_all = a_pad[...]
         wk = wt[width : 2 * width, :]
         wv = wt[2 * width :, :]
-        qt[...] = (dot_nt(wt[:width, :], a_out[...]) + qb_col[...]).astype(BF16)
-        kx[...] = dot_nt(a_all, wk).astype(BF16)
-        kt[...] = dot_nt(wk, a_all).astype(BF16)
-        vx[...] = (dot_nt(a_all, wv) + vb_row[...]).astype(BF16)
-        vt[...] = (dot_nt(wv, a_all) + vb_col[...]).astype(BF16)
+
+        def project(first, end, first_pad, end_pad):
+            q_rows = slice(first, end)
+            rows = slice(first_pad, end_pad)
+            a_some = a_pad[rows, :]
+            qt[:, q_rows] = (dot_nt(wt[:width, :], a_out[q_rows, :]) + qb_col[...]).astype(BF16)
+            kx[rows, :] = dot_nt(a_some, wk).astype(BF16)
+            kt[:, rows] = dot_nt(wk, a_some).astype(BF16)
+            vx[rows, :] = (dot_nt(a_some, wv) + vb_row[...]).astype(BF16)
+            vt[:, rows] = (dot_nt(wv, a_some) + vb_col[...]).astype(BF16)
+
+        lax.fori_loop(0, low // QB, norm_rows, 0)
+        project(0, low, 0, low)
+        rest.wait()
+        tok[low:, half_lanes(1 - me, half)] = tok_got[...]
+        lax.fori_loop(low // QB, rows_all // QB, norm_rows, 0)
+        project(low, rows_all, low, rows_all + 2 * HALO)
 
     start = pl.multiple_of(step * QB, QB)
     span = pl.ds(start, SPAN)
@@ -232,8 +249,8 @@
     return [pltpu.SemaphoreType.DMA((n,)), pltpu.SemaphoreType.DMA((n,))]
 
 
-def attn_fwd(w_own, cot_own, tok, gain, shift, wt, qb_col, vb_col, vb_row, khot, qhott, table, kwin, qwin):
-    rows, model = tok.shape
+def attn_fwd(w_own, cot_own, tok_low, tok_own, gain, shift, wt, qb_col, vb_col, vb_row, khot, qhott, table, kwin, qwin):
+    rows, model = tok_low.shape[0] + tok_own.shape[0], tok_low.shape[1]
     width = wt.shape[0] // 3
     heads = width // HEAD_DIM
     ext = rows + 2 * HALO
@@ -242,15 +259,16 @@
         partial(attn_fwd_kernel, heads // GROUP),
         grid=(rows // QB,),
         in_specs=[pl.BlockSpec(memory_space=pltpu.VMEM)] * 2
-        + [whole(x) for x in (tok, gain, shift, wt, qb_col, vb_col, vb_row, khot)]
+        + [whole(tok_low), pl.BlockSpec(memory_space=pltpu.VMEM)]
+        + [whole(x) for x in (gain, shift, wt, qb_col, vb_col, vb_row, khot)]
         + [cols(CP), whole(table), whole(kwin), cols(1)],
         out_specs=[
-            same(rows, model), same(width, rows), same(ext, width), same(width, ext), same(ext, width),
+            same(rows, model), same(rows, model), same(width, rows), same(ext, width), same(width, ext), same(ext, width),
             same(rows, width), same(rows, width), same(width, model), same(rows, model),
             cols(heads),
         ],
         out_shape=[
-            shape((rows, model), BF16), shape((width, rows), BF16), shape((ext, width), BF16),
+            shape((rows, model), BF16), shape((rows, model), BF16), shape((width, rows), BF16), shape((ext, width), BF16),
             shape((width, ext), BF16), shape((ext, width), BF16), shape((rows, width), BF16),
             shape((rows, width), BF16), shape((width, model), BF16), shape((rows, model), BF16),
             shape((heads, rows), F32),
@@ -259,10 +277,11 @@
             pltpu.VMEM((ext, model), BF16), pltpu.VMEM((width, ext), BF16),
             pltpu.VMEM((rows, width), BF16), pltpu.VMEM((rows, width), BF16),
             pltpu.VMEM((width, model), BF16), pltpu.VMEM(cot_own.shape, BF16),
-        ] + two_sems(rows // QB + 3),
+            pltpu.VMEM(tok_own.shape, BF16),
+        ] + two_sems(rows // QB + 4),
         compiler_params=pltpu.CompilerParams(collective_id=0, has_side_effects=True),
         name="attn_fwd",
-    )(w_own, cot_own, tok, gain, shift, wt, qb_col, vb_col, vb_row, khot, qhott, table, kwin, qwin)
+    )(w_own, cot_own, tok_low, tok_own, gain, shift, wt, qb_col, vb_col, vb_row, khot, qhott, table, kwin, qwin)
 
 
 def ffn_kernel(
@@ -718,11 +737,11 @@
     khot, khott, qhott, qhot, table, kwin, qwin, offset_hot = window_data(
         crop_counts, crop_patches, rel_index, rel_table, rows
     )
-    whole_in = lax.all_gather(tokens, "mp", axis=1, tiled=True)
+    low = rows // 2
+    whole_low = lax.all_gather(tokens[:low], "mp", axis=1, tiled=True)
     wt = jnp.transpose(w_qkv, (1, 2, 0)).reshape(3 * width, model)
-    mixer_in, qt, kx, kt, vx, heads_out, heads_peer, w_peer, whole_cot, lse = attn_fwd(
-        w_out, cotangent,
-        whole_in, ln1_gain[None, :], ln1_shift[None, :], wt, qv_bias[0][:, None], qv_bias[1][:, None],
+    whole_in, mixer_in, qt, kx, kt, vx, heads_out, heads_peer, w_peer, whole_cot, lse = attn_fwd(
+        w_out, cotangent, whole_low, tokens[low:], ln1_gain[None, :], ln1_shift[None, :], wt, qv_bias[0][:, None], qv_bias[1][:, None],
         qv_bias[1][None, :], khot, qhott, table, kwin, qwin,
     )
     keep, give, gr, dot_t, grad_w_out, grad_w_in, grad_w_back, vec2, grad_b_in = ffn(

time: 293 us -> 305 us (1.041)
  waiting for transfers between devices: 17.3 us -> 4.19 us
  blocking collectives: 0 us -> 13 us
  Pallas kernels: 218 us -> 228 us
    all_gather x0 -> x1, blocking collectives: none -> 13 us  [body(): whole_low = lax.all_gather(tokens[:low], 'mp', axis=1, tiled=True)]
    all_gather x1 -> x0, waiting for transfers between devices: 11.8 us -> none  [body(): whole_in = lax.all_gather(tokens, 'mp', axis=1, tiled=True)]
    pallas_call x1, Pallas kernels: 48.8 us -> 58.5 us  [attn_fwd(): pl.pallas_call(partial(attn_fwd_kernel, heads // GROUP), grid=(rows // QB...]
  transfers between devices with their start and end apart: 2 -> 1, of which waited for: 2 -> 1; matrix products, arithmetic and copies ran while one was open for 11% -> 4% of each run, Pallas kernels for 42% -> 40%
where the time goes in v7:
time: 305 us; the launch traced here: 304 us
  Pallas kernels  228 us (75%)
  local copies, waits for them, and re-layouts  21.4 us (7%)
  other arithmetic  19.7 us (6%)
  between operations  14.9 us (5%)
  blocking collectives  13 us (4%)
  waiting for transfers between devices  4.19 us (1%)
    pallas_call x1, Pallas kernels, attn_fwd(): pl.pallas_call(partial(attn_fwd_kernel, heads // GROUP), grid=(rows // QB...  58.5 us
    pallas_call x1, Pallas kernels, dp_sum(): pl.pallas_call(partial(dp_sum_kernel, flows), in_specs=[pl.BlockSpec(memo...  53.2 us
    pallas_call x1, Pallas kernels, ffn(): pl.pallas_call(ffn_kernel, in_specs=[pl.BlockSpec(memory_space=pltpu.VMEM...  47 us
    pallas_call x1, Pallas kernels, close(): pl.pallas_call(close_kernel, in_specs=[pl.BlockSpec(memory_space=pltpu.VM...  36.6 us
    pallas_call x1, Pallas kernels, attn_bwd(): pl.pallas_call(partial(attn_bwd_kernel, heads // GROUP), grid=(rows // QB...  33.3 us
    all_gather x1, blocking collectives, body(): whole_low = lax.all_gather(tokens[:low], 'mp', axis=1, tiled=True)  13 us
    convert_element_type x3, other arithmetic, body(): grad_w_in, grad_w_back, grad_w_out = (item.astype(F32) for item in early)  8.28 us
  transfers between devices with their start and end apart: 1, of which 1 were waited for; matrix products, arithmetic and copies ran while one was open for 4% of the time, Pallas kernels for 40%

profile of v7, /device:TPU:0, one launch (start us, length us, event | category | flops | bytes accessed | tf_op | source)
XLA Modules:
  0.0 304.2 jit_solution(4628536326145858806)
XLA Ops:
  7.2 0.0 copy-start
  7.2 0.0 all-reduce.7.cloned.1.call-start
  7.3 0.9 fusion.13
  8.1 0.1 reshape.173
  8.2 0.1 reduce-window.4
  8.3 0.5 slice.66
  8.8 0.1 reduce
  9.6 0.2 convert_reduce_fusion
  9.7 0.8 fusion.10
  10.5 0.1 pad.15
  10.6 0.7 fusion.6.qhott
  11.3 0.6 subtract_select_fusion
  11.9 0.1 pad.17
  12.0 1.0 broadcast_in_dim.90.kwin
  13.0 1.2 compare_select_fusion.qwin
  14.3 0.8 copy.61
  15.1 0.1 eq.88
  15.2 1.1 subtract_convert_fusion
  16.3 0.2 stack_reshape.6
  16.5 0.2 stack_reshape.7
  16.7 0.6 fusion.17
  17.2 0.8 copy.54.qb_col
  18.1 0.8 copy.55.vb_col
  18.9 0.0 copy-start.10
  18.9 0.0 copy-start.11
  18.9 0.0 copy-start.12
  19.0 2.3 copy.49
  21.2 0.8 fusion.16
  22.0 13.0 %all_gather.3.tok_low = bf16[512,768]{1,0:T(8,128)(2,1)} all-gather(bf16[512,384]{1,0:T(8,128)(2,1)S(1)} %get-tuple-element.127), channel_id=1, replica_groups=mesh['dp'=16,'mp'=2] {'mp'}, dimensions={1}, use_global_device_ids=true | all-gather | bytes 1179648 | tf_op jit(solution)/shard_map/all_gather | solution.py:741
  35.1 0.6 broadcast_in_dim.77.gain
  35.7 0.6 broadcast_in_dim.78.shift
  36.2 0.6 broadcast_in_dim.88.b_in
  36.8 0.6 broadcast_in_dim.85.bo
  37.4 0.6 broadcast_in_dim.86.gain
  38.0 0.6 broadcast_in_dim.87.shift
  38.6 0.6 broadcast_in_dim.89.bb
  39.2 0.9 compare_convert_fusion.khot
  40.1 0.8 pad_maximum_fusion
  40.9 58.5 %attn_fwd.1 = (bf16[1024,768]{1,0:T(8,128)(2,1)}, bf16[1024,768]{1,0:T(8,128)(2,1)}, bf16[384,1024]{1,0:T(8,128)(2,1)}, bf16[1152,384]{1,0:T(8,128)(2,1)}, bf16[...) custom-call(bf16[384,768]{1,0:T(8,128)(2,1)} %w_own.3, ...), custom_call_target="tpu_custom_call" | custom-call | tf_op jit(solution)/shard_map/attn_fwd/pallas_call | solution.py:258
  99.4 47.0 %ffn.1 = (f32[1024,384]{1,0:T(8,128)}, bf16[1024,384]{1,0:T(8,128)(2,1)}, f32[1024,384]{1,0:T(8,128)}, bf16[384,1024]{1,0:T(8,128)(2,1)}, bf16[384,768]{1,0:T(8,...) custom-call(bf16[1024,768]{1,0:T(8,128)(2,1)} %get-tuple-element.48.tok, ...), custom_call_target="tpu_custom_call" | custom-call | tf_op jit(solution)/shard_map/ffn/pallas_call | solution.py:386
  146.4 0.0 all-reduce.7.cloned.1.call-update
  146.4 0.9 fusion.4.qhot
  147.3 0.7 fusion.5.khott
  148.0 33.3 %attn_bwd.1 = (bf16[1024,384]{1,0:T(8,128)(2,1)}, bf16[1024,384]{1,0:T(8,128)(2,1)}, bf16[1024,384]{1,0:T(8,128)(2,1)}, bf16[1024,384]{1,0:T(8,128)(2,1)}, f32[768,64]{1,0:T(8,128)}) custom-call(f32[1024,384]{1,0:T(8,128)} %get-tuple-element.53.keep, bf16[1024,384]{1,0:T(8,128)(2,1)} %get-tuple-element.54.give, bf16[384,1024]{1,0:T(8,128)(2,1)} %get-tuple-element.55.qt, ...), custom_call_target="tpu_custom_call" | custom-call | tf_op jit(solution)/shard_map/attn_bwd/pallas_call | solution.py:468
  181.3 1.1 reshape.168
  182.4 1.4 fusion.1
  183.8 0.1 reshape.169
  183.9 0.6 reshape.170.table
  184.6 36.6 %close.1 = (bf16[1024,384]{1,0:T(8,128)(2,1)}, bf16[1280,768]{1,0:T(8,128)(2,1)}) custom-call(bf16[1024,768]{1,0:T(8,128)(2,1)} %get-tuple-element.48.tok, bf16[1024,768]{1,0:T(8,128)(2,1)} %get-tuple-element.62.a, bf16[1024,384]{1,0:T(8,128)(2,1)} %get-tuple-element.63.dq, bf16[1024,384]{1,0:T(8,128)(2,1)} %get-tuple-element.64.dk, ...), custom_call_target="tpu_custom_call" | custom-call | tf_op jit(solution)/shard_map/close/pallas_call | solution.py:577
  221.2 53.2 %dp_sum.1 = (bf16[2304,384]{1,0:T(8,128)(2,1)}, f32[16,768]{1,0:T(8,128)}) custom-call(bf16[1280,768]{1,0:T(8,128)(2,1)} %get-tuple-element.71.x), custom_call_target="tpu_custom_call" | custom-call | tf_op jit(solution)/shard_map/dp_sum/pallas_call | solution.py:680
  274.3 0.7 slice.58
  275.1 0.8 slice.64
  275.9 3.5 %convert_element_type.47 = f32[2304,384]{1,0:T(8,128)} convert(bf16[2304,384]{1,0:T(8,128)(2,1)} %get-tuple-element.76) | non-fusion elementwise | flops 884736 | bytes 5308416 | tf_op jit(solution)/shard_map/convert_element_type | solution.py:767
  279.4 0.1 slice.59
  279.6 0.7 copy.59
  280.2 1.7 slice_reduce_fusion
  281.9 0.6 reshape_squeeze.3
  282.5 0.6 reshape.172
  283.1 4.2 %all-reduce.7.cloned.1.call-done = (bf16[768,1536]{1,0:T(8,128)(2,1)}, bf16[1536,768]{1,0:T(8,128)(2,1)}, bf16[384,768]{1,0:T(8,128)(2,1)}) async-done(((bf16[768,1536]{1,0:T(8,128)(2,1)}, bf16[1536,768]{1,0:T(8,128)(2,1)}, bf16[384,768]{1,0:T(8,128)(2,1)}), (bf16[768,1536]{1,0:T(8,128)(2,1)}, bf16[1536,768]{1,0:T(8,128)(2,1)}, bf16[384,768]{1,0:T(8,128)(2,1)})) %all-reduce.7.cloned.1.call-update) | async-done | bytes 5308432 | tf_op jit(solution)/shard_map/psum | solution.py:751
  287.3 4.6 %convert_element_type.49 = f32[768,1536]{1,0:T(8,128)} convert(bf16[768,1536]{1,0:T(8,128)(2,1)} %get-tuple-element.79) | non-fusion elementwise | flops 1179648 | bytes 7077888 | tf_op jit(solution)/shard_map/convert_element_type | solution.py:769
  291.9 2.5 convert_element_type.50
  294.5 1.1 convert_element_type.48
  295.6 0.9 copy.67
  296.5 0.9 copy.68
  (30 shorter events, 0.1 us)
Async XLA Ops:
  7.2 8.0 %copy-start = (f32[169,12]{0,1:T(8,128)S(1)}, f32[169,12]{0,1:T(8,128)}, u32[]{:S(2)}) copy-start(f32[169,12]{0,1:T(8,128)} %param.26) | copy-start | bytes 24340
  7.2 9.5 %copy-start.14 = (f32[2,384]{1,0:T(2,128)S(1)}, f32[2,384]{1,0:T(2,128)}, u32[]{:S(2)}) copy-start(f32[2,384]{1,0:T(2,128)} %param.25) | copy-start | bytes 9220
  7.2 11.7 %copy-start.2 = (bf16[768,3,384]{2,0,1:T(8,128)(2,1)S(1)}, bf16[768,3,384]{2,0,1:T(8,128)(2,1)}, u32[]{:S(2)}) copy-start(bf16[768,3,384]{2,0,1:T(8,128)(2,1)} %param.24) | copy-start | bytes 5308420
  7.2 280.1 %all-reduce.7.cloned.1.call-start = ((), (), s32[]{:S(2)}) async-start(), calls=%async_computation | async-start | bytes 10616832 | tf_op jit(solution)/shard_map/psum | solution.py:751
  16.3 4.9 %copy-start.3 = (bf16[1024,384]{1,0:T(8,128)(2,1)S(1)}, bf16[1024,384]{1,0:T(8,128)(2,1)}, u32[]{:S(2)}) copy-start(bf16[1024,384]{1,0:T(8,128)(2,1)} %param.18) | copy-start | bytes 2359300
  18.9 16.2 %copy-start.8 = (f32[768]{0:T(1024)S(1)}, f32[768]{0:T(1024)}, u32[]{:S(2)}) copy-start(f32[768]{0:T(1024)} %param.22) | copy-start | bytes 9220
  18.9 16.8 %copy-start.9 = (f32[768]{0:T(1024)S(1)}, f32[768]{0:T(1024)}, u32[]{:S(2)}) copy-start(f32[768]{0:T(1024)} %param.23) | copy-start | bytes 9220
  18.9 17.3 %copy-start.7 = (f32[1536]{0:T(1024)S(1)}, f32[1536]{0:T(1024)}, u32[]{:S(2)}) copy-start(f32[1536]{0:T(1024)} %param.32) | copy-start | bytes 18436
  18.9 17.9 %copy-start.10 = (f32[768]{0:T(1024)S(1)}, f32[768]{0:T(1024)}, u32[]{:S(2)}) copy-start(f32[768]{0:T(1024)} %param.28) | copy-start | bytes 9220
  18.9 18.5 %copy-start.11 = (f32[768]{0:T(1024)S(1)}, f32[768]{0:T(1024)}, u32[]{:S(2)}) copy-start(f32[768]{0:T(1024)} %param.29) | copy-start | bytes 9220
  18.9 19.1 %copy-start.12 = (f32[768]{0:T(1024)S(1)}, f32[768]{0:T(1024)}, u32[]{:S(2)}) copy-start(f32[768]{0:T(1024)} %param.30) | copy-start | bytes 9220
  18.9 19.7 %copy-start.13 = (f32[768]{0:T(1024)S(1)}, f32[768]{0:T(1024)}, u32[]{:S(2)}) copy-start(f32[768]{0:T(1024)} %param.34) | copy-start | bytes 9220
  287.3 4.7 %copy-start.1 = (bf16[1536,768]{1,0:T(8,128)(2,1)S(1)}, bf16[1536,768]{1,0:T(8,128)(2,1)}, u32[]{:S(2)}) copy-start(bf16[1536,768]{1,0:T(8,128)(2,1)} %get-tuple-element.80) | copy-start | bytes 7077892
  291.9 2.6 copy-start.6
  291.9 3.6 %copy-start.4 = (bf16[1024,384]{1,0:T(8,128)(2,1)S(1)}, bf16[1024,384]{1,0:T(8,128)(2,1)}, u32[]{:S(2)}) copy-start(bf16[1024,384]{1,0:T(8,128)(2,1)} %get-tuple-element.146) | copy-start | bytes 2359300
  294.5 2.0 copy-start.5
Sparse Core Ops, SparseCore 0:
  146.5 140.6 all-reduce.6
